TPU v7x, 32 devices: a whole 2x2x4 slice. The times are simulated.
32 devices in a mesh: zm: 8 (over y, x, core), zv: 4 (over z).
Axes of the slice: x: 2, y: 2, z: 4, core: 2. Of those that a mesh axis runs over, the one named last changes fastest.
Arguments:
- table: float32 [128, 256, 256], P('zm', 'zv'), may hold values from -6 to 6
- refined: float32 [4, 256, 16, 1024], P(None, ('zm', 'zv')), may hold values from -18 to 18
- assign: int32 [4, 32, 8], replicated, may hold values from -1 to 511, as said below
Outputs:
- table_out: float32 [128, 256, 256], P('zm', 'zv')
- block_error: float32 [4, 512], P(None, ('zm', 'zv'))
- worst: float32 [4], replicated
Inputs may be any that keep to these rules, and one draw needn't show every extreme that they name: `assign`: devices are numbered d = zm index * 4 + zv index; block b is homed on device b // 16, and its home device has the same zv index as the owner d of the slot. In an iteration no block appears twice, at most 1 block of one home device sit in the slots of one owner (reached in every iteration), and some owner of every zv index has all 8 slots filled.
All inputs are finite; a program needn't handle non-finite values.
Results may differ from a plain program's by a relative error of at most 0.0001.
Values sent between devices are 32-bit elements; how exact they have to be, the bound alone decides.
No kernel may reach another device: no remote copies, remote signals or barrier semaphores. Data moves between devices by JAX's collectives and lax.ppermute only.
A program may use at most 128 MiB of HBM per device.

v0:
```python
import functools

import jax
import jax.numpy as jnp
from jax import lax
from jax.experimental import pallas as pl
from jax.experimental.pallas import tpu as pltpu
from jax.sharding import PartitionSpec as P


S = 8
BLOCK_Z = 16
BLOCK_V = 16
BLOCK_C = 8
ITERS = 4
HALF = BLOCK_C * S
PAIRS = BLOCK_V // 2
LANES = 2 * HALF
ROWS = BLOCK_Z * PAIRS
DEEP = BLOCK_Z + ITERS
AXES = ("zm", "zv")
F32 = jnp.float32
TILE = (PAIRS, LANES)


def halo_rows(iteration):
    return ITERS - 1 - iteration


LAYERS = [BLOCK_Z + halo_rows(i) for i in range(ITERS)]
OFFSET = [sum(LAYERS[:i]) * PAIRS for i in range(ITERS)]


def lane_ids():
    return lax.broadcasted_iota(jnp.int32, TILE, 1)


def sub_ids():
    return lax.broadcasted_iota(jnp.int32, TILE, 0)


VMEM = pl.BlockSpec(memory_space=pltpu.VMEM)
SMEM = pl.BlockSpec(memory_space=pltpu.SMEM)
HBM = pl.BlockSpec(memory_space=pltpu.HBM)
WHOLE = 60
PART = 24


def call(body, outs, in_specs, out_specs, scratch, limit, flops=2000000):
    return pl.pallas_call(
        body,
        out_shape=outs,
        in_specs=in_specs,
        out_specs=out_specs,
        scratch_shapes=list(scratch),
        compiler_params=pltpu.CompilerParams(vmem_limit_bytes=limit << 20),
        cost_estimate=pl.CostEstimate(flops=flops, bytes_accessed=1 << 20, transcendentals=0),
    )


def struct(*shape, dtype=F32):
    return jax.ShapeDtypeStruct(shape, dtype)


def dma(count):
    return pltpu.SemaphoreType.DMA((count,))


class Shape:
    def __init__(self, table, assign, zm_count, zv_count):
        self.zm, self.zv = zm_count, zv_count
        self.span, self.wide = table[1], table[2]
        self.vb = self.span // BLOCK_V
        self.cb = self.wide // HALF
        self.vt = self.span // 8
        self.ct = self.wide // LANES
        self.blocks = self.vb * self.cb
        self.pairs = self.vb * self.ct
        self.slots = assign[2]
        self.cells = BLOCK_Z * BLOCK_V * BLOCK_C * S

    def main(self, layers):
        return (self.ct, layers, self.span, LANES)

    def halo(self, layers):
        return (self.ct, layers, 8, LANES)


def fill_inverse(g, iterations, assign, inverse):
    me = lax.axis_index("zm") * g.zv + lax.axis_index("zv")
    for t in iterations:
        for peer in range(g.zm):
            inverse[t, peer] = 0
        for slot in range(g.slots):
            block = assign[t * g.slots + slot, me]

            @pl.when(block >= 0)
            def _():
                inverse[t, block // (g.blocks * g.zv)] = slot


def pack_three_body(g, assign, refined, out, inverse, held, sems, out_sems):
    three = range(ITERS - 1)
    fill_inverse(g, three, assign, inverse)
    reads, writes = {}, []
    for t in three:
        for peer in range(g.zm):
            rows = slice(OFFSET[t], OFFSET[t] + ROWS)
            source = refined.at[t * g.slots + inverse[t, peer]]
            reads[t, peer] = pltpu.make_async_copy(source, held.at[peer, rows, :], sems.at[t * g.zm + peer])
            reads[t, peer].start()
    for t in three:
        for peer in range(g.zm):
            rows = slice(OFFSET[t], OFFSET[t] + ROWS)
            reads[t, peer].wait()
            sem = out_sems.at[t * g.zm + peer]
            writes.append(pltpu.make_async_copy(held.at[peer, rows, :], out.at[peer, rows, :], sem))
            writes[-1].start()
        for peer in range(g.zm):
            after = min(peer + 1, g.zm - 1)
            for z in range(halo_rows(t)):
                at = OFFSET[t] + ROWS + z * PAIRS
                held[peer, at : at + PAIRS, :] = held[after, pl.ds(OFFSET[t] + z, PAIRS, stride=8), :]
        rows = slice(OFFSET[t] + ROWS, OFFSET[t + 1])
        writes.append(pltpu.make_async_copy(held.at[:, rows, :], out.at[:, rows, :], out_sems.at[3 * g.zm + t]))
        writes[-1].start()
    for write in writes:
        write.wait()


def pack_last_body(g, assign, refined, *rest):
    outs, inverse, sems = rest[: g.zm], rest[-2], rest[-1]
    t = ITERS - 1
    fill_inverse(g, [t], assign, inverse)
    here = lax.axis_index("zm")
    copies = []
    for k in range(g.zm):
        source = refined.at[t * g.slots + inverse[t, here ^ k]]
        copies.append(pltpu.make_async_copy(source, outs[k], sems.at[k]))
    for copy in copies:
        copy.start()
    for copy in copies:
        copy.wait()


def block_row(z):
    return z // 8 * 8 * PAIRS + z % 8


def pair_tiles(left, first, second):
    even = jnp.where(left, first, pltpu.roll(second, HALF, 1))
    odd = jnp.where(left, pltpu.roll(first, HALF, 1), second)
    return even, odd


def pair_live(meta, iteration, column, left):
    first, second = meta[iteration, column] >= 0, meta[iteration, column + 1] >= 0
    return (left & first) | (~left & second)


def strip_body(g, meta, data, unused_a, unused_b, out, held, planes, sems):
    three = range(ITERS - 1)
    left, sub = lane_ids() < HALF, sub_ids()

    def copies(t, c):
        mine = data.at[jnp.maximum(meta[t, c], 0), OFFSET[t] : OFFSET[t] + ROWS, :]
        far = data.at[jnp.maximum(meta[t, g.blocks + c], 0), OFFSET[t] + ROWS : OFFSET[t] + LAYERS[t] * PAIRS, :]
        at = t * g.cb + c
        return (
            pltpu.make_async_copy(mine, held.at[at, 0:ROWS, :], sems.at[2 * at]),
            pltpu.make_async_copy(far, held.at[at, ROWS : LAYERS[t] * PAIRS, :], sems.at[2 * at + 1]),
        )

    for t in three:
        for c in range(g.cb):
            for copy in copies(t, c):
                copy.start()
    for t in three:
        for c in range(g.cb):
            for copy in copies(t, c):
                copy.wait()
        first = sum(LAYERS[:t])
        for z in range(LAYERS[t]):
            for col in range(g.ct):
                tiles = []
                for c in (2 * col, 2 * col + 1):
                    if z < BLOCK_Z:
                        tiles.append(held[t * g.cb + c, pl.ds(block_row(z), PAIRS, stride=8), :])
                    else:
                        tiles.append(held[t * g.cb + c, z * PAIRS : (z + 1) * PAIRS, :])
                even, odd = pair_tiles(left, *tiles)
                planes[col, first + z, pl.ds(0, PAIRS, stride=2), :] = even
                planes[col, first + z, pl.ds(1, PAIRS, stride=2), :] = odd
        for z in range(first, first + LAYERS[t]):
            out[z] = jnp.where(sub < 4, planes[0, z, 0:8, :], pltpu.roll(planes[1, z, 0:8, :], 4, 0))


def strip_tile(strips, z, col):
    return strips[z] if col == 0 else pltpu.roll(strips[z], 4, 0)


class Stencil:
    def __init__(self, g, edge):
        self.g = g
        lane, sub = lane_ids(), sub_ids()
        self.inner = lane < LANES - S
        self.above = sub < 7
        self.last = edge & (sub == 7)

    def __call__(self, get, z, low):
        g = self.g
        sums, turned = {}, {}
        for vt in range(g.vt + 1):
            for col in range(g.ct):
                sums[col, vt] = get(col, vt, z) + get(col, vt, low)
                turned[col, vt] = pltpu.roll(sums[col, vt], LANES - S, 1)
        both, up = {}, {}
        for vt in range(g.vt + 1):
            for col in range(g.ct):
                beside = sums[col, vt] if col == g.ct - 1 else turned[col + 1, vt]
                both[col, vt] = sums[col, vt] + jnp.where(self.inner, turned[col, vt], beside)
                up[col, vt] = pltpu.roll(both[col, vt], 7, 0)
        result = {}
        for vt in range(g.vt + 1):
            for col in range(g.ct):
                value = up[col, vt]
                if vt < g.vt:
                    value = jnp.where(self.above, value, up[col, vt + 1])
                if vt == g.vt - 1:
                    value = jnp.where(self.last, both[col, vt], value)
                result[col, vt] = 0.125 * (both[col, vt] + value)
        return result


def edges(meta):
    return meta[0, 120] == 1, meta[0, 121] == 1


def layer_below(z, edge):
    return jnp.where((z == BLOCK_Z - 1) & edge, z, z + 1)


def clip(z, top):
    return jnp.minimum(jnp.maximum(z, 0), top)


def tile_rows(vt):
    return slice(vt * 8, vt * 8 + 8)


def reader(g, main, halo):
    return lambda col, vt, z: halo[col, z] if vt == g.vt else main[col, z, tile_rows(vt), :]


def put(g, main, halo, z, values):
    for (col, vt), value in values.items():
        if vt == g.vt:
            halo[col, z] = value
        else:
            main[col, z, tile_rows(vt), :] = value


def interp_body(g, meta, table, below, strip, interp, interp_halo, nodes, nodes_halo):
    edge_z, edge_v = edges(meta)
    stencil = Stencil(g, edge_v)

    def take(source, z, target):
        for col in range(g.ct):
            lanes = slice(col * LANES, (col + 1) * LANES)
            nodes[col, target] = source[z, :, lanes]
            nodes_halo[col, target] = strip[target, :, lanes]

    @pl.loop(0, BLOCK_Z)
    def _(z):
        take(table, z, z)

    @pl.loop(0, ITERS)
    def _(z):
        take(below, z, BLOCK_Z + z)

    get = reader(g, nodes, nodes_halo)

    @pl.loop(0, LAYERS[0])
    def _(z):
        put(g, interp, interp_halo, z, stencil(get, z, layer_below(z, edge_z)))


PRODUCTS = 14


def spread_rows(values, count):
    rows = [jnp.sum(value, axis=0, keepdims=True) for value in values]
    rows += [jnp.zeros_like(rows[0])] * (-len(rows) % 8)
    column = jnp.sum(jnp.concatenate(rows, 0), axis=1, keepdims=True)
    lane = lax.broadcasted_iota(jnp.int32, (len(rows), 128), 1)
    row = lax.broadcasted_iota(jnp.int32, (len(rows), 128), 0)
    line = jnp.sum(jnp.where(lane == row, column, 0.0), axis=0, keepdims=True)
    return jnp.broadcast_to(line, (count, 128))


def fill_masks(g, meta, masks, iterations, left):
    for at, t in enumerate(iterations):
        for far in range(2):
            for pair in range(g.pairs):
                column = pair // g.ct * g.cb + pair % g.ct * 2 + far * g.blocks
                masks[at, far, pair] = jnp.where(pair_live(meta, t, column, left), 1.0, 0.0)


def halo_live(g, meta, iteration, left):
    first = 2 * g.blocks
    return [[pair_live(meta, iteration, first + far * g.cb + 2 * col, left) for col in range(g.ct)] for far in range(2)]


def segments(top, counts):
    result, high = [], top
    for count in counts:
        result.append((high - count + 1, high))
        high -= count
    return result


def convert(g, meta, t, held, offset, z, out, left):
    row = offset + z // 8 * 8 * PAIRS + z % 8
    for pair in range(g.pairs):
        vb, col = pair // g.ct, pair % g.ct
        tiles = []
        for half in range(2):
            owner = jnp.maximum(meta[t, vb * g.cb + 2 * col + half], 0)
            tiles.append(held[owner, pl.ds(row, PAIRS, stride=8), :])
        even, odd = pair_tiles(left, *tiles)
        out[col, z, pl.ds(vb * BLOCK_V, PAIRS, stride=2), :] = even
        out[col, z, pl.ds(vb * BLOCK_V + 1, PAIRS, stride=2), :] = odd


def between(z):
    return jnp.where((z >= 0) & (z < BLOCK_Z), 1.0, 0.0)


def pair_tile_rows(g, pair):
    return [tile_rows(vt) for vt in (pair // g.ct * 2, pair // g.ct * 2 + 1)]


def middle_body(g, meta, strips, interp_halo, data, interp_in,
                out, a0_out, a1_out, a2_out, ca0_out, ca1_out, cb1_out, halos, peaks,
                held, interp, f0, f1, f2, a0, a1, a2, b1, ca0, ca1, cb1, a0_halo, a1_halo, b1_halo, masks, sems, out_sems):
    f, a = (f0, f1, f2), (a0, a1, a2)
    split = BLOCK_Z // 2
    groups = ([], [])
    for t in range(3):
        first, middle, end = OFFSET[t], OFFSET[t] + ROWS // 2, OFFSET[t + 1]
        for group, rows in ((0, slice(middle, end)), (1, slice(first, middle))):
            groups[group].append(pltpu.make_async_copy(data.at[:, rows, :], held.at[:, rows, :], sems.at[2 * t + group]))
    for col in range(g.ct):
        for group, layers in ((0, slice(split, LAYERS[0])), (1, slice(0, split))):
            sem = sems.at[6 + 2 * col + group]
            groups[group].append(pltpu.make_async_copy(interp_in.at[col, layers], interp.at[col, layers], sem))
    for group in groups:
        for copy in group:
            copy.start()
    edge_z, edge_v = edges(meta)
    stencil = Stencil(g, edge_v)
    left = lane_ids() < HALF
    live0, live1 = halo_live(g, meta, 0, left), halo_live(g, meta, 1, left)
    fill_masks(g, meta, masks, (0, 1, 2), left)
    for col in range(g.ct):
        for z in range(LAYERS[0]):
            value = strip_tile(strips, z, col) - interp_halo[col, z]
            a0_halo[col, z] = jnp.where(live0[z >= BLOCK_Z][col], value, 0.0)
        for z in range(LAYERS[1]):
            value = strip_tile(strips, LAYERS[0] + z, col) - interp_halo[col, z]
            a1_halo[col, z] = jnp.where(live1[z >= BLOCK_Z][col], value, 0.0)
    peaks[...] = jnp.zeros_like(peaks)
    get0, get1, getb = reader(g, a0, a0_halo), reader(g, a1, a1_halo), reader(g, b1, b1_halo)
    top0, top1 = LAYERS[1] - 1, LAYERS[2] - 1
    for copy in groups[0]:
        copy.wait()

    @pl.loop(0, g.pairs)
    def _(pair):
        vb, col = pair // g.ct, pair % g.ct
        row = pl.multiple_of(vb * BLOCK_V, BLOCK_V)
        column = g.blocks + vb * g.cb + 2 * col
        for t in range(3):
            owners = [jnp.maximum(meta[t, column + half], 0) for half in range(2)]
            for z in range(BLOCK_Z, LAYERS[t]):
                at = OFFSET[t] + z * PAIRS
                even, odd = pair_tiles(left, *[held[owner, at : at + PAIRS, :] for owner in owners])
                f[t][col, z, pl.ds(row, PAIRS, stride=2), :] = even
                f[t][col, z, pl.ds(row + 1, PAIRS, stride=2), :] = odd
        for t in range(3):
            live = masks[t, 1, pair] > 0.5
            for z in range(BLOCK_Z, LAYERS[t]):
                for half in range(2):
                    rows = pl.ds(row + 8 * half, 8)
                    value = f[t][col, z, rows, :] - interp[col, z, rows, :]
                    a[t][col, z, rows, :] = jnp.where(live, value, 0.0)

    def step(i, carry):
        carry = list(carry)
        base = BLOCK_Z - 1 - i
        z = base + 3
        at = clip(z, top1)
        low = layer_below(at, edge_z)
        after_a = stencil(get1, at, low)
        after_b = stencil(getb, at, low)
        put(g, ca1, halos.at[1], at, after_a)
        put(g, cb1, halos.at[2], at, after_b)
        row = jnp.minimum(at, BLOCK_Z - 1)
        counts = between(z)
        inside = jnp.full(TILE, counts, F32) > 0.5
        for pair in range(g.pairs):
            col = pair % g.ct
            live = masks[2, 0, pair] * counts > 0.5
            for half, rows in enumerate(pair_tile_rows(g, pair)):
                vt = pair // g.ct * 2 + half
                one, two = a1[col, row, rows, :], jnp.where(inside, b1[col, row, rows, :], 0.0)
                carry[3] = carry[3] + one * two
                carry[4] = carry[4] + two * two
                parts = [a2[col, row, rows, :]] + [
                    jnp.where(live, value, 0.0) for value in (ca0[col, row, rows, :], after_a[col, vt], after_b[col, vt])
                ]
                slot = 5
                for m in range(4):
                    for n in range(max(m, 1), 4):
                        carry[slot] = carry[slot] + parts[m] * parts[n]
                        slot += 1
        at = clip(base + 2, top0)
        after = stencil(get0, at, layer_below(at, edge_z))
        put(g, ca0, halos.at[0], at, after)
        far = jnp.where(at >= BLOCK_Z, 1, 0)
        for (col, vt), value in after.items():
            if vt == g.vt:
                live = (live1[0][col] & (at < BLOCK_Z)) | (live1[1][col] & (at >= BLOCK_Z))
                b1_halo[col, at] = jnp.where(live, value, 0.0)
            else:
                mask = masks[1, far, vt // 2 * g.ct + col]
                b1[col, at, tile_rows(vt), :] = jnp.where(mask > 0.5, value, 0.0)
        at = clip(base + 1, BLOCK_Z - 1)
        counts = between(base + 1)
        for pair in range(g.pairs):
            col = pair % g.ct
            peak = peaks[pair]
            for rows in pair_tile_rows(g, pair):
                mean = interp[col, at, rows, :]
                for t in range(3):
                    value = jnp.where(masks[t, 0, pair] > 0.5, f[t][col, at, rows, :] - mean, 0.0)
                    a[t][col, at, rows, :] = value
                    counted = jnp.where(masks[t, 0, pair] * counts > 0.5, value, 0.0)
                    carry[t] = carry[t] + counted * counted
                    if t == 0:
                        peak = jnp.maximum(peak, jnp.abs(counted))
            peaks[pair] = peak
        at = clip(base, BLOCK_Z - 1)
        for t in range(3):
            convert(g, meta, t, held, OFFSET[t], at, f[t], left)
        return tuple(carry)

    carry = (jnp.zeros(TILE, F32),) * (3 + 11)
    writes = []
    outs = ((a0, a0_out, BLOCK_Z), (a1, a1_out, BLOCK_Z), (a2, a2_out, BLOCK_Z + 1),
            (ca0, ca0_out, BLOCK_Z + 1), (ca1, ca1_out, BLOCK_Z + 1), (cb1, cb1_out, BLOCK_Z + 1))
    bounds = (0, split, split + 5, BLOCK_Z + 3)
    for index in range(3):
        if index == 1:
            for copy in groups[1]:
                copy.wait()
        carry = lax.fori_loop(bounds[index], bounds[index + 1], step, carry)
        lowest = BLOCK_Z - bounds[index + 1] + 3
        highest = BLOCK_Z - bounds[index] + 2 if index else top1
        for which, (source, target, layers) in enumerate(outs):
            for col in range(g.ct):
                span = slice(lowest, min(highest + 1, layers))
                sem = out_sems.at[(index * 6 + which) * g.ct + col]
                writes.append(pltpu.make_async_copy(source.at[col, span], target.at[col, span], sem))
                writes[-1].start()
    values = [carry[0], carry[1], carry[3], carry[4], carry[2]] + list(carry[5:])
    out[...] = spread_rows(values, out.shape[0])
    for write in writes:
        write.wait()


def weight_of(total, count):
    return 1.0 / (1.0 + jnp.sqrt(jnp.maximum(total, 0.0) / count))


def lane_values(line, count):
    lane = lax.broadcasted_iota(jnp.int32, line.shape, 1)
    return [jnp.sum(jnp.where(lane == i, line, 0.0), axis=1, keepdims=True) for i in range(count)]


def live_cells(g, meta, iteration):
    return jnp.full((1, 1), meta[iteration, 122], jnp.int32).astype(F32) * F32(g.cells)


def three_weights(g, meta, parts):
    q = lane_values(jnp.sum(parts[...], axis=0, keepdims=True), PRODUCTS)
    w0 = weight_of(q[0], live_cells(g, meta, 0))
    w1 = weight_of(q[1] - 2.0 * w0 * q[2] + w0 * w0 * q[3], live_cells(g, meta, 1))
    f = [jnp.ones_like(w0), -w0, -w1, w0 * w1]
    total, at = jnp.zeros_like(w0), 4
    for i in range(4):
        for j in range(i, 4):
            total = total + (1.0 if i == j else 2.0) * f[i] * f[j] * q[at]
            at += 1
    return [jnp.broadcast_to(w, TILE) for w in (w0, w1, weight_of(total, live_cells(g, meta, 2)))]


def last_body(g, meta, parts, strips, interp_halo, halos_in, peaks0, a1_in, a2_in, interp_in, ca0_in, ca1_in, cb1_in,
              *rest):
    data, rest = rest[: g.zm], rest[g.zm :]
    (r2_out, r3_out, errors, out, weights,
     held, f3, a1, a2, interp, ca0, ca1, cb1, r2, r2_halo, change, r3, masks, peaks, sems, out_sems) = rest
    top = LAYERS[2] - 1
    chunks = segments(top, (5, 4, 4, 4))
    reads, at = [], 0
    for lowest, highest in chunks:
        group = []
        if not reads:
            for k in range(g.zm):
                group.append(pltpu.make_async_copy(data[k], held.at[k], sems.at[at]))
                at += 1
        for source, target, layers in ((ca0_in, ca0, BLOCK_Z + 1), (ca1_in, ca1, BLOCK_Z + 1), (cb1_in, cb1, BLOCK_Z + 1),
                                       (a1_in, a1, BLOCK_Z), (a2_in, a2, BLOCK_Z + 1), (interp_in, interp, BLOCK_Z)):
            for col in range(g.ct):
                span = slice(lowest, min(highest + 1, layers))
                group.append(pltpu.make_async_copy(source.at[col, span], target.at[col, span], sems.at[at]))
                at += 1
        reads.append(group)
    for group in reads:
        for copy in group:
            copy.start()
    edge_z, edge_v = edges(meta)
    stencil = Stencil(g, edge_v)
    left = lane_ids() < HALF
    fill_masks(g, meta, masks, (1, 2, 3), left)
    w0, w1, w2 = three_weights(g, meta, parts)
    w01 = w0 * w1
    weights[0], weights[1], weights[2] = w0, w1, w2
    live = halo_live(g, meta, 2, left)
    peaks[...] = jnp.zeros_like(peaks)
    first = sum(LAYERS[:2])
    for col in range(g.ct):
        for z in range(LAYERS[2]):
            value = interp_halo[col, z] + w0 * halos_in[0, col, z] + w1 * halos_in[1, col, z] - w01 * halos_in[2, col, z]
            r2_halo[col, z] = jnp.where(live[z >= BLOCK_Z][col], strip_tile(strips, first + z, col) - value, 0.0)
    get = reader(g, r2, r2_halo)

    def step(i, total):
        base = top - i
        z = base + 1
        at = clip(z, BLOCK_Z - 1)
        counts = between(z)
        after = stencil(get, at, layer_below(at, edge_z))
        for pair in range(g.pairs):
            col = pair % g.ct
            mask = masks[2, 0, pair] * counts > 0.5
            peak = peaks[2, pair]
            for half, rows in enumerate(pair_tile_rows(g, pair)):
                value = f3[col, at, rows, :] - interp[col, at, rows, :] - change[col, at, rows, :]
                value = jnp.where(mask, value - w2 * after[col, pair // g.ct * 2 + half], 0.0)
                r3[col, at, rows, :] = value
                total = total + value * value
                peak = jnp.maximum(peak, jnp.abs(value))
            peaks[2, pair] = peak
        at = clip(base, top)
        far = jnp.where(at >= BLOCK_Z, 1, 0)
        own = jnp.minimum(at, BLOCK_Z - 1)
        inside = jnp.full(TILE, between(at), F32) > 0.5
        for pair in range(g.pairs):
            col = pair % g.ct
            mask1, mask2 = masks[0, 0, pair] > 0.5, masks[1, far, pair] > 0.5
            peak1, peak2 = peaks[0, pair], peaks[1, pair]
            for rows in pair_tile_rows(g, pair):
                zero = w0 * ca0[col, at, rows, :]
                whole = zero + w1 * ca1[col, at, rows, :] - w01 * cb1[col, at, rows, :]
                change[col, at, rows, :] = whole
                value = a2[col, at, rows, :] - jnp.where(mask2, whole, 0.0)
                r2[col, at, rows, :] = value
                peak2 = jnp.maximum(peak2, jnp.where(inside, jnp.abs(value), 0.0))
                value = a1[col, own, rows, :] - jnp.where(mask1, zero, 0.0)
                peak1 = jnp.maximum(peak1, jnp.where(inside, jnp.abs(value), 0.0))
            peaks[0, pair] = peak1
            peaks[1, pair] = peak2
        convert(g, meta, ITERS - 1, held, 0, own, f3, left)
        return total

    total, start, writes = jnp.zeros(TILE, F32), 0, []
    for index, (lowest, highest) in enumerate(chunks):
        for copy in reads[index]:
            copy.wait()
        stop = top - lowest + 1 + (1 if lowest == 0 else 0)
        total = lax.fori_loop(start, stop, step, total)
        start = stop
        below = lowest + 1 if lowest else 0
        above = min((chunks[index - 1][0] if index else BLOCK_Z - 1), BLOCK_Z - 1)
        for which, (source, target, layers) in enumerate(
            ((r2, r2_out, slice(lowest, min(highest, BLOCK_Z - 1) + 1)), (r3, r3_out, slice(below, above + 1)))
        ):
            for col in range(g.ct):
                sem = out_sems.at[(index * 2 + which) * g.ct + col]
                writes.append(pltpu.make_async_copy(source.at[col, layers], target.at[col, layers], sem))
                writes[-1].start()

    line = spread_rows([total], 1)
    lane = lax.broadcasted_iota(jnp.int32, (1, 128), 1)
    lane_p = lax.broadcasted_iota(jnp.int32, (g.pairs, 128), 1)
    row_p = lax.broadcasted_iota(jnp.int32, (g.pairs, 128), 0)
    for i in range(ITERS):
        tiles = [peaks0[pair] if i == 0 else peaks[i - 1, pair] for pair in range(g.pairs)]
        rows = jnp.concatenate([jnp.max(tile, axis=0, keepdims=True) for tile in tiles], 0)
        found = jnp.zeros((1, 128), F32)
        for half in range(2):
            inside = lane_p // HALF == half
            column = jnp.max(jnp.where(inside, rows, 0.0), axis=1, keepdims=True)
            place = row_p // g.ct * g.cb + row_p % g.ct * 2 + half
            found = found + jnp.sum(jnp.where(lane_p == place, column, 0.0), axis=0, keepdims=True)
        errors[i : i + 1, :] = found
        line = jnp.where(lane == 1 + i, jnp.max(found, axis=1, keepdims=True), line)
    out[...] = jnp.broadcast_to(line, out.shape)
    for write in writes:
        write.wait()


def assemble_body(g, meta, weights, table_in, a0_in, a1_in, ca0_in, r2_in, grown_out,
                  table, a0, a1, ca0, r2, grown, masks, sems):
    copies = [pltpu.make_async_copy(table_in, table, sems.at[0])]
    for i, (source, target) in enumerate(((a0_in, a0), (a1_in, a1), (ca0_in, ca0), (r2_in, r2))):
        for col in range(g.ct):
            copies.append(pltpu.make_async_copy(source.at[col, 0:BLOCK_Z], target.at[col], sems.at[1 + i * g.ct + col]))
    for copy in copies:
        copy.start()
    fill_masks(g, meta, masks, (1,), lane_ids() < HALF)
    w0, w1, w2 = weights[0], weights[1], weights[2]
    w01 = w0 * w1
    for copy in copies:
        copy.wait()

    @pl.loop(0, BLOCK_Z)
    def _(z):
        for pair in range(g.pairs):
            col = pair % g.ct
            lanes = slice(col * LANES, (col + 1) * LANES)
            mask = masks[0, 0, pair] > 0.5
            for vt in (pair // g.ct * 2, pair // g.ct * 2 + 1):
                rows = tile_rows(vt)
                value = w0 * a0[col, z, rows, :] + w1 * a1[col, z, rows, :] + w2 * r2[col, z, rows, :]
                value = value - jnp.where(mask, w01 * ca0[col, z, rows, :], 0.0)
                grown[z, rows, lanes] = table[z, rows, lanes] + value

    write = pltpu.make_async_copy(grown, grown_out, sems.at[0])
    write.start()
    write.wait()


def finish_body(g, meta, parts, grown_in, r3_in, out_hbm, worst, grown, r3, out, sems, out_sems):
    quarter = BLOCK_Z // 4
    reads, at = [], 0
    for part in range(4):
        layers = slice(part * quarter, (part + 1) * quarter)
        group = [pltpu.make_async_copy(grown_in.at[layers], grown.at[layers], sems.at[at])]
        for col in range(g.ct):
            group.append(pltpu.make_async_copy(r3_in.at[col, layers], r3.at[col, layers], sems.at[at + 1 + col]))
        at += 1 + g.ct
        reads.append(group)
    for group in reads:
        for copy in group:
            copy.start()
    total = lane_values(jnp.sum(parts[...], axis=0, keepdims=True), 1)[0]
    w3 = jnp.broadcast_to(weight_of(total, live_cells(g, meta, 3)), TILE)
    line = jnp.max(parts[...], axis=0, keepdims=True)
    for i, value in enumerate(lane_values(line, 1 + ITERS)[1:]):
        worst[i] = jnp.max(value)
    writes = []
    for part in range(4):
        for copy in reads[part]:
            copy.wait()
        layers = slice(part * quarter, (part + 1) * quarter)
        for z in range(part * quarter, (part + 1) * quarter):
            for col in range(g.ct):
                lanes = slice(col * LANES, (col + 1) * LANES)
                for vt in range(g.vt):
                    rows = tile_rows(vt)
                    out[z, rows, lanes] = grown[z, rows, lanes] + w3 * r3[col, z, rows, :]
        writes.append(pltpu.make_async_copy(out.at[layers], out_hbm.at[layers], out_sems.at[part]))
        writes[-1].start()
    for write in writes:
        write.wait()


def index_table(g, assign):
    zm_here, zv_here = lax.axis_index("zm"), lax.axis_index("zv")
    me = zm_here * g.zv + zv_here
    slots = assign.reshape(ITERS, -1)
    owner = jnp.arange(slots.shape[1]) // g.slots // g.zv
    owner = jnp.where(jnp.arange(ITERS)[:, None] == ITERS - 1, owner ^ zm_here, owner)
    column = jnp.arange(2 * g.blocks + 2 * g.cb)
    here = column % g.blocks
    far = jnp.where(column < 2 * g.blocks, column // g.blocks, (column - 2 * g.blocks) // g.cb)
    local = jnp.where(column < 2 * g.blocks, here, (column - 2 * g.blocks) % g.cb)
    side = jnp.where(column < 2 * g.blocks, 0, 1)
    inside = (zm_here + far < g.zm) & (zv_here + side < g.zv)
    target = jnp.where(inside, (me + far * g.zv + side) * g.blocks + local, -2)
    found = jnp.max(jnp.where(slots[:, None, :] == target[None, :, None], owner[:, None, :], -1), axis=2)
    count = jnp.sum((slots >= 0).astype(jnp.int32), axis=1, keepdims=True)
    flags = jnp.stack([zm_here == g.zm - 1, zv_here == g.zv - 1]).astype(jnp.int32)
    gap = jnp.zeros((ITERS, 120 - found.shape[1]), jnp.int32)
    flags = jnp.broadcast_to(flags[None, :], (ITERS, 2))
    return jnp.concatenate([found, gap, flags, count, jnp.zeros((ITERS, 5), jnp.int32)], axis=1)


def to_all(rows):
    count = lax.axis_size("zm") * lax.axis_size("zv")
    return lax.all_to_all(rows.reshape(count, 1, 128), AXES, 0, 0, tiled=True).reshape(count, 128)


def from_next(value, axis):
    count = lax.axis_size(axis)
    return lax.ppermute(value, axis, [(i, i - 1) for i in range(1, count)])


def shards(table, refined, assign):
    g = Shape(table.shape, assign.shape, lax.axis_size("zm"), lax.axis_size("zv"))
    everyone = g.zm * g.zv
    part = functools.partial
    slots = assign.transpose(0, 2, 1).reshape(ITERS * g.slots, -1)
    views = refined.reshape(ITERS * g.slots, BLOCK_Z // 8, 8, PAIRS, LANES).transpose(0, 1, 3, 2, 4)
    views = views.reshape(ITERS * g.slots, ROWS, LANES)
    vmem = lambda *shape: pltpu.VMEM(shape, F32)
    main, halo = g.main, g.halo

    below = from_next(table[:ITERS], "zm")
    packed = call(
        part(pack_three_body, g), struct(g.zm, OFFSET[3], LANES), [SMEM, HBM], HBM,
        [pltpu.SMEM((ITERS, g.zm), jnp.int32), vmem(g.zm, OFFSET[3], LANES), dma(3 * g.zm), dma(3 * g.zm + 3)],
        WHOLE,
    )(slots, views)
    data = lax.all_to_all(packed, "zm", 0, 0, tiled=True)
    strip = from_next(jnp.concatenate([table[:, :8], below[:, :8]], 0), "zv")
    packed = call(
        part(pack_last_body, g), [struct(ROWS, LANES)] * g.zm, [SMEM, HBM], [VMEM] * g.zm,
        [pltpu.SMEM((ITERS, g.zm), jnp.int32), dma(g.zm)], PART,
    )(slots, views)
    last_data = [packed[0]]
    for k in range(1, g.zm):
        last_data.append(lax.ppermute(packed[k], "zm", [(i, i ^ k) for i in range(g.zm)]))
    meta = index_table(g, assign)
    interp, interp_halo = call(
        part(interp_body, g), [struct(*main(LAYERS[0])), struct(*halo(LAYERS[0]))],
        [SMEM] + [VMEM] * 3, [VMEM] * 2, [vmem(*main(DEEP)), vmem(*halo(DEEP))], PART,
    )(meta, table, below, strip)

    strips = call(
        part(strip_body, g), struct(sum(LAYERS[:3]), *TILE), [SMEM] + [HBM] * 3, VMEM,
        [vmem(3 * g.cb, LAYERS[0] * PAIRS, LANES), vmem(g.ct, sum(LAYERS[:3]), BLOCK_V, LANES), dma(6 * g.cb)],
        PART,
    )(meta, data, interp_halo, packed[0])
    strips = from_next(strips, "zv")
    own, more = struct(*main(BLOCK_Z)), struct(*main(LAYERS[2]))
    products, a0, a1, a2, ca0, ca1, cb1, halos, peaks0 = call(
        part(middle_body, g),
        [struct(everyone, 128), own, own, more, more, more, more, struct(3, *halo(LAYERS[1])), struct(g.pairs, *TILE)],
        [SMEM] + [VMEM] * 2 + [HBM] * 2, [VMEM] + [HBM] * 6 + [VMEM] * 2,
        [vmem(*data.shape), vmem(*main(LAYERS[0]))] + [vmem(*main(LAYERS[0] + 1))] * 10
        + [vmem(*halo(LAYERS[0] + 1))] * 3 + [vmem(3, 2, g.pairs, *TILE), dma(6 + 2 * g.ct), dma(18 * g.ct)],
        WHOLE,
    )(meta, strips, interp_halo, data, interp)
    products = to_all(products)
    r2, r3, errors, stats, weights = call(
        part(last_body, g), [own, own, struct(ITERS, 128), struct(everyone, 128), struct(3, *TILE)],
        [SMEM] + [VMEM] * 5 + [HBM] * (6 + g.zm), [HBM] * 2 + [VMEM] * 3,
        [vmem(g.zm, ROWS, LANES), vmem(*main(BLOCK_Z)), vmem(*main(BLOCK_Z)), vmem(*main(LAYERS[2])), vmem(*main(BLOCK_Z))]
        + [vmem(*main(LAYERS[2]))] * 4 + [vmem(*halo(LAYERS[2])), vmem(*main(LAYERS[2])), vmem(*main(BLOCK_Z)),
           vmem(3, 2, g.pairs, *TILE), vmem(3, g.pairs, *TILE), dma(g.zm + 24 * g.ct), dma(8 * g.ct)],
        WHOLE,
    )(meta, products, strips, interp_halo, halos, peaks0, a1, a2, interp, ca0, ca1, cb1, *last_data)
    stats = to_all(stats)
    grown = call(
        part(assemble_body, g), struct(*table.shape), [SMEM, VMEM] + [HBM] * 5, HBM,
        [vmem(*table.shape)] + [vmem(*main(BLOCK_Z))] * 4 + [vmem(*table.shape), vmem(1, 2, g.pairs, *TILE), dma(1 + 4 * g.ct)],
        WHOLE,
    )(meta, weights, table, a0, a1, ca0, r2)
    table_out, worst = call(
        part(finish_body, g), [struct(*table.shape), struct(ITERS)], [SMEM, VMEM] + [HBM] * 2, [HBM, SMEM],
        [vmem(*table.shape), vmem(*main(BLOCK_Z)), vmem(*table.shape), dma(4 * (1 + g.ct)), dma(4)], WHOLE,
    )(meta, stats, grown, r3)
    return (table_out, errors[:, : g.blocks], worst)


def solution(mesh):
    in_specs = (P("zm", "zv", None), P(None, ("zm", "zv"), None, None), P())
    out_specs = (P("zm", "zv", None), P(None, ("zm", "zv")), P())

    return jax.shard_map(shards, mesh=mesh, in_specs=in_specs, out_specs=out_specs, check_vma=False)
```

profile of v0, /device:TPU:0, one launch (start us, length us, event | category | flops | bytes accessed | tf_op | source)
XLA Modules:
  0.0 106.2 jit_solution(823245920404353057)
XLA Ops:
  0.6 4.2 %shard_map.58 = f32[8,432,128]{2,1,0:T(8,128)} custom-call(s32[32,32]{1,0:T(8,128)} %bitcast.22, f32[32,128,128]{2,1,0:T(8,128)} %bitcast.20), custom_call_target="tpu_custom_call" | custom-call | flops 2000000 | bytes 1048576 | tf_op jit(solution)/shard_map/pallas_call | solution.py:732
  4.8 0.0 copy-start.2
  4.8 0.0 copy-start.6
  4.9 5.2 %all-to-all-start = ((f32[8,432,128]{2,1,0:T(8,128)}), f32[8,432,128]{2,1,0:T(8,128)S(1)}, u32[]{:S(2)}, u32[]{:S(2)}) async-start(f32[8,432,128]{2,1,0:T(8,128)} %shard_map.58), calls=%async_computation | async-start | bytes 3538944 | tf_op jit(solution)/shard_map/all_to_all | solution.py:737
  10.1 1.3 %collective-permute-start = (f32[4,64,256]{2,1,0:T(8,128)S(1)}, f32[4,64,256]{2,1,0:T(8,128)S(1)}, u32[]{:S(2)}, u32[]{:S(2)}) collective-permute-start(f32[4,64,256]{2,1,0:T(8,128)S(1)} %slice.12), channel_id=1, source_target_pairs={{4,0},{8,4},{12,8},{16,12},{20,16},{24,20},{28,24},{5,1},{9,5},{13... | collective-permute-start | bytes 786440 | tf_op jit(solution)/shard_map/ppermute | solution.py:718
  11.4 0.2 convert_reduce_fusion
  11.6 0.1 broadcast_select_fusion
  11.7 1.8 %collective-permute-done.below = f32[4,64,256]{2,1,0:T(8,128)S(1)} collective-permute-done((f32[4,64,256]{2,1,0:T(8,128)S(1)}, f32[4,64,256]{2,1,0:T(8,128)S(1)}, u32[]{:S(2)}, u32[]{:S(2)}) %collective-permute-start) | collective-permute-done | bytes 262176 | tf_op jit(solution)/shard_map/ppermute | solution.py:718
  13.5 0.7 pad_maximum_fusion
  14.2 1.3 %collective-permute-start.1 = (f32[20,8,256]{2,1,0:T(8,128)}, f32[20,8,256]{2,1,0:T(8,128)S(1)}, u32[]{:S(2)}, u32[]{:S(2)}) collective-permute-start(f32[20,8,256]{2,1,0:T(8,128)} %pad_maximum_fusion), channel_id=1, source_target_pairs={{1,0},{2,1},{3,2},{5,4},{6,5},{7,6},{9,8},{10,9},{11,10},{13,12},{... | collective-permute-start | bytes 491528 | tf_op jit(solution)/shard_map/ppermute | solution.py:718
  15.5 0.1 add_convert_fusion
  15.6 0.1 copy.13
  15.6 0.1 copy.14
  15.7 0.1 eq.32
  15.8 0.2 select_reduce_fusion
  16.1 0.1 concatenate.10.meta
  16.2 1.6 %copy-done.1 = f32[4,8,16,1024]{3,2,1,0:T(8,128)S(1)} copy-done((f32[4,8,16,1024]{3,2,1,0:T(8,128)S(1)}, f32[4,8,16,1024]{3,2,1,0:T(8,128)}, u32[]{:S(2)}) %copy-start.1) | copy-done | bytes 2097176
  17.8 1.7 %shard_map.60 = (f32[128,128]{1,0:T(8,128)S(1)}, f32[128,128]{1,0:T(8,128)S(1)}, f32[128,128]{1,0:T(8,128)S(1)}, f32[128,128]{1,0:T(8,128)S(1)}, f32[128,128]{1,...) custom-call(s32[32,32]{1,0:T(8,128)S(1)} %bitcast.23, ...), custom_call_target="tpu_custom_call" | custom-call | flops 2000000 | bytes 1048576 | tf_op jit(solution)/shard_map/pallas_call | solution.py:739
  19.5 0.6 copy-done.8
  20.1 0.6 copy-done.10
  20.8 0.6 copy-done.12
  21.4 0.6 copy-done.14
  22.0 0.6 copy-done.16
  22.6 0.6 copy-done.18
  23.2 0.0 collective-permute-done.1.strip
  23.2 2.5 %shard_map.59 = (f32[2,19,64,128]{3,2,1,0:T(8,128)S(1)}, f32[2,19,8,128]{3,2,1,0:T(8,128)S(1)}) custom-call(s32[4,128]{1,0:T(4,128)S(1)} %concatenate.10.meta, f32[16,64,256]{2,1,0:T(8,128)S(1)} %copy-done.2, f32[4,64,256]{2,1,0:T(8,128)S(1)} %collective-permute-done.below, f32[20,8,256]{2,1,0:T(8,128)S(1)} %collective-permute-done.1.strip), custom_call_target="tpu_custom_call" | custom-call | flops 2000000 | bytes 1048576 | tf_op jit(solution)/shard_map/pallas_call | solution.py:747
  25.8 1.1 %copy-done.3 = f32[2,19,64,128]{3,2,1,0:T(8,128)} copy-done((f32[2,19,64,128]{3,2,1,0:T(8,128)}, f32[2,19,64,128]{3,2,1,0:T(8,128)S(1)}, u32[]{:S(2)}) %copy-start.3) | copy-done | bytes 1245208
  26.9 6.3 %all-to-all-done.data = f32[8,432,128]{2,1,0:T(8,128)S(1)} async-done(((f32[8,432,128]{2,1,0:T(8,128)}), f32[8,432,128]{2,1,0:T(8,128)S(1)}, u32[]{:S(2)}, u32[]{:S(2)}) %all-to-all-start) | async-done | bytes 1769504 | tf_op jit(solution)/shard_map/all_to_all | solution.py:737
  33.2 2.6 %shard_map.61 = f32[54,8,128]{2,1,0:T(8,128)S(1)} custom-call(s32[4,128]{1,0:T(4,128)S(1)} %concatenate.10.meta, f32[8,432,128]{2,1,0:T(8,128)S(1)} %all-to-all-done.data, f32[2,19,8,128]{3,2,1,0:T(8,128)S(1)} %get-tuple-element.29.unused_a.interp_halo, f32[128,128]{1,0:T(8,128)S(1)} %get-tuple-element.30.unused_b.rest_0_), custom_call_target="tpu_custom_call" | custom-call | flops 2000000 | bytes 1048576 | tf_op jit(solution)/shard_map/pallas_call | solution.py:752
  35.8 1.3 %collective-permute-start.2 = (f32[54,8,128]{2,1,0:T(8,128)S(1)}, f32[54,8,128]{2,1,0:T(8,128)S(1)}, u32[]{:S(2)}, u32[]{:S(2)}) collective-permute-start(f32[54,8,128]{2,1,0:T(8,128)S(1)} %shard_map.61), channel_id=1, source_target_pairs={{1,0},{2,1},{3,2},{5,4},{6,5},{7,6},{9,8},{10,9},{11,10},{13,12},{... | collective-permute-start | bytes 663560 | tf_op jit(solution)/shard_map/ppermute | solution.py:718
  37.1 15.2 %collective-permute-start.3 = (f32[128,128]{1,0:T(8,128)S(1)}, f32[128,128]{1,0:T(8,128)S(1)}, u32[]{:S(2)}, u32[]{:S(2)}) collective-permute-start(f32[128,128]{1,0:T(8,128)S(1)} %copy-done.19), channel_id=1, source_target_pairs={{0,4},{4,0},{8,12},{12,8},{16,20},{20,16},{24,28},{28,24},{1,5},{5... | collective-permute-start | bytes 196616 | tf_op jit(solution)/shard_map/ppermute | solution.py:745
  52.3 1.5 %collective-permute-start.4 = (f32[128,128]{1,0:T(8,128)S(1)}, f32[128,128]{1,0:T(8,128)S(1)}, u32[]{:S(2)}, u32[]{:S(2)}) collective-permute-start(f32[128,128]{1,0:T(8,128)S(1)} %copy-done.17), channel_id=1, source_target_pairs={{0,8},{4,12},{8,0},{12,4},{16,24},{20,28},{24,16},{28,20},{1,9},{5... | collective-permute-start | bytes 196616 | tf_op jit(solution)/shard_map/ppermute | solution.py:745
  53.8 0.0 collective-permute-start.5
  53.8 1.4 %collective-permute-start.6 = (f32[128,128]{1,0:T(8,128)S(1)}, f32[128,128]{1,0:T(8,128)S(1)}, u32[]{:S(2)}, u32[]{:S(2)}) collective-permute-start(f32[128,128]{1,0:T(8,128)S(1)} %copy-done.13), channel_id=1, source_target_pairs={{0,16},{4,20},{8,24},{12,28},{16,0},{20,4},{24,8},{28,12},{1,17},{... | collective-permute-start | bytes 196616 | tf_op jit(solution)/shard_map/ppermute | solution.py:745
  55.2 0.6 collective-permute-start.7
  55.8 0.7 collective-permute-done.4.rest_2_
  56.5 1.0 collective-permute-start.8
  57.5 0.8 collective-permute-start.9
  58.4 10.4 %shard_map.62 = (f32[32,128]{1,0:T(8,128)}, f32[2,16,64,128]{3,2,1,0:T(8,128)}, f32[2,16,64,128]{3,2,1,0:T(8,128)}, f32[2,17,64,128]{3,2,1,0:T(8,128)}, f32[2,17...) custom-call(s32[4,128]{1,0:T(4,128)} %copy-done.7, ...), custom_call_target="tpu_custom_call" | custom-call | flops 2000000 | bytes 1048576 | tf_op jit(solution)/shard_map/pallas_call | solution.py:759
  68.8 8.2 %all-to-all-start.1 = ((f32[32,1,128]{2,1,0:T(1,128)}), f32[32,1,128]{2,1,0:T(1,128)S(1)}, u32[]{:S(2)}, u32[]{:S(2)}) async-start(f32[32,1,128]{2,1,0:T(1,128)} %bitcast.26), calls=%async_computation.1 | async-start | bytes 32768 | tf_op jit(solution)/shard_map/all_to_all | solution.py:713
  77.1 7.1 %all-to-all-done.1 = f32[32,1,128]{2,1,0:T(1,128)S(1)} async-done(((f32[32,1,128]{2,1,0:T(1,128)}), f32[32,1,128]{2,1,0:T(1,128)S(1)}, u32[]{:S(2)}, u32[]{:S(2)}) %all-to-all-start.1) | async-done | bytes 16416 | tf_op jit(solution)/shard_map/all_to_all | solution.py:713
  84.3 0.5 copy-done.28
  84.8 7.4 %shard_map.63 = (f32[2,16,64,128]{3,2,1,0:T(8,128)}, f32[2,16,64,128]{3,2,1,0:T(8,128)}, f32[4,128]{1,0:T(4,128)}, f32[32,128]{1,0:T(8,128)}, f32[3,8,128]{2,1,0:T(8,128)}) custom-call(s32[4,128]{1,0:T(4,128)} %copy-done.7, f32[32,128]{1,0:T(8,128)} %bitcast.24, f32[54,8,128]{2,1,0:T(8,128)} %copy-done.20, f32[2,19,8,128]{3,2,1,0:T(8,128)} %copy-done.4, ...), custom_call_target="tpu_custom_call" | custom-call | flops 2000000 | bytes 1048576 | tf_op jit(solution)/shard_map/pallas_call | solution.py:768
  92.3 2.5 %all-to-all-start.2 = ((f32[32,1,128]{2,1,0:T(1,128)}), f32[32,1,128]{2,1,0:T(1,128)S(1)}, u32[]{:S(2)}, u32[]{:S(2)}) async-start(f32[32,1,128]{2,1,0:T(1,128)} %bitcast.27), calls=%async_computation.2 | async-start | bytes 32768 | tf_op jit(solution)/shard_map/all_to_all | solution.py:713
  94.8 4.7 %shard_map.64.grown_in = f32[16,64,256]{2,1,0:T(8,128)} custom-call(s32[4,128]{1,0:T(4,128)} %copy-done.7, f32[3,8,128]{2,1,0:T(8,128)} %get-tuple-element.48.weights, f32[16,64,256]{2,1,0:T(8,128)} %table_in.1, f32[2,16,64,128]{3,2,1,0:T(8,128)} %get-tuple-element.49.a0_in, f32[2,16,64,128]{3,2,1,0:T(8,128)} %get-tuple-element.35.a1_in, ...), custom_call_target="tpu_custom_call" | custom-call | flops 2000000 | bytes 1048576 | tf_op jit(solution)/shard_map/pallas_call | solution.py:777
  99.4 2.5 %all-to-all-done.2 = f32[32,1,128]{2,1,0:T(1,128)S(1)} async-done(((f32[32,1,128]{2,1,0:T(1,128)}), f32[32,1,128]{2,1,0:T(1,128)S(1)}, u32[]{:S(2)}, u32[]{:S(2)}) %all-to-all-start.2) | async-done | bytes 16416 | tf_op jit(solution)/shard_map/all_to_all | solution.py:713
  102.0 0.6 copy-done.29
  102.6 3.7 %shard_map.65 = (f32[16,64,256]{2,1,0:T(8,128)}, f32[4]{0:T(128)}) custom-call(s32[4,128]{1,0:T(4,128)} %copy-done.7, f32[32,128]{1,0:T(8,128)} %bitcast.25, f32[16,64,256]{2,1,0:T(8,128)} %shard_map.64.grown_in, f32[2,16,64,128]{3,2,1,0:T(8,128)} %get-tuple-element.51.r3_in), custom_call_target="tpu_custom_call" | custom-call | flops 2000000 | bytes 1048576 | tf_op jit(solution)/shard_map/pallas_call | solution.py:782
  (65 shorter events, 0.2 us)
Async XLA Ops:
  4.8 5.2 %copy-start.2 = (f32[16,64,256]{2,1,0:T(8,128)S(1)}, f32[16,64,256]{2,1,0:T(8,128)}, u32[]{:S(2)}) copy-start(f32[16,64,256]{2,1,0:T(8,128)} %table_in.1) | copy-start | bytes 3145732
  4.8 6.6 %copy-start.6 = (s32[4,32,8]{1,2,0:T(8,128)S(1)}, s32[4,32,8]{1,2,0:T(8,128)}, u32[]{:S(2)}) copy-start(s32[4,32,8]{1,2,0:T(8,128)} %param.5) | copy-start | bytes 12292
  4.9 8.7 %slice-start = ((f32[16,64,256]{2,1,0:T(8,128)}), f32[16,8,256]{2,1,0:T(8,128)S(1)}, s32[]{:S(2)}) async-start(f32[16,64,256]{2,1,0:T(8,128)} %table_in.1), calls=%async_computation.3 | async-start | bytes 262144 | tf_op jit(solution)/shard_map/slice | solution.py:738
  4.9 28.3 %all-to-all-start = ((f32[8,432,128]{2,1,0:T(8,128)}), f32[8,432,128]{2,1,0:T(8,128)S(1)}, u32[]{:S(2)}, u32[]{:S(2)}) async-start(f32[8,432,128]{2,1,0:T(8,128)} %shard_map.58), calls=%async_computation | async-start | bytes 3538944 | tf_op jit(solution)/shard_map/all_to_all | solution.py:737
  10.1 3.4 %collective-permute-start = (f32[4,64,256]{2,1,0:T(8,128)S(1)}, f32[4,64,256]{2,1,0:T(8,128)S(1)}, u32[]{:S(2)}, u32[]{:S(2)}) collective-permute-start(f32[4,64,256]{2,1,0:T(8,128)S(1)} %slice.12), channel_id=1, source_target_pairs={{4,0},{8,4},{12,8},{16,12},{20,16},{24,20},{28,24},{5,1},{9,5},{13... | collective-permute-start | bytes 786440 | tf_op jit(solution)/shard_map/ppermute | solution.py:718
  14.2 9.0 %collective-permute-start.1 = (f32[20,8,256]{2,1,0:T(8,128)}, f32[20,8,256]{2,1,0:T(8,128)S(1)}, u32[]{:S(2)}, u32[]{:S(2)}) collective-permute-start(f32[20,8,256]{2,1,0:T(8,128)} %pad_maximum_fusion), channel_id=1, source_target_pairs={{1,0},{2,1},{3,2},{5,4},{6,5},{7,6},{9,8},{10,9},{11,10},{13,12},{... | collective-permute-start | bytes 491528 | tf_op jit(solution)/shard_map/ppermute | solution.py:718
  16.2 1.6 %copy-start.1 = (f32[4,8,16,1024]{3,2,1,0:T(8,128)S(1)}, f32[4,8,16,1024]{3,2,1,0:T(8,128)}, u32[]{:S(2)}) copy-start(f32[4,8,16,1024]{3,2,1,0:T(8,128)} %param.4) | copy-start | bytes 6291460
  17.8 15.4 %copy-start.7 = (s32[4,128]{1,0:T(4,128)}, s32[4,128]{1,0:T(4,128)S(1)}, u32[]{:S(2)}) copy-start(s32[4,128]{1,0:T(4,128)S(1)} %concatenate.10.meta) | copy-start | bytes 6148
  19.5 0.6 copy-start.8
  20.1 0.6 copy-start.10
  20.8 0.6 copy-start.12
  21.4 0.6 copy-start.14
  22.0 0.6 copy-start.16
  22.6 0.6 copy-start.18
  23.2 12.5 %copy-start.5 = (f32[128,128]{1,0:T(8,128)}, f32[128,128]{1,0:T(8,128)S(1)}, u32[]{:S(2)}) copy-start(f32[128,128]{1,0:T(8,128)S(1)} %get-tuple-element.30.unused_b.rest_0_) | copy-start | bytes 196612
  25.8 1.1 %copy-start.3 = (f32[2,19,64,128]{3,2,1,0:T(8,128)}, f32[2,19,64,128]{3,2,1,0:T(8,128)S(1)}, u32[]{:S(2)}) copy-start(f32[2,19,64,128]{3,2,1,0:T(8,128)S(1)} %get-tuple-element.31.interp_in) | copy-start | bytes 3735556
  26.9 31.5 %copy-start.4 = (f32[2,19,8,128]{3,2,1,0:T(8,128)}, f32[2,19,8,128]{3,2,1,0:T(8,128)S(1)}, u32[]{:S(2)}) copy-start(f32[2,19,8,128]{3,2,1,0:T(8,128)S(1)} %get-tuple-element.29.unused_a.interp_halo) | copy-start | bytes 466948
  26.9 10.2 %copy-start.19 = (f32[128,128]{1,0:T(8,128)S(1)}, f32[128,128]{1,0:T(8,128)}, u32[]{:S(2)}) copy-start(f32[128,128]{1,0:T(8,128)} %copy-done.18) | copy-start | bytes 196612
  26.9 25.4 %copy-start.17 = (f32[128,128]{1,0:T(8,128)S(1)}, f32[128,128]{1,0:T(8,128)}, u32[]{:S(2)}) copy-start(f32[128,128]{1,0:T(8,128)} %copy-done.16) | copy-start | bytes 196612
  26.9 26.9 %copy-start.15 = (f32[128,128]{1,0:T(8,128)S(1)}, f32[128,128]{1,0:T(8,128)}, u32[]{:S(2)}) copy-start(f32[128,128]{1,0:T(8,128)} %copy-done.14) | copy-start | bytes 196612
  26.9 26.9 %copy-start.13 = (f32[128,128]{1,0:T(8,128)S(1)}, f32[128,128]{1,0:T(8,128)}, u32[]{:S(2)}) copy-start(f32[128,128]{1,0:T(8,128)} %copy-done.12) | copy-start | bytes 196612
  26.9 28.3 %copy-start.11 = (f32[128,128]{1,0:T(8,128)S(1)}, f32[128,128]{1,0:T(8,128)}, u32[]{:S(2)}) copy-start(f32[128,128]{1,0:T(8,128)} %copy-done.10) | copy-start | bytes 196612
  26.9 29.6 %copy-start.9 = (f32[128,128]{1,0:T(8,128)S(1)}, f32[128,128]{1,0:T(8,128)}, u32[]{:S(2)}) copy-start(f32[128,128]{1,0:T(8,128)} %copy-done.8) | copy-start | bytes 196612
  33.2 25.2 %copy-start = (f32[8,432,128]{2,1,0:T(8,128)}, f32[8,432,128]{2,1,0:T(8,128)S(1)}, u32[]{:S(2)}) copy-start(f32[8,432,128]{2,1,0:T(8,128)S(1)} %all-to-all-done.data) | copy-start | bytes 5308420
  35.8 21.8 %collective-permute-start.2 = (f32[54,8,128]{2,1,0:T(8,128)S(1)}, f32[54,8,128]{2,1,0:T(8,128)S(1)}, u32[]{:S(2)}, u32[]{:S(2)}) collective-permute-start(f32[54,8,128]{2,1,0:T(8,128)S(1)} %shard_map.61), channel_id=1, source_target_pairs={{1,0},{2,1},{3,2},{5,4},{6,5},{7,6},{9,8},{10,9},{11,10},{13,12},{... | collective-permute-start | bytes 663560 | tf_op jit(solution)/shard_map/ppermute | solution.py:718
  37.1 18.1 %collective-permute-start.3 = (f32[128,128]{1,0:T(8,128)S(1)}, f32[128,128]{1,0:T(8,128)S(1)}, u32[]{:S(2)}, u32[]{:S(2)}) collective-permute-start(f32[128,128]{1,0:T(8,128)S(1)} %copy-done.19), channel_id=1, source_target_pairs={{0,4},{4,0},{8,12},{12,8},{16,20},{20,16},{24,28},{28,24},{1,5},{5... | collective-permute-start | bytes 196616 | tf_op jit(solution)/shard_map/ppermute | solution.py:745
  52.3 4.3 %collective-permute-start.4 = (f32[128,128]{1,0:T(8,128)S(1)}, f32[128,128]{1,0:T(8,128)S(1)}, u32[]{:S(2)}, u32[]{:S(2)}) collective-permute-start(f32[128,128]{1,0:T(8,128)S(1)} %copy-done.17), channel_id=1, source_target_pairs={{0,8},{4,12},{8,0},{12,4},{16,24},{20,28},{24,16},{28,20},{1,9},{5... | collective-permute-start | bytes 196616 | tf_op jit(solution)/shard_map/ppermute | solution.py:745
  53.8 23.2 %collective-permute-start.5 = (f32[128,128]{1,0:T(8,128)S(1)}, f32[128,128]{1,0:T(8,128)S(1)}, u32[]{:S(2)}, u32[]{:S(2)}) collective-permute-start(f32[128,128]{1,0:T(8,128)S(1)} %copy-done.15), channel_id=1, source_target_pairs={{0,12},{4,8},{8,4},{12,0},{16,28},{20,24},{24,20},{28,16},{1,13},{... | collective-permute-start | bytes 196616 | tf_op jit(solution)/shard_map/ppermute | solution.py:745
  53.8 23.2 %collective-permute-start.6 = (f32[128,128]{1,0:T(8,128)S(1)}, f32[128,128]{1,0:T(8,128)S(1)}, u32[]{:S(2)}, u32[]{:S(2)}) collective-permute-start(f32[128,128]{1,0:T(8,128)S(1)} %copy-done.13), channel_id=1, source_target_pairs={{0,16},{4,20},{8,24},{12,28},{16,0},{20,4},{24,8},{28,12},{1,17},{... | collective-permute-start | bytes 196616 | tf_op jit(solution)/shard_map/ppermute | solution.py:745
  55.2 29.0 %copy-start.21 = (f32[128,128]{1,0:T(8,128)}, f32[128,128]{1,0:T(8,128)S(1)}, u32[]{:S(2)}) copy-start(f32[128,128]{1,0:T(8,128)S(1)} %collective-permute-done.3.rest_1_) | copy-start | bytes 196612
  55.2 21.9 %collective-permute-start.7 = (f32[128,128]{1,0:T(8,128)S(1)}, f32[128,128]{1,0:T(8,128)S(1)}, u32[]{:S(2)}, u32[]{:S(2)}) collective-permute-start(f32[128,128]{1,0:T(8,128)S(1)} %copy-done.11), channel_id=1, source_target_pairs={{0,20},{4,16},{8,28},{12,24},{16,4},{20,0},{24,12},{28,8},{1,21},{... | collective-permute-start | bytes 196616 | tf_op jit(solution)/shard_map/ppermute | solution.py:745
  56.5 27.7 %copy-start.22 = (f32[128,128]{1,0:T(8,128)}, f32[128,128]{1,0:T(8,128)S(1)}, u32[]{:S(2)}) copy-start(f32[128,128]{1,0:T(8,128)S(1)} %collective-permute-done.4.rest_2_) | copy-start | bytes 196612
  56.5 20.5 %collective-permute-start.8 = (f32[128,128]{1,0:T(8,128)S(1)}, f32[128,128]{1,0:T(8,128)S(1)}, u32[]{:S(2)}, u32[]{:S(2)}) collective-permute-start(f32[128,128]{1,0:T(8,128)S(1)} %copy-done.9), channel_id=1, source_target_pairs={{0,24},{4,28},{8,16},{12,20},{16,8},{20,12},{24,0},{28,4},{1,25},{... | collective-permute-start | bytes 196616 | tf_op jit(solution)/shard_map/ppermute | solution.py:745
  57.5 0.8 copy-start.20
  57.5 19.5 %collective-permute-start.9 = (f32[128,128]{1,0:T(8,128)S(1)}, f32[128,128]{1,0:T(8,128)S(1)}, u32[]{:S(2)}, u32[]{:S(2)}) collective-permute-start(f32[128,128]{1,0:T(8,128)S(1)} %get-tuple-element.46), channel_id=1, source_target_pairs={{0,28},{4,24},{8,20},{12,16},{16,12},{20,8},{24,4},{28,0},{1,29},{... | collective-permute-start | bytes 196616 | tf_op jit(solution)/shard_map/ppermute | solution.py:745
  68.8 15.4 %all-to-all-start.1 = ((f32[32,1,128]{2,1,0:T(1,128)}), f32[32,1,128]{2,1,0:T(1,128)S(1)}, u32[]{:S(2)}, u32[]{:S(2)}) async-start(f32[32,1,128]{2,1,0:T(1,128)} %bitcast.26), calls=%async_computation.1 | async-start | bytes 32768 | tf_op jit(solution)/shard_map/all_to_all | solution.py:713
  77.0 7.2 %copy-start.23 = (f32[128,128]{1,0:T(8,128)}, f32[128,128]{1,0:T(8,128)S(1)}, u32[]{:S(2)}) copy-start(f32[128,128]{1,0:T(8,128)S(1)} %collective-permute-done.5.rest_3_) | copy-start | bytes 196612
  77.0 7.2 %copy-start.24 = (f32[128,128]{1,0:T(8,128)}, f32[128,128]{1,0:T(8,128)S(1)}, u32[]{:S(2)}) copy-start(f32[128,128]{1,0:T(8,128)S(1)} %collective-permute-done.6.rest_4_) | copy-start | bytes 196612
  77.1 7.2 %copy-start.25 = (f32[128,128]{1,0:T(8,128)}, f32[128,128]{1,0:T(8,128)S(1)}, u32[]{:S(2)}) copy-start(f32[128,128]{1,0:T(8,128)S(1)} %collective-permute-done.7.rest_5_) | copy-start | bytes 196612
  77.1 7.2 %copy-start.26 = (f32[128,128]{1,0:T(8,128)}, f32[128,128]{1,0:T(8,128)S(1)}, u32[]{:S(2)}) copy-start(f32[128,128]{1,0:T(8,128)S(1)} %collective-permute-done.8.rest_6_) | copy-start | bytes 196612
  77.1 7.2 %copy-start.27 = (f32[128,128]{1,0:T(8,128)}, f32[128,128]{1,0:T(8,128)S(1)}, u32[]{:S(2)}) copy-start(f32[128,128]{1,0:T(8,128)S(1)} %collective-permute-done.9.rest_7_) | copy-start | bytes 196612
  84.2 0.6 copy-start.28
  92.3 9.7 %all-to-all-start.2 = ((f32[32,1,128]{2,1,0:T(1,128)}), f32[32,1,128]{2,1,0:T(1,128)S(1)}, u32[]{:S(2)}, u32[]{:S(2)}) async-start(f32[32,1,128]{2,1,0:T(1,128)} %bitcast.27), calls=%async_computation.2 | async-start | bytes 32768 | tf_op jit(solution)/shard_map/all_to_all | solution.py:713
  102.0 0.6 copy-start.29
where the time goes:
time: 107 us; the launch traced here: 106 us
  starting transfers between devices  40.4 us (38%)
  Pallas kernels  37.2 us (35%)
  waiting for transfers between devices  18.4 us (17%)
  local copies, waits for them, and re-layouts  7.99 us (7%)
  other arithmetic  1.24 us (1%)
    ppermute x7, starting transfers between devices, shards(): lax.ppermute(packed[k], 'zm', [(i, i ^ k) for i in range(g.zm)])  20.6 us
    all_to_all x2, starting transfers between devices, to_all(): lax.all_to_all(rows.reshape(count, 1, 128), AXES, 0, 0, tiled=True)  10.7 us
    pallas_call x1, Pallas kernels, shards(): call(part(middle_body, g), [struct(everyone, 128), own, own, more, more,...  10.4 us
    all_to_all x2, waiting for transfers between devices, to_all(): lax.all_to_all(rows.reshape(count, 1, 128), AXES, 0, 0, tiled=True)  9.62 us
    unnamed x61, local copies, waits for them, and re-layouts  7.67 us
    pallas_call x1, Pallas kernels, shards(): call(part(last_body, g), [own, own, struct(ITERS, 128), struct(everyone,...  7.44 us
    all_to_all x1, waiting for transfers between devices, shards(): data = lax.all_to_all(packed, 'zm', 0, 0, tiled=True)  6.26 us
    all_to_all x1, starting transfers between devices, shards(): data = lax.all_to_all(packed, 'zm', 0, 0, tiled=True)  5.19 us
  transfers between devices with their start and end apart: 13, of which 5 were waited for; matrix products, arithmetic and copies ran while one was open for 2% of the time, Pallas kernels for 18%

commit v1 on v0

--- a/solution.py
+++ b/solution.py
@@ -99,33 +99,42 @@
                 inverse[t, block // (g.blocks * g.zv)] = slot
 
 
-def pack_three_body(g, assign, refined, out, inverse, held, sems, out_sems):
+def pack_three_body(g, assign, refined, table, out, top, inverse, held, extras, rows_held, sems, out_sems):
     three = range(ITERS - 1)
+    reads = [
+        pltpu.make_async_copy(refined.at[i], held.at[i], sems.at[i]) for i in range(3 * g.slots)
+    ]
+    rows_in = pltpu.make_async_copy(table.at[0:ITERS], rows_held, sems.at[3 * g.slots])
+    rows_out = pltpu.make_async_copy(rows_held, top, out_sems.at[3 * g.zm + 3])
+    rows_in.start()
+    for read in reads:
+        read.start()
     fill_inverse(g, three, assign, inverse)
-    reads, writes = {}, []
+    rows_in.wait()
+    rows_out.start()
+    writes = []
     for t in three:
+        for slot in range(g.slots):
+            reads[t * g.slots + slot].wait()
         for peer in range(g.zm):
-            rows = slice(OFFSET[t], OFFSET[t] + ROWS)
-            source = refined.at[t * g.slots + inverse[t, peer]]
-            reads[t, peer] = pltpu.make_async_copy(source, held.at[peer, rows, :], sems.at[t * g.zm + peer])
-            reads[t, peer].start()
+            source = held.at[t * g.slots + inverse[t, peer]]
+            target = out.at[peer, OFFSET[t] : OFFSET[t] + ROWS, :]
+            writes.append(pltpu.make_async_copy(source, target, out_sems.at[t * g.zm + peer]))
+            writes[-1].start()
     for t in three:
+        first = OFFSET[t] - t * ROWS
         for peer in range(g.zm):
-            rows = slice(OFFSET[t], OFFSET[t] + ROWS)
-            reads[t, peer].wait()
-            sem = out_sems.at[t * g.zm + peer]
-            writes.append(pltpu.make_async_copy(held.at[peer, rows, :], out.at[peer, rows, :], sem))
-            writes[-1].start()
-        for peer in range(g.zm):
-            after = min(peer + 1, g.zm - 1)
+            after = t * g.slots + inverse[t, min(peer + 1, g.zm - 1)]
             for z in range(halo_rows(t)):
-                at = OFFSET[t] + ROWS + z * PAIRS
-                held[peer, at : at + PAIRS, :] = held[after, pl.ds(OFFSET[t] + z, PAIRS, stride=8), :]
-        rows = slice(OFFSET[t] + ROWS, OFFSET[t + 1])
-        writes.append(pltpu.make_async_copy(held.at[:, rows, :], out.at[:, rows, :], out_sems.at[3 * g.zm + t]))
+                at = first + z * PAIRS
+                extras[peer, at : at + PAIRS, :] = held[after, pl.ds(z, PAIRS, stride=8), :]
+        count = halo_rows(t) * PAIRS
+        target = out.at[:, OFFSET[t] + ROWS : OFFSET[t + 1], :]
+        writes.append(pltpu.make_async_copy(extras.at[:, first : first + count, :], target, out_sems.at[3 * g.zm + t]))
         writes[-1].start()
     for write in writes:
         write.wait()
+    rows_out.wait()
 
 
 def pack_last_body(g, assign, refined, *rest):
@@ -143,10 +152,6 @@
         copy.wait()
 
 
-def block_row(z):
-    return z // 8 * 8 * PAIRS + z % 8
-
-
 def pair_tiles(left, first, second):
     even = jnp.where(left, first, pltpu.roll(second, HALF, 1))
     odd = jnp.where(left, pltpu.roll(first, HALF, 1), second)
@@ -161,15 +166,17 @@
 def strip_body(g, meta, data, unused_a, unused_b, out, held, planes, sems):
     three = range(ITERS - 1)
     left, sub = lane_ids() < HALF, sub_ids()
+    two = 2 * 8
 
     def copies(t, c):
-        mine = data.at[jnp.maximum(meta[t, c], 0), OFFSET[t] : OFFSET[t] + ROWS, :]
+        at, mine = t * g.cb + c, jnp.maximum(meta[t, c], 0)
         far = data.at[jnp.maximum(meta[t, g.blocks + c], 0), OFFSET[t] + ROWS : OFFSET[t] + LAYERS[t] * PAIRS, :]
-        at = t * g.cb + c
-        return (
-            pltpu.make_async_copy(mine, held.at[at, 0:ROWS, :], sems.at[2 * at]),
-            pltpu.make_async_copy(far, held.at[at, ROWS : LAYERS[t] * PAIRS, :], sems.at[2 * at + 1]),
-        )
+        result = [pltpu.make_async_copy(far, held.at[at, 2 * two : 2 * two + halo_rows(t) * PAIRS, :], sems.at[3 * at])]
+        for zt in range(2):
+            first = OFFSET[t] + zt * 8 * PAIRS
+            source = data.at[mine, first : first + two, :]
+            result.append(pltpu.make_async_copy(source, held.at[at, zt * two : zt * two + two, :], sems.at[3 * at + 1 + zt]))
+        return result
 
     for t in three:
         for c in range(g.cb):
@@ -185,18 +192,28 @@
                 tiles = []
                 for c in (2 * col, 2 * col + 1):
                     if z < BLOCK_Z:
-                        tiles.append(held[t * g.cb + c, pl.ds(block_row(z), PAIRS, stride=8), :])
+                        tiles.append(held[t * g.cb + c, pl.ds(z // 8 * two + z % 8, PAIRS, stride=8), :])
                     else:
-                        tiles.append(held[t * g.cb + c, z * PAIRS : (z + 1) * PAIRS, :])
+                        at = 2 * two + (z - BLOCK_Z) * PAIRS
+                        tiles.append(held[t * g.cb + c, at : at + PAIRS, :])
                 even, odd = pair_tiles(left, *tiles)
                 planes[col, first + z, pl.ds(0, PAIRS, stride=2), :] = even
                 planes[col, first + z, pl.ds(1, PAIRS, stride=2), :] = odd
-        for z in range(first, first + LAYERS[t]):
-            out[z] = jnp.where(sub < 4, planes[0, z, 0:8, :], pltpu.roll(planes[1, z, 0:8, :], 4, 0))
-
-
-def strip_tile(strips, z, col):
-    return strips[z] if col == 0 else pltpu.roll(strips[z], 4, 0)
+        if t == 0:
+            for z in range(LAYERS[0]):
+                out[z] = jnp.where(sub < 4, planes[0, z, 0:8, :], pltpu.roll(planes[1, z, 0:8, :], 4, 0))
+    for z in range(LAYERS[1]):
+        one, two_at = LAYERS[0] + z, LAYERS[0] + LAYERS[1] + min(z, LAYERS[2] - 1)
+        low = jnp.where(sub < 2, planes[0, one, 0:8, :], pltpu.roll(planes[1, one, 0:8, :], 2, 0))
+        high = pltpu.roll(planes[0, two_at, 0:8, :], 4, 0)
+        high = jnp.where(sub < 6, high, pltpu.roll(planes[1, two_at, 0:8, :], 6, 0))
+        out[LAYERS[0] + z] = jnp.where(sub < 4, low, high)
+
+
+def strip_tile(strips, t, z, col):
+    tile = strips[z] if t == 0 else strips[LAYERS[0] + z]
+    shift = (4 * col, 2 * col, 4 + 2 * col)[t]
+    return pltpu.roll(tile, 8 - shift, 0) if shift else tile
 
 
 class Stencil:
@@ -340,10 +357,9 @@
     return [tile_rows(vt) for vt in (pair // g.ct * 2, pair // g.ct * 2 + 1)]
 
 
-def middle_body(g, meta, strips, interp_halo, data, interp_in,
-                out, a0_out, a1_out, a2_out, ca0_out, ca1_out, cb1_out, halos, peaks,
-                held, interp, f0, f1, f2, a0, a1, a2, b1, ca0, ca1, cb1, a0_halo, a1_halo, b1_halo, masks, sems, out_sems):
-    f, a = (f0, f1, f2), (a0, a1, a2)
+def local_body(g, meta, data, interp_in, a0_out, a1_out, a2_out, totals, peaks,
+               held, interp, f0, f1, f2, a0, a1, a2, masks, sems, out_sems):
+    f, a, outs = (f0, f1, f2), (a0, a1, a2), (a0_out, a1_out, a2_out)
     split = BLOCK_Z // 2
     groups = ([], [])
     for t in range(3):
@@ -357,21 +373,9 @@
     for group in groups:
         for copy in group:
             copy.start()
-    edge_z, edge_v = edges(meta)
-    stencil = Stencil(g, edge_v)
     left = lane_ids() < HALF
-    live0, live1 = halo_live(g, meta, 0, left), halo_live(g, meta, 1, left)
     fill_masks(g, meta, masks, (0, 1, 2), left)
-    for col in range(g.ct):
-        for z in range(LAYERS[0]):
-            value = strip_tile(strips, z, col) - interp_halo[col, z]
-            a0_halo[col, z] = jnp.where(live0[z >= BLOCK_Z][col], value, 0.0)
-        for z in range(LAYERS[1]):
-            value = strip_tile(strips, LAYERS[0] + z, col) - interp_halo[col, z]
-            a1_halo[col, z] = jnp.where(live1[z >= BLOCK_Z][col], value, 0.0)
     peaks[...] = jnp.zeros_like(peaks)
-    get0, get1, getb = reader(g, a0, a0_halo), reader(g, a1, a1_halo), reader(g, b1, b1_halo)
-    top0, top1 = LAYERS[1] - 1, LAYERS[2] - 1
     for copy in groups[0]:
         copy.wait()
 
@@ -398,33 +402,112 @@
     def step(i, carry):
         carry = list(carry)
         base = BLOCK_Z - 1 - i
-        z = base + 3
+        at = clip(base + 1, BLOCK_Z - 1)
+        inside = jnp.full(TILE, between(base + 1), F32) > 0.5
+        for pair in range(g.pairs):
+            col = pair % g.ct
+            peak = peaks[pair]
+            for rows in pair_tile_rows(g, pair):
+                mean = interp[col, at, rows, :]
+                for t in range(3):
+                    live = (masks[t, 0, pair] > 0.5) & inside
+                    value = jnp.where(live, f[t][col, at, rows, :] - mean, 0.0)
+                    a[t][col, at, rows, :] = value
+                    carry[t] = carry[t] + value * value
+                    if t == 0:
+                        peak = jnp.maximum(peak, jnp.abs(value))
+            peaks[pair] = peak
+        at = clip(base, BLOCK_Z - 1)
+        for t in range(3):
+            convert(g, meta, t, held, OFFSET[t], at, f[t], left)
+        return tuple(carry)
+
+    carry = (jnp.zeros(TILE, F32),) * 3
+    writes, bounds = [], (0, split, split + 5, BLOCK_Z + 1)
+    for index in range(3):
+        if index == 1:
+            for copy in groups[1]:
+                copy.wait()
+        carry = lax.fori_loop(bounds[index], bounds[index + 1], step, carry)
+        lowest = BLOCK_Z - bounds[index + 1] + 1
+        for t in range(3):
+            highest = BLOCK_Z - bounds[index] if index else LAYERS[t] - 1
+            for col in range(g.ct):
+                span = slice(lowest, highest + 1)
+                sem = out_sems.at[(index * 3 + t) * g.ct + col]
+                writes.append(pltpu.make_async_copy(a[t].at[col, span], outs[t].at[col, span], sem))
+                writes[-1].start()
+    for t in range(3):
+        totals[t] = carry[t]
+    for write in writes:
+        write.wait()
+
+
+def middle_body(g, meta, strips, interp_halo, totals, a0_in, a1_in, a2_in,
+                out, ca0_out, ca1_out, cb1_out, halos,
+                a0, a1, a2, b1, ca0, ca1, cb1, a0_halo, a1_halo, b1_halo, masks, sems, out_sems):
+    split = BLOCK_Z // 2
+    groups, at = ([], []), 0
+    for source, target, layers in ((a0_in, a0, LAYERS[0]), (a1_in, a1, LAYERS[1]), (a2_in, a2, BLOCK_Z)):
+        for col in range(g.ct):
+            for group, span in ((0, slice(split, layers)), (1, slice(0, split))):
+                groups[group].append(pltpu.make_async_copy(source.at[col, span], target.at[col, span], sems.at[at]))
+                at += 1
+    for group in groups:
+        for copy in group:
+            copy.start()
+    edge_z, edge_v = edges(meta)
+    stencil = Stencil(g, edge_v)
+    left = lane_ids() < HALF
+    live0, live1 = halo_live(g, meta, 0, left), halo_live(g, meta, 1, left)
+    fill_masks(g, meta, masks, (1, 2), left)
+    for pair in range(g.pairs):
+        masks[1, 1, pair] = jnp.zeros(TILE, F32)
+    for col in range(g.ct):
+        for z in range(LAYERS[0]):
+            value = strip_tile(strips, 0, z, col) - interp_halo[col, z]
+            a0_halo[col, z] = jnp.where(live0[z >= BLOCK_Z][col], value, 0.0)
+        for z in range(LAYERS[1]):
+            value = strip_tile(strips, 1, z, col) - interp_halo[col, z]
+            a1_halo[col, z] = jnp.where(live1[z >= BLOCK_Z][col], value, 0.0)
+    get0, get1, getb = reader(g, a0, a0_halo), reader(g, a1, a1_halo), reader(g, b1, b1_halo)
+    top0, top1 = LAYERS[1] - 1, LAYERS[2] - 1
+    none = LAYERS[0]
+    for col in range(g.ct):
+        for field in (a1, a2, b1, ca0):
+            field[col, none] = jnp.zeros((g.span, LANES), F32)
+    for copy in groups[0]:
+        copy.wait()
+
+    def step(i, carry):
+        carry = list(carry)
+        base = top0 - i
+        z = base + 1
         at = clip(z, top1)
         low = layer_below(at, edge_z)
         after_a = stencil(get1, at, low)
         after_b = stencil(getb, at, low)
         put(g, ca1, halos.at[1], at, after_a)
         put(g, cb1, halos.at[2], at, after_b)
-        row = jnp.minimum(at, BLOCK_Z - 1)
-        counts = between(z)
-        inside = jnp.full(TILE, counts, F32) > 0.5
+        own = (z >= 0) & (z < BLOCK_Z)
+        row, kind = jnp.where(own, z, none), jnp.where(own, 0, 1)
         for pair in range(g.pairs):
             col = pair % g.ct
-            live = masks[2, 0, pair] * counts > 0.5
+            live = masks[1, kind, pair] > 0.5
             for half, rows in enumerate(pair_tile_rows(g, pair)):
                 vt = pair // g.ct * 2 + half
-                one, two = a1[col, row, rows, :], jnp.where(inside, b1[col, row, rows, :], 0.0)
-                carry[3] = carry[3] + one * two
-                carry[4] = carry[4] + two * two
+                one, two = a1[col, row, rows, :], b1[col, row, rows, :]
+                carry[0] = carry[0] + one * two
+                carry[1] = carry[1] + two * two
                 parts = [a2[col, row, rows, :]] + [
                     jnp.where(live, value, 0.0) for value in (ca0[col, row, rows, :], after_a[col, vt], after_b[col, vt])
                 ]
-                slot = 5
+                slot = 2
                 for m in range(4):
                     for n in range(max(m, 1), 4):
                         carry[slot] = carry[slot] + parts[m] * parts[n]
                         slot += 1
-        at = clip(base + 2, top0)
+        at = clip(base, top0)
         after = stencil(get0, at, layer_below(at, edge_z))
         put(g, ca0, halos.at[0], at, after)
         far = jnp.where(at >= BLOCK_Z, 1, 0)
@@ -433,47 +516,27 @@
                 live = (live1[0][col] & (at < BLOCK_Z)) | (live1[1][col] & (at >= BLOCK_Z))
                 b1_halo[col, at] = jnp.where(live, value, 0.0)
             else:
-                mask = masks[1, far, vt // 2 * g.ct + col]
+                mask = masks[0, far, vt // 2 * g.ct + col]
                 b1[col, at, tile_rows(vt), :] = jnp.where(mask > 0.5, value, 0.0)
-        at = clip(base + 1, BLOCK_Z - 1)
-        counts = between(base + 1)
-        for pair in range(g.pairs):
-            col = pair % g.ct
-            peak = peaks[pair]
-            for rows in pair_tile_rows(g, pair):
-                mean = interp[col, at, rows, :]
-                for t in range(3):
-                    value = jnp.where(masks[t, 0, pair] > 0.5, f[t][col, at, rows, :] - mean, 0.0)
-                    a[t][col, at, rows, :] = value
-                    counted = jnp.where(masks[t, 0, pair] * counts > 0.5, value, 0.0)
-                    carry[t] = carry[t] + counted * counted
-                    if t == 0:
-                        peak = jnp.maximum(peak, jnp.abs(counted))
-            peaks[pair] = peak
-        at = clip(base, BLOCK_Z - 1)
-        for t in range(3):
-            convert(g, meta, t, held, OFFSET[t], at, f[t], left)
         return tuple(carry)
 
-    carry = (jnp.zeros(TILE, F32),) * (3 + 11)
+    carry = (jnp.zeros(TILE, F32),) * 11
     writes = []
-    outs = ((a0, a0_out, BLOCK_Z), (a1, a1_out, BLOCK_Z), (a2, a2_out, BLOCK_Z + 1),
-            (ca0, ca0_out, BLOCK_Z + 1), (ca1, ca1_out, BLOCK_Z + 1), (cb1, cb1_out, BLOCK_Z + 1))
-    bounds = (0, split, split + 5, BLOCK_Z + 3)
+    bounds = (0, top0 - split + 1, top0 - split + 6, top0 + 2)
     for index in range(3):
         if index == 1:
             for copy in groups[1]:
                 copy.wait()
         carry = lax.fori_loop(bounds[index], bounds[index + 1], step, carry)
-        lowest = BLOCK_Z - bounds[index + 1] + 3
-        highest = BLOCK_Z - bounds[index] + 2 if index else top1
-        for which, (source, target, layers) in enumerate(outs):
+        lowest = top0 - bounds[index + 1] + 2
+        highest = top0 - bounds[index] + 1 if index else top1
+        for which, (source, target) in enumerate(((ca0, ca0_out), (ca1, ca1_out), (cb1, cb1_out))):
             for col in range(g.ct):
-                span = slice(lowest, min(highest + 1, layers))
-                sem = out_sems.at[(index * 6 + which) * g.ct + col]
+                span = slice(lowest, highest + 1)
+                sem = out_sems.at[(index * 3 + which) * g.ct + col]
                 writes.append(pltpu.make_async_copy(source.at[col, span], target.at[col, span], sem))
                 writes[-1].start()
-    values = [carry[0], carry[1], carry[3], carry[4], carry[2]] + list(carry[5:])
+    values = [totals[0], totals[1], carry[0], carry[1], totals[2]] + list(carry[2:])
     out[...] = spread_rows(values, out.shape[0])
     for write in writes:
         write.wait()
@@ -505,11 +568,11 @@
     return [jnp.broadcast_to(w, TILE) for w in (w0, w1, weight_of(total, live_cells(g, meta, 2)))]
 
 
-def last_body(g, meta, parts, strips, interp_halo, halos_in, peaks0, a1_in, a2_in, interp_in, ca0_in, ca1_in, cb1_in,
+def last_body(g, meta, parts, strips, interp_halo, halos_in, peaks0, a0_in, a1_in, a2_in, interp_in, ca0_in, ca1_in, cb1_in,
               *rest):
     data, rest = rest[: g.zm], rest[g.zm :]
-    (r2_out, r3_out, errors, out, weights,
-     held, f3, a1, a2, interp, ca0, ca1, cb1, r2, r2_halo, change, r3, masks, peaks, sems, out_sems) = rest
+    (sum_hbm, r3_hbm, errors, out,
+     held, f3, a0, a1, a2, interp, ca0, ca1, cb1, r2, r2_halo, change, sum_out, r3, masks, peaks, sems, out_sems) = rest
     top = LAYERS[2] - 1
     chunks = segments(top, (5, 4, 4, 4))
     reads, at = [], 0
@@ -520,7 +583,8 @@
                 group.append(pltpu.make_async_copy(data[k], held.at[k], sems.at[at]))
                 at += 1
         for source, target, layers in ((ca0_in, ca0, BLOCK_Z + 1), (ca1_in, ca1, BLOCK_Z + 1), (cb1_in, cb1, BLOCK_Z + 1),
-                                       (a1_in, a1, BLOCK_Z), (a2_in, a2, BLOCK_Z + 1), (interp_in, interp, BLOCK_Z)):
+                                       (a0_in, a0, BLOCK_Z), (a1_in, a1, BLOCK_Z), (a2_in, a2, BLOCK_Z + 1),
+                                       (interp_in, interp, BLOCK_Z)):
             for col in range(g.ct):
                 span = slice(lowest, min(highest + 1, layers))
                 group.append(pltpu.make_async_copy(source.at[col, span], target.at[col, span], sems.at[at]))
@@ -535,14 +599,12 @@
     fill_masks(g, meta, masks, (1, 2, 3), left)
     w0, w1, w2 = three_weights(g, meta, parts)
     w01 = w0 * w1
-    weights[0], weights[1], weights[2] = w0, w1, w2
     live = halo_live(g, meta, 2, left)
     peaks[...] = jnp.zeros_like(peaks)
-    first = sum(LAYERS[:2])
     for col in range(g.ct):
         for z in range(LAYERS[2]):
             value = interp_halo[col, z] + w0 * halos_in[0, col, z] + w1 * halos_in[1, col, z] - w01 * halos_in[2, col, z]
-            r2_halo[col, z] = jnp.where(live[z >= BLOCK_Z][col], strip_tile(strips, first + z, col) - value, 0.0)
+            r2_halo[col, z] = jnp.where(live[z >= BLOCK_Z][col], strip_tile(strips, 2, z, col) - value, 0.0)
     get = reader(g, r2, r2_halo)
 
     def step(i, total):
@@ -577,8 +639,9 @@
                 value = a2[col, at, rows, :] - jnp.where(mask2, whole, 0.0)
                 r2[col, at, rows, :] = value
                 peak2 = jnp.maximum(peak2, jnp.where(inside, jnp.abs(value), 0.0))
-                value = a1[col, own, rows, :] - jnp.where(mask1, zero, 0.0)
-                peak1 = jnp.maximum(peak1, jnp.where(inside, jnp.abs(value), 0.0))
+                one = a1[col, own, rows, :] - jnp.where(mask1, zero, 0.0)
+                peak1 = jnp.maximum(peak1, jnp.where(inside, jnp.abs(one), 0.0))
+                sum_out[col, own, rows, :] = w0 * a0[col, own, rows, :] + w1 * one + w2 * value
             peaks[0, pair] = peak1
             peaks[1, pair] = peak2
         convert(g, meta, ITERS - 1, held, 0, own, f3, left)
@@ -594,7 +657,7 @@
         below = lowest + 1 if lowest else 0
         above = min((chunks[index - 1][0] if index else BLOCK_Z - 1), BLOCK_Z - 1)
         for which, (source, target, layers) in enumerate(
-            ((r2, r2_out, slice(lowest, min(highest, BLOCK_Z - 1) + 1)), (r3, r3_out, slice(below, above + 1)))
+            ((sum_out, sum_hbm, slice(lowest, min(highest, BLOCK_Z - 1) + 1)), (r3, r3_hbm, slice(below, above + 1)))
         ):
             for col in range(g.ct):
                 sem = out_sems.at[(index * 2 + which) * g.ct + col]
@@ -621,68 +684,38 @@
         write.wait()
 
 
-def assemble_body(g, meta, weights, table_in, a0_in, a1_in, ca0_in, r2_in, grown_out,
-                  table, a0, a1, ca0, r2, grown, masks, sems):
-    copies = [pltpu.make_async_copy(table_in, table, sems.at[0])]
-    for i, (source, target) in enumerate(((a0_in, a0), (a1_in, a1), (ca0_in, ca0), (r2_in, r2))):
+def finish_body(g, meta, parts, table_in, change_in, r3_in, out_hbm, worst, table, change, r3, out, sems, out_sems):
+    quarter = BLOCK_Z // 4
+    spans = [slice(part * quarter, (part + 1) * quarter) for part in range(4)]
+    reads = []
+    for part, span in enumerate(spans):
+        at = part * (1 + 2 * g.ct)
+        group = [pltpu.make_async_copy(table_in.at[span], table.at[span], sems.at[at])]
         for col in range(g.ct):
-            copies.append(pltpu.make_async_copy(source.at[col, 0:BLOCK_Z], target.at[col], sems.at[1 + i * g.ct + col]))
-    for copy in copies:
-        copy.start()
-    fill_masks(g, meta, masks, (1,), lane_ids() < HALF)
-    w0, w1, w2 = weights[0], weights[1], weights[2]
-    w01 = w0 * w1
-    for copy in copies:
-        copy.wait()
-
-    @pl.loop(0, BLOCK_Z)
-    def _(z):
-        for pair in range(g.pairs):
-            col = pair % g.ct
-            lanes = slice(col * LANES, (col + 1) * LANES)
-            mask = masks[0, 0, pair] > 0.5
-            for vt in (pair // g.ct * 2, pair // g.ct * 2 + 1):
-                rows = tile_rows(vt)
-                value = w0 * a0[col, z, rows, :] + w1 * a1[col, z, rows, :] + w2 * r2[col, z, rows, :]
-                value = value - jnp.where(mask, w01 * ca0[col, z, rows, :], 0.0)
-                grown[z, rows, lanes] = table[z, rows, lanes] + value
-
-    write = pltpu.make_async_copy(grown, grown_out, sems.at[0])
-    write.start()
-    write.wait()
-
-
-def finish_body(g, meta, parts, grown_in, r3_in, out_hbm, worst, grown, r3, out, sems, out_sems):
-    quarter = BLOCK_Z // 4
-    reads, at = [], 0
-    for part in range(4):
-        layers = slice(part * quarter, (part + 1) * quarter)
-        group = [pltpu.make_async_copy(grown_in.at[layers], grown.at[layers], sems.at[at])]
-        for col in range(g.ct):
-            group.append(pltpu.make_async_copy(r3_in.at[col, layers], r3.at[col, layers], sems.at[at + 1 + col]))
-        at += 1 + g.ct
+            at += 2
+            group.append(pltpu.make_async_copy(change_in.at[col, span], change.at[col, span], sems.at[at - 1]))
+            group.append(pltpu.make_async_copy(r3_in.at[col, span], r3.at[col, span], sems.at[at]))
         reads.append(group)
     for group in reads:
-        for copy in group:
-            copy.start()
+        for read in group:
+            read.start()
     total = lane_values(jnp.sum(parts[...], axis=0, keepdims=True), 1)[0]
     w3 = jnp.broadcast_to(weight_of(total, live_cells(g, meta, 3)), TILE)
-    line = jnp.max(parts[...], axis=0, keepdims=True)
-    for i, value in enumerate(lane_values(line, 1 + ITERS)[1:]):
-        worst[i] = jnp.max(value)
     writes = []
-    for part in range(4):
-        for copy in reads[part]:
-            copy.wait()
-        layers = slice(part * quarter, (part + 1) * quarter)
+    for part, span in enumerate(spans):
+        for read in reads[part]:
+            read.wait()
         for z in range(part * quarter, (part + 1) * quarter):
             for col in range(g.ct):
                 lanes = slice(col * LANES, (col + 1) * LANES)
                 for vt in range(g.vt):
                     rows = tile_rows(vt)
-                    out[z, rows, lanes] = grown[z, rows, lanes] + w3 * r3[col, z, rows, :]
-        writes.append(pltpu.make_async_copy(out.at[layers], out_hbm.at[layers], out_sems.at[part]))
+                    out[z, rows, lanes] = table[z, rows, lanes] + (change[col, z, rows, :] + w3 * r3[col, z, rows, :])
+        writes.append(pltpu.make_async_copy(out.at[span], out_hbm.at[span], out_sems.at[part]))
         writes[-1].start()
+    line = jnp.max(parts[...], axis=0, keepdims=True)
+    for i, value in enumerate(lane_values(line, 1 + ITERS)[1:]):
+        worst[i] = jnp.max(value)
     for write in writes:
         write.wait()
 
@@ -728,17 +761,19 @@
     vmem = lambda *shape: pltpu.VMEM(shape, F32)
     main, halo = g.main, g.halo
 
-    below = from_next(table[:ITERS], "zm")
-    packed = call(
-        part(pack_three_body, g), struct(g.zm, OFFSET[3], LANES), [SMEM, HBM], HBM,
-        [pltpu.SMEM((ITERS, g.zm), jnp.int32), vmem(g.zm, OFFSET[3], LANES), dma(3 * g.zm), dma(3 * g.zm + 3)],
+    packed, top = call(
+        part(pack_three_body, g), [struct(g.zm, OFFSET[3], LANES), struct(ITERS, *table.shape[1:])], [SMEM, HBM, HBM], [HBM] * 2,
+        [pltpu.SMEM((ITERS, g.zm), jnp.int32), vmem(3 * g.slots, ROWS, LANES), vmem(g.zm, OFFSET[3] - 3 * ROWS, LANES),
+         vmem(ITERS, *table.shape[1:]), dma(3 * g.slots + 1), dma(3 * g.zm + 4)],
         WHOLE,
-    )(slots, views)
+    )(slots, views, table)
+    below = from_next(top, "zm")
     data = lax.all_to_all(packed, "zm", 0, 0, tiled=True)
-    strip = from_next(jnp.concatenate([table[:, :8], below[:, :8]], 0), "zv")
+    strip = jnp.concatenate([table[:, :8], below[:, :8]], 0)
+    strip = from_next(strip, "zv")
     packed = call(
         part(pack_last_body, g), [struct(ROWS, LANES)] * g.zm, [SMEM, HBM], [VMEM] * g.zm,
-        [pltpu.SMEM((ITERS, g.zm), jnp.int32), dma(g.zm)], PART,
+        [pltpu.SMEM((ITERS, g.zm), jnp.int32), dma(g.zm)], WHOLE,
     )(slots, views)
     last_data = [packed[0]]
     for k in range(1, g.zm):
@@ -750,39 +785,41 @@
     )(meta, table, below, strip)
 
     strips = call(
-        part(strip_body, g), struct(sum(LAYERS[:3]), *TILE), [SMEM] + [HBM] * 3, VMEM,
-        [vmem(3 * g.cb, LAYERS[0] * PAIRS, LANES), vmem(g.ct, sum(LAYERS[:3]), BLOCK_V, LANES), dma(6 * g.cb)],
+        part(strip_body, g), struct(sum(LAYERS[:2]), *TILE), [SMEM] + [HBM] * 3, VMEM,
+        [vmem(3 * g.cb, ROWS, LANES), vmem(g.ct, sum(LAYERS[:3]), BLOCK_V, LANES), dma(9 * g.cb)],
         PART,
     )(meta, data, interp_halo, packed[0])
     strips = from_next(strips, "zv")
-    own, more = struct(*main(BLOCK_Z)), struct(*main(LAYERS[2]))
-    products, a0, a1, a2, ca0, ca1, cb1, halos, peaks0 = call(
-        part(middle_body, g),
-        [struct(everyone, 128), own, own, more, more, more, more, struct(3, *halo(LAYERS[1])), struct(g.pairs, *TILE)],
-        [SMEM] + [VMEM] * 2 + [HBM] * 2, [VMEM] + [HBM] * 6 + [VMEM] * 2,
-        [vmem(*data.shape), vmem(*main(LAYERS[0]))] + [vmem(*main(LAYERS[0] + 1))] * 10
-        + [vmem(*halo(LAYERS[0] + 1))] * 3 + [vmem(3, 2, g.pairs, *TILE), dma(6 + 2 * g.ct), dma(18 * g.ct)],
+    own, more, most = struct(*main(BLOCK_Z)), struct(*main(LAYERS[2])), struct(*main(LAYERS[1]))
+    a0, a1, a2, totals, peaks0 = call(
+        part(local_body, g), [struct(*main(LAYERS[0])), most, more, struct(3, *TILE), struct(g.pairs, *TILE)],
+        [SMEM] + [HBM] * 2, [HBM] * 3 + [VMEM] * 2,
+        [vmem(*data.shape)] + [vmem(*main(LAYERS[0]))] * 7
+        + [vmem(3, 2, g.pairs, *TILE), dma(6 + 2 * g.ct), dma(9 * g.ct)], WHOLE,
+    )(meta, data, interp)
+    products, ca0, ca1, cb1, halos = call(
+        part(middle_body, g), [struct(everyone, 128), more, more, more, struct(3, *halo(LAYERS[1]))],
+        [SMEM] + [VMEM] * 3 + [HBM] * 3, [VMEM] + [HBM] * 3 + [VMEM],
+        [vmem(*main(LAYERS[0] + 1))] * 7 + [vmem(*halo(LAYERS[0] + 1))] * 3
+        + [vmem(2, 2, g.pairs, *TILE), dma(6 * g.ct), dma(9 * g.ct)],
         WHOLE,
-    )(meta, strips, interp_halo, data, interp)
+    )(meta, strips, interp_halo, totals, a0, a1, a2)
     products = to_all(products)
-    r2, r3, errors, stats, weights = call(
-        part(last_body, g), [own, own, struct(ITERS, 128), struct(everyone, 128), struct(3, *TILE)],
-        [SMEM] + [VMEM] * 5 + [HBM] * (6 + g.zm), [HBM] * 2 + [VMEM] * 3,
-        [vmem(g.zm, ROWS, LANES), vmem(*main(BLOCK_Z)), vmem(*main(BLOCK_Z)), vmem(*main(LAYERS[2])), vmem(*main(BLOCK_Z))]
-        + [vmem(*main(LAYERS[2]))] * 4 + [vmem(*halo(LAYERS[2])), vmem(*main(LAYERS[2])), vmem(*main(BLOCK_Z)),
-           vmem(3, 2, g.pairs, *TILE), vmem(3, g.pairs, *TILE), dma(g.zm + 24 * g.ct), dma(8 * g.ct)],
+    change, r3, errors, stats = call(
+        part(last_body, g), [own, own, struct(ITERS, 128), struct(everyone, 128)],
+        [SMEM] + [VMEM] * 5 + [HBM] * (7 + g.zm), [HBM] * 2 + [VMEM] * 2,
+        [vmem(g.zm, ROWS, LANES)] + [vmem(*main(BLOCK_Z))] * 3 + [vmem(*main(LAYERS[2])), vmem(*main(BLOCK_Z))]
+        + [vmem(*main(LAYERS[2]))] * 4 + [vmem(*halo(LAYERS[2])), vmem(*main(LAYERS[2]))]
+        + [vmem(*main(BLOCK_Z))] * 2
+        + [vmem(3, 2, g.pairs, *TILE), vmem(3, g.pairs, *TILE), dma(g.zm + 28 * g.ct), dma(8 * g.ct)],
         WHOLE,
-    )(meta, products, strips, interp_halo, halos, peaks0, a1, a2, interp, ca0, ca1, cb1, *last_data)
+    )(meta, products, strips, interp_halo, halos, peaks0, a0, a1, a2, interp, ca0, ca1, cb1, *last_data)
     stats = to_all(stats)
-    grown = call(
-        part(assemble_body, g), struct(*table.shape), [SMEM, VMEM] + [HBM] * 5, HBM,
-        [vmem(*table.shape)] + [vmem(*main(BLOCK_Z))] * 4 + [vmem(*table.shape), vmem(1, 2, g.pairs, *TILE), dma(1 + 4 * g.ct)],
+    table_out, worst = call(
+        part(finish_body, g), [struct(*table.shape), struct(ITERS)], [SMEM, VMEM] + [HBM] * 3, [HBM, SMEM],
+        [vmem(*table.shape)] + [vmem(*main(BLOCK_Z))] * 2 + [vmem(*table.shape), dma(4 * (1 + 2 * g.ct)), dma(4)],
         WHOLE,
-    )(meta, weights, table, a0, a1, ca0, r2)
-    table_out, worst = call(
-        part(finish_body, g), [struct(*table.shape), struct(ITERS)], [SMEM, VMEM] + [HBM] * 2, [HBM, SMEM],
-        [vmem(*table.shape), vmem(*main(BLOCK_Z)), vmem(*table.shape), dma(4 * (1 + g.ct)), dma(4)], WHOLE,
-    )(meta, stats, grown, r3)
+    )(meta, stats, table, change, r3)
     return (table_out, errors[:, : g.blocks], worst)
 
 

time: 107 us -> 108 us (level)
  blocking collectives: 0 us -> 10.2 us
  local copies, waits for them, and re-layouts: 7.99 us -> 2.1 us
  starting transfers between devices: 40.4 us -> 34.7 us
  waiting for transfers between devices: 18.4 us -> 20.5 us
    all_to_all x0 -> x1, blocking collectives: none -> 10.2 us  [to_all(): lax.all_to_all(rows.reshape(count, 1, 128), AXES, 0, 0, tiled=True)]
    unnamed x61 -> x49, local copies, waits for them, and re-layouts: 7.67 us -> 1.79 us
    all_to_all x2 -> x1, starting transfers between devices: 10.7 us -> 6.56 us  [to_all(): lax.all_to_all(rows.reshape(count, 1, 128), AXES, 0, 0, tiled=True)]
    all_to_all x2 -> x1, waiting for transfers between devices: 9.62 us -> 7.1 us  [to_all(): lax.all_to_all(rows.reshape(count, 1, 128), AXES, 0, 0, tiled=True)]
    ppermute x3, waiting for transfers between devices: 1.82 us -> 4.25 us  [from_next(): return lax.ppermute(value, axis, [(i, i - 1) for i in range(1, count)])]
    ppermute x7, starting transfers between devices: 20.6 us -> 18.9 us  [shards(): lax.ppermute(packed[k], 'zm', [(i, i ^ k) for i in range(g.zm)])]
    all_to_all x1, waiting for transfers between devices: 6.26 us -> 7.9 us  [shards(): data = lax.all_to_all(packed, 'zm', 0, 0, tiled=True)]
    pallas_call x4, Pallas kernels: 21.8 us -> 20.3 us  [the longest x1 7.49 us: shards(): call(part(middle_body, g), [struct(everyone, 128), more, more, more, stru...]
  transfers between devices with their start and end apart: 13 -> 12, of which waited for: 5 -> 5; matrix products, arithmetic and copies ran while one was open for 2% -> 2% of each run, Pallas kernels for 18% -> 19%
where the time goes in v1:
time: 108 us; the launch traced here: 107 us
  Pallas kernels  37.5 us (35%)
  starting transfers between devices  34.7 us (32%)
  waiting for transfers between devices  20.5 us (19%)
  blocking collectives  10.2 us (9%)
  local copies, waits for them, and re-layouts  2.1 us (2%)
  other arithmetic  1.25 us (1%)
    ppermute x7, starting transfers between devices, shards(): lax.ppermute(packed[k], 'zm', [(i, i ^ k) for i in range(g.zm)])  18.9 us
    all_to_all x1, blocking collectives, to_all(): lax.all_to_all(rows.reshape(count, 1, 128), AXES, 0, 0, tiled=True)  10.2 us
    all_to_all x1, waiting for transfers between devices, shards(): data = lax.all_to_all(packed, 'zm', 0, 0, tiled=True)  7.9 us
    pallas_call x1, Pallas kernels, shards(): call(part(last_body, g), [own, own, struct(ITERS, 128), struct(everyone,...  7.69 us
    pallas_call x1, Pallas kernels, shards(): call(part(middle_body, g), [struct(everyone, 128), more, more, more, stru...  7.49 us
    pallas_call x1, Pallas kernels, shards(): call(part(local_body, g), [struct(*main(LAYERS[0])), most, more, struct(3...  7.2 us
    all_to_all x1, waiting for transfers between devices, to_all(): lax.all_to_all(rows.reshape(count, 1, 128), AXES, 0, 0, tiled=True)  7.1 us
    all_to_all x1, starting transfers between devices, to_all(): lax.all_to_all(rows.reshape(count, 1, 128), AXES, 0, 0, tiled=True)  6.56 us
  transfers between devices with their start and end apart: 12, of which 5 were waited for; matrix products, arithmetic and copies ran while one was open for 2% of the time, Pallas kernels for 19%

profile of v1, /device:TPU:0, one launch (start us, length us, event | category | flops | bytes accessed | tf_op | source)
XLA Modules:
  0.0 107.3 jit_solution(18061473879162301191)
XLA Ops:
  0.6 3.7 %shard_map.58 = (f32[8,432,128]{2,1,0:T(8,128)}, f32[4,64,256]{2,1,0:T(8,128)}) custom-call(s32[32,32]{1,0:T(8,128)} %bitcast.22, f32[32,128,128]{2,1,0:T(8,128)} %bitcast.20, f32[16,64,256]{2,1,0:T(8,128)} %table_in.1), custom_call_target="tpu_custom_call" | custom-call | flops 2000000 | bytes 1048576 | tf_op jit(solution)/shard_map/pallas_call | solution.py:764
  4.3 0.0 copy-start.16
  4.3 0.0 copy-start.7
  4.3 0.0 slice-start
  4.4 5.3 %all-to-all-start = ((f32[8,432,128]{2,1,0:T(8,128)}), f32[8,432,128]{2,1,0:T(8,128)S(1)}, u32[]{:S(2)}, u32[]{:S(2)}) async-start(f32[8,432,128]{2,1,0:T(8,128)} %get-tuple-element.31), calls=%async_computation | async-start | bytes 3538944 | tf_op jit(solution)/shard_map/all_to_all | solution.py:771
  9.7 1.3 %collective-permute-start = (f32[4,64,256]{2,1,0:T(8,128)S(1)}, f32[4,64,256]{2,1,0:T(8,128)S(1)}, u32[]{:S(2)}, u32[]{:S(2)}) collective-permute-start(f32[4,64,256]{2,1,0:T(8,128)S(1)} %copy-done.16), channel_id=1, source_target_pairs={{4,0},{8,4},{12,8},{16,12},{20,16},{24,20},{28,24},{5,1},{9,5},{13... | collective-permute-start | bytes 786440 | tf_op jit(solution)/shard_map/ppermute | solution.py:751
  11.0 0.0 copy-done.7
  11.1 0.2 convert_reduce_fusion
  11.2 0.1 broadcast_select_fusion
  11.3 1.8 %collective-permute-done.below = f32[4,64,256]{2,1,0:T(8,128)S(1)} collective-permute-done((f32[4,64,256]{2,1,0:T(8,128)S(1)}, f32[4,64,256]{2,1,0:T(8,128)S(1)}, u32[]{:S(2)}, u32[]{:S(2)}) %collective-permute-start) | collective-permute-done | bytes 262176 | tf_op jit(solution)/shard_map/ppermute | solution.py:751
  13.1 0.7 pad_maximum_fusion
  13.8 1.3 %collective-permute-start.1 = (f32[20,8,256]{2,1,0:T(8,128)}, f32[20,8,256]{2,1,0:T(8,128)S(1)}, u32[]{:S(2)}, u32[]{:S(2)}) collective-permute-start(f32[20,8,256]{2,1,0:T(8,128)} %pad_maximum_fusion), channel_id=1, source_target_pairs={{1,0},{2,1},{3,2},{5,4},{6,5},{7,6},{9,8},{10,9},{11,10},{13,12},{... | collective-permute-start | bytes 491528 | tf_op jit(solution)/shard_map/ppermute | solution.py:751
  15.1 0.1 add_convert_fusion
  15.2 0.1 copy.13
  15.3 0.1 copy.14
  15.4 0.1 eq.32
  15.5 0.2 select_reduce_fusion
  15.7 0.1 concatenate.10.meta
  15.8 3.0 %shard_map.60 = (f32[128,128]{1,0:T(8,128)}, f32[128,128]{1,0:T(8,128)}, f32[128,128]{1,0:T(8,128)}, f32[128,128]{1,0:T(8,128)}, f32[128,128]{1,0:T(8,128)}, /*i...) custom-call(s32[32,32]{1,0:T(8,128)} %bitcast.23, f32[32,128,128]{2,1,0:T(8,128)} %bitcast.21), custom_call_target="tpu_custom_call" | custom-call | flops 2000000 | bytes 1048576 | tf_op jit(solution)/shard_map/pallas_call | solution.py:774
  18.8 2.4 %collective-permute-done.1.strip = f32[20,8,256]{2,1,0:T(8,128)S(1)} collective-permute-done((f32[20,8,256]{2,1,0:T(8,128)}, f32[20,8,256]{2,1,0:T(8,128)S(1)}, u32[]{:S(2)}, u32[]{:S(2)}) %collective-permute-start.1) | collective-permute-done | bytes 163872 | tf_op jit(solution)/shard_map/ppermute | solution.py:751
  21.2 2.5 %shard_map.59 = (f32[2,19,64,128]{3,2,1,0:T(8,128)S(1)}, f32[2,19,8,128]{3,2,1,0:T(8,128)S(1)}) custom-call(s32[4,128]{1,0:T(4,128)S(1)} %concatenate.10.meta, f32[16,64,256]{2,1,0:T(8,128)S(1)} %copy-done.1, f32[4,64,256]{2,1,0:T(8,128)S(1)} %collective-permute-done.below, f32[20,8,256]{2,1,0:T(8,128)S(1)} %collective-permute-done.1.strip), custom_call_target="tpu_custom_call" | custom-call | flops 2000000 | bytes 1048576 | tf_op jit(solution)/shard_map/pallas_call | solution.py:782
  23.8 1.1 copy-done.2
  24.9 7.9 %all-to-all-done.data = f32[8,432,128]{2,1,0:T(8,128)S(1)} async-done(((f32[8,432,128]{2,1,0:T(8,128)}), f32[8,432,128]{2,1,0:T(8,128)S(1)}, u32[]{:S(2)}, u32[]{:S(2)}) %all-to-all-start) | async-done | bytes 1769504 | tf_op jit(solution)/shard_map/all_to_all | solution.py:771
  32.8 1.9 %shard_map.61 = f32[37,8,128]{2,1,0:T(8,128)S(1)} custom-call(s32[4,128]{1,0:T(4,128)S(1)} %concatenate.10.meta, f32[8,432,128]{2,1,0:T(8,128)S(1)} %all-to-all-done.data, f32[2,19,8,128]{3,2,1,0:T(8,128)S(1)} %get-tuple-element.33.unused_a.interp_halo, f32[128,128]{1,0:T(8,128)S(1)} %copy-done.4), custom_call_target="tpu_custom_call" | custom-call | flops 2000000 | bytes 1048576 | tf_op jit(solution)/shard_map/pallas_call | solution.py:787
  34.7 1.3 %collective-permute-start.2 = (f32[37,8,128]{2,1,0:T(8,128)S(1)}, f32[37,8,128]{2,1,0:T(8,128)S(1)}, u32[]{:S(2)}, u32[]{:S(2)}) collective-permute-start(f32[37,8,128]{2,1,0:T(8,128)S(1)} %shard_map.61), channel_id=1, source_target_pairs={{1,0},{2,1},{3,2},{5,4},{6,5},{7,6},{9,8},{10,9},{11,10},{13,12},{... | collective-permute-start | bytes 454664 | tf_op jit(solution)/shard_map/ppermute | solution.py:751
  36.1 14.2 %collective-permute-start.3 = (f32[128,128]{1,0:T(8,128)S(1)}, f32[128,128]{1,0:T(8,128)S(1)}, u32[]{:S(2)}, u32[]{:S(2)}) collective-permute-start(f32[128,128]{1,0:T(8,128)S(1)} %copy-done.23), channel_id=1, source_target_pairs={{0,4},{4,0},{8,12},{12,8},{16,20},{20,16},{24,28},{28,24},{1,5},{5... | collective-permute-start | bytes 196616 | tf_op jit(solution)/shard_map/ppermute | solution.py:780
  50.2 0.7 collective-permute-start.4
  50.9 0.7 collective-permute-start.5
  51.7 0.7 collective-permute-start.6
  52.4 0.0 collective-permute-done.3.rest_1_
  52.4 1.4 %collective-permute-start.7 = (f32[128,128]{1,0:T(8,128)S(1)}, f32[128,128]{1,0:T(8,128)S(1)}, u32[]{:S(2)}, u32[]{:S(2)}) collective-permute-start(f32[128,128]{1,0:T(8,128)S(1)} %copy-done.19), channel_id=1, source_target_pairs={{0,20},{4,16},{8,28},{12,24},{16,4},{20,0},{24,12},{28,8},{1,21},{... | collective-permute-start | bytes 196616 | tf_op jit(solution)/shard_map/ppermute | solution.py:780
  53.8 1.3 %collective-permute-done.4.rest_2_ = f32[128,128]{1,0:T(8,128)S(1)} collective-permute-done((f32[128,128]{1,0:T(8,128)S(1)}, f32[128,128]{1,0:T(8,128)S(1)}, u32[]{:S(2)}, u32[]{:S(2)}) %collective-permute-start.4) | collective-permute-done | bytes 65568 | tf_op jit(solution)/shard_map/ppermute | solution.py:780
  55.1 0.0 collective-permute-start.8
  55.1 0.0 collective-permute-done.2.strips
  55.1 1.2 %collective-permute-start.9 = (f32[128,128]{1,0:T(8,128)S(1)}, f32[128,128]{1,0:T(8,128)S(1)}, u32[]{:S(2)}, u32[]{:S(2)}) collective-permute-start(f32[128,128]{1,0:T(8,128)S(1)} %copy-done.17), channel_id=1, source_target_pairs={{0,28},{4,24},{8,20},{12,16},{16,12},{20,8},{24,4},{28,0},{1,29},{... | collective-permute-start | bytes 196616 | tf_op jit(solution)/shard_map/ppermute | solution.py:780
  56.3 7.2 %shard_map.62 = (f32[2,19,64,128]{3,2,1,0:T(8,128)}, f32[2,18,64,128]{3,2,1,0:T(8,128)}, f32[2,17,64,128]{3,2,1,0:T(8,128)}, f32[3,8,128]{2,1,0:T(8,128)}, f32[8,8,128]{2,1,0:T(8,128)}) custom-call(s32[4,128]{1,0:T(4,128)} %copy-done.5, f32[8,432,128]{2,1,0:T(8,128)} %copy-done, f32[2,19,64,128]{3,2,1,0:T(8,128)} %copy-done.2), custom_call_target="tpu_custom_call" | custom-call | flops 2000000 | bytes 1048576 | tf_op jit(solution)/shard_map/pallas_call | solution.py:794
  63.5 7.5 %shard_map.63 = (f32[32,128]{1,0:T(8,128)}, f32[2,17,64,128]{3,2,1,0:T(8,128)}, f32[2,17,64,128]{3,2,1,0:T(8,128)}, f32[2,17,64,128]{3,2,1,0:T(8,128)}, f32[3,2,18,8,128]{4,3,2,1,0:T(8,128)}) custom-call(s32[4,128]{1,0:T(4,128)} %copy-done.5, f32[37,8,128]{2,1,0:T(8,128)} %copy-done.6, f32[2,19,8,128]{3,2,1,0:T(8,128)} %copy-done.3, ...), custom_call_target="tpu_custom_call" | custom-call | flops 2000000 | bytes 1048576 | tf_op jit(solution)/shard_map/pallas_call | solution.py:800
  71.0 6.6 %all-to-all-start.1 = ((f32[32,1,128]{2,1,0:T(1,128)}), f32[32,1,128]{2,1,0:T(1,128)S(1)}, u32[]{:S(2)}, u32[]{:S(2)}) async-start(f32[32,1,128]{2,1,0:T(1,128)} %bitcast.26), calls=%async_computation.1 | async-start | bytes 32768 | tf_op jit(solution)/shard_map/all_to_all | solution.py:746
  77.6 0.0 collective-permute-done.5.rest_3_
  77.6 0.0 collective-permute-done.6.rest_4_
  77.6 0.0 collective-permute-done.7.rest_5_
  77.7 0.0 collective-permute-done.8.rest_6_
  77.7 0.0 collective-permute-done.9.rest_7_
  77.7 7.1 %all-to-all-done.1 = f32[32,1,128]{2,1,0:T(1,128)S(1)} async-done(((f32[32,1,128]{2,1,0:T(1,128)}), f32[32,1,128]{2,1,0:T(1,128)S(1)}, u32[]{:S(2)}, u32[]{:S(2)}) %all-to-all-start.1) | async-done | bytes 16416 | tf_op jit(solution)/shard_map/all_to_all | solution.py:746
  84.8 0.6 copy-done.15
  85.4 7.7 %shard_map.64 = (f32[2,16,64,128]{3,2,1,0:T(8,128)}, f32[2,16,64,128]{3,2,1,0:T(8,128)}, f32[4,128]{1,0:T(4,128)}, f32[32,128]{1,0:T(8,128)}) custom-call(s32[4,128]{1,0:T(4,128)} %copy-done.5, f32[32,128]{1,0:T(8,128)} %bitcast.24, f32[37,8,128]{2,1,0:T(8,128)} %copy-done.6, f32[2,19,8,128]{3,2,1,0:T(8,128)} %copy-done.3, ...), custom_call_target="tpu_custom_call" | custom-call | flops 2000000 | bytes 1048576 | tf_op jit(solution)/shard_map/pallas_call | solution.py:808
  93.1 10.2 %all_to_all.15 = f32[32,1,128]{2,1,0:T(1,128)} all-to-all(f32[32,1,128]{2,1,0:T(1,128)} %bitcast.27), channel_id=1, replica_groups=mesh['zm'=8,'zv'=4] {'zm','zv'}, dimensions={0} | all-to-all | bytes 32768 | tf_op jit(solution)/shard_map/all_to_all | solution.py:746
  103.3 4.1 %shard_map.65 = (f32[16,64,256]{2,1,0:T(8,128)}, f32[4]{0:T(128)}) custom-call(s32[4,128]{1,0:T(4,128)} %copy-done.5, f32[32,128]{1,0:T(8,128)} %bitcast.25, f32[16,64,256]{2,1,0:T(8,128)} %table_in.1, f32[2,16,64,128]{3,2,1,0:T(8,128)} %get-tuple-element.54.change_in, f32[2,16,64,128]{3,2,1,0:T(8,128)} %get-tuple-element.55.r3_in), custom_call_target="tpu_custom_call" | custom-call | flops 2000000 | bytes 1048576 | tf_op jit(solution)/shard_map/pallas_call | solution.py:818
  (51 shorter events, 0.1 us)
Async XLA Ops:
  4.3 5.4 %copy-start.16 = (f32[4,64,256]{2,1,0:T(8,128)S(1)}, f32[4,64,256]{2,1,0:T(8,128)}, u32[]{:S(2)}) copy-start(f32[4,64,256]{2,1,0:T(8,128)} %get-tuple-element.32) | copy-start | bytes 786436
  4.3 6.7 %copy-start.7 = (s32[4,32,8]{1,2,0:T(8,128)S(1)}, s32[4,32,8]{1,2,0:T(8,128)}, u32[]{:S(2)}) copy-start(s32[4,32,8]{1,2,0:T(8,128)} %param.5) | copy-start | bytes 12292
  4.3 8.8 %slice-start = ((f32[16,64,256]{2,1,0:T(8,128)}), f32[16,8,256]{2,1,0:T(8,128)S(1)}, s32[]{:S(2)}) async-start(f32[16,64,256]{2,1,0:T(8,128)} %table_in.1), calls=%async_computation.3 | async-start | bytes 262144 | tf_op jit(solution)/shard_map/slice | solution.py:772
  4.4 28.4 %all-to-all-start = ((f32[8,432,128]{2,1,0:T(8,128)}), f32[8,432,128]{2,1,0:T(8,128)S(1)}, u32[]{:S(2)}, u32[]{:S(2)}) async-start(f32[8,432,128]{2,1,0:T(8,128)} %get-tuple-element.31), calls=%async_computation | async-start | bytes 3538944 | tf_op jit(solution)/shard_map/all_to_all | solution.py:771
  9.7 3.4 %collective-permute-start = (f32[4,64,256]{2,1,0:T(8,128)S(1)}, f32[4,64,256]{2,1,0:T(8,128)S(1)}, u32[]{:S(2)}, u32[]{:S(2)}) collective-permute-start(f32[4,64,256]{2,1,0:T(8,128)S(1)} %copy-done.16), channel_id=1, source_target_pairs={{4,0},{8,4},{12,8},{16,12},{20,16},{24,20},{28,24},{5,1},{9,5},{13... | collective-permute-start | bytes 786440 | tf_op jit(solution)/shard_map/ppermute | solution.py:751
  13.1 8.1 %copy-start.1 = (f32[16,64,256]{2,1,0:T(8,128)S(1)}, f32[16,64,256]{2,1,0:T(8,128)}, u32[]{:S(2)}) copy-start(f32[16,64,256]{2,1,0:T(8,128)} %table_in.1) | copy-start | bytes 3145732
  13.8 7.4 %collective-permute-start.1 = (f32[20,8,256]{2,1,0:T(8,128)}, f32[20,8,256]{2,1,0:T(8,128)S(1)}, u32[]{:S(2)}, u32[]{:S(2)}) collective-permute-start(f32[20,8,256]{2,1,0:T(8,128)} %pad_maximum_fusion), channel_id=1, source_target_pairs={{1,0},{2,1},{3,2},{5,4},{6,5},{7,6},{9,8},{10,9},{11,10},{13,12},{... | collective-permute-start | bytes 491528 | tf_op jit(solution)/shard_map/ppermute | solution.py:751
  15.8 17.0 %copy-start.5 = (s32[4,128]{1,0:T(4,128)}, s32[4,128]{1,0:T(4,128)S(1)}, u32[]{:S(2)}) copy-start(s32[4,128]{1,0:T(4,128)S(1)} %concatenate.10.meta) | copy-start | bytes 6148
  18.8 14.0 %copy-start.4 = (f32[128,128]{1,0:T(8,128)S(1)}, f32[128,128]{1,0:T(8,128)}, u32[]{:S(2)}) copy-start(f32[128,128]{1,0:T(8,128)} %get-tuple-element.34.unused_b.rest_0_) | copy-start | bytes 196612
  23.8 1.1 copy-start.2
  24.9 38.6 %copy-start.3 = (f32[2,19,8,128]{3,2,1,0:T(8,128)}, f32[2,19,8,128]{3,2,1,0:T(8,128)S(1)}, u32[]{:S(2)}) copy-start(f32[2,19,8,128]{3,2,1,0:T(8,128)S(1)} %get-tuple-element.33.unused_a.interp_halo) | copy-start | bytes 466948
  24.9 11.2 %copy-start.23 = (f32[128,128]{1,0:T(8,128)S(1)}, f32[128,128]{1,0:T(8,128)}, u32[]{:S(2)}) copy-start(f32[128,128]{1,0:T(8,128)} %get-tuple-element.46) | copy-start | bytes 196612
  24.9 25.4 %copy-start.22 = (f32[128,128]{1,0:T(8,128)S(1)}, f32[128,128]{1,0:T(8,128)}, u32[]{:S(2)}) copy-start(f32[128,128]{1,0:T(8,128)} %get-tuple-element.47) | copy-start | bytes 196612
  24.9 26.1 %copy-start.21 = (f32[128,128]{1,0:T(8,128)S(1)}, f32[128,128]{1,0:T(8,128)}, u32[]{:S(2)}) copy-start(f32[128,128]{1,0:T(8,128)} %get-tuple-element.48) | copy-start | bytes 196612
  24.9 26.8 %copy-start.20 = (f32[128,128]{1,0:T(8,128)S(1)}, f32[128,128]{1,0:T(8,128)}, u32[]{:S(2)}) copy-start(f32[128,128]{1,0:T(8,128)} %get-tuple-element.49) | copy-start | bytes 196612
  24.9 27.6 %copy-start.19 = (f32[128,128]{1,0:T(8,128)S(1)}, f32[128,128]{1,0:T(8,128)}, u32[]{:S(2)}) copy-start(f32[128,128]{1,0:T(8,128)} %get-tuple-element.50) | copy-start | bytes 196612
  24.9 30.2 %copy-start.18 = (f32[128,128]{1,0:T(8,128)S(1)}, f32[128,128]{1,0:T(8,128)}, u32[]{:S(2)}) copy-start(f32[128,128]{1,0:T(8,128)} %get-tuple-element.51) | copy-start | bytes 196612
  24.9 30.2 %copy-start.17 = (f32[128,128]{1,0:T(8,128)S(1)}, f32[128,128]{1,0:T(8,128)}, u32[]{:S(2)}) copy-start(f32[128,128]{1,0:T(8,128)} %get-tuple-element.52) | copy-start | bytes 196612
  32.8 23.5 %copy-start = (f32[8,432,128]{2,1,0:T(8,128)}, f32[8,432,128]{2,1,0:T(8,128)S(1)}, u32[]{:S(2)}) copy-start(f32[8,432,128]{2,1,0:T(8,128)S(1)} %all-to-all-done.data) | copy-start | bytes 5308420
  34.7 20.4 %collective-permute-start.2 = (f32[37,8,128]{2,1,0:T(8,128)S(1)}, f32[37,8,128]{2,1,0:T(8,128)S(1)}, u32[]{:S(2)}, u32[]{:S(2)}) collective-permute-start(f32[37,8,128]{2,1,0:T(8,128)S(1)} %shard_map.61), channel_id=1, source_target_pairs={{1,0},{2,1},{3,2},{5,4},{6,5},{7,6},{9,8},{10,9},{11,10},{13,12},{... | collective-permute-start | bytes 454664 | tf_op jit(solution)/shard_map/ppermute | solution.py:751
  36.1 16.4 %collective-permute-start.3 = (f32[128,128]{1,0:T(8,128)S(1)}, f32[128,128]{1,0:T(8,128)S(1)}, u32[]{:S(2)}, u32[]{:S(2)}) collective-permute-start(f32[128,128]{1,0:T(8,128)S(1)} %copy-done.23), channel_id=1, source_target_pairs={{0,4},{4,0},{8,12},{12,8},{16,20},{20,16},{24,28},{28,24},{1,5},{5... | collective-permute-start | bytes 196616 | tf_op jit(solution)/shard_map/ppermute | solution.py:780
  50.2 4.8 %collective-permute-start.4 = (f32[128,128]{1,0:T(8,128)S(1)}, f32[128,128]{1,0:T(8,128)S(1)}, u32[]{:S(2)}, u32[]{:S(2)}) collective-permute-start(f32[128,128]{1,0:T(8,128)S(1)} %copy-done.22), channel_id=1, source_target_pairs={{0,8},{4,12},{8,0},{12,4},{16,24},{20,28},{24,16},{28,20},{1,9},{5... | collective-permute-start | bytes 196616 | tf_op jit(solution)/shard_map/ppermute | solution.py:780
  50.9 26.6 %collective-permute-start.5 = (f32[128,128]{1,0:T(8,128)S(1)}, f32[128,128]{1,0:T(8,128)S(1)}, u32[]{:S(2)}, u32[]{:S(2)}) collective-permute-start(f32[128,128]{1,0:T(8,128)S(1)} %copy-done.21), channel_id=1, source_target_pairs={{0,12},{4,8},{8,4},{12,0},{16,28},{20,24},{24,20},{28,16},{1,13},{... | collective-permute-start | bytes 196616 | tf_op jit(solution)/shard_map/ppermute | solution.py:780
  51.7 25.9 %collective-permute-start.6 = (f32[128,128]{1,0:T(8,128)S(1)}, f32[128,128]{1,0:T(8,128)S(1)}, u32[]{:S(2)}, u32[]{:S(2)}) collective-permute-start(f32[128,128]{1,0:T(8,128)S(1)} %copy-done.20), channel_id=1, source_target_pairs={{0,16},{4,20},{8,24},{12,28},{16,0},{20,4},{24,8},{28,12},{1,17},{... | collective-permute-start | bytes 196616 | tf_op jit(solution)/shard_map/ppermute | solution.py:780
  52.4 11.1 %copy-start.8 = (f32[128,128]{1,0:T(8,128)}, f32[128,128]{1,0:T(8,128)S(1)}, u32[]{:S(2)}) copy-start(f32[128,128]{1,0:T(8,128)S(1)} %collective-permute-done.3.rest_1_) | copy-start | bytes 196612
  52.4 25.2 %collective-permute-start.7 = (f32[128,128]{1,0:T(8,128)S(1)}, f32[128,128]{1,0:T(8,128)S(1)}, u32[]{:S(2)}, u32[]{:S(2)}) collective-permute-start(f32[128,128]{1,0:T(8,128)S(1)} %copy-done.19), channel_id=1, source_target_pairs={{0,20},{4,16},{8,28},{12,24},{16,4},{20,0},{24,12},{28,8},{1,21},{... | collective-permute-start | bytes 196616 | tf_op jit(solution)/shard_map/ppermute | solution.py:780
  55.1 8.4 %copy-start.9 = (f32[128,128]{1,0:T(8,128)}, f32[128,128]{1,0:T(8,128)S(1)}, u32[]{:S(2)}) copy-start(f32[128,128]{1,0:T(8,128)S(1)} %collective-permute-done.4.rest_2_) | copy-start | bytes 196612
  55.1 22.6 %collective-permute-start.8 = (f32[128,128]{1,0:T(8,128)S(1)}, f32[128,128]{1,0:T(8,128)S(1)}, u32[]{:S(2)}, u32[]{:S(2)}) collective-permute-start(f32[128,128]{1,0:T(8,128)S(1)} %copy-done.18), channel_id=1, source_target_pairs={{0,24},{4,28},{8,16},{12,20},{16,8},{20,12},{24,0},{28,4},{1,25},{... | collective-permute-start | bytes 196616 | tf_op jit(solution)/shard_map/ppermute | solution.py:780
  55.1 8.4 %copy-start.6 = (f32[37,8,128]{2,1,0:T(8,128)}, f32[37,8,128]{2,1,0:T(8,128)S(1)}, u32[]{:S(2)}) copy-start(f32[37,8,128]{2,1,0:T(8,128)S(1)} %collective-permute-done.2.strips) | copy-start | bytes 454660
  55.1 22.6 %collective-permute-start.9 = (f32[128,128]{1,0:T(8,128)S(1)}, f32[128,128]{1,0:T(8,128)S(1)}, u32[]{:S(2)}, u32[]{:S(2)}) collective-permute-start(f32[128,128]{1,0:T(8,128)S(1)} %copy-done.17), channel_id=1, source_target_pairs={{0,28},{4,24},{8,20},{12,16},{16,12},{20,8},{24,4},{28,0},{1,29},{... | collective-permute-start | bytes 196616 | tf_op jit(solution)/shard_map/ppermute | solution.py:780
  71.0 13.8 %all-to-all-start.1 = ((f32[32,1,128]{2,1,0:T(1,128)}), f32[32,1,128]{2,1,0:T(1,128)S(1)}, u32[]{:S(2)}, u32[]{:S(2)}) async-start(f32[32,1,128]{2,1,0:T(1,128)} %bitcast.26), calls=%async_computation.1 | async-start | bytes 32768 | tf_op jit(solution)/shard_map/all_to_all | solution.py:746
  77.6 7.2 %copy-start.10 = (f32[128,128]{1,0:T(8,128)}, f32[128,128]{1,0:T(8,128)S(1)}, u32[]{:S(2)}) copy-start(f32[128,128]{1,0:T(8,128)S(1)} %collective-permute-done.5.rest_3_) | copy-start | bytes 196612
  77.6 7.2 %copy-start.11 = (f32[128,128]{1,0:T(8,128)}, f32[128,128]{1,0:T(8,128)S(1)}, u32[]{:S(2)}) copy-start(f32[128,128]{1,0:T(8,128)S(1)} %collective-permute-done.6.rest_4_) | copy-start | bytes 196612
  77.6 7.2 %copy-start.12 = (f32[128,128]{1,0:T(8,128)}, f32[128,128]{1,0:T(8,128)S(1)}, u32[]{:S(2)}) copy-start(f32[128,128]{1,0:T(8,128)S(1)} %collective-permute-done.7.rest_5_) | copy-start | bytes 196612
  77.7 7.1 %copy-start.13 = (f32[128,128]{1,0:T(8,128)}, f32[128,128]{1,0:T(8,128)S(1)}, u32[]{:S(2)}) copy-start(f32[128,128]{1,0:T(8,128)S(1)} %collective-permute-done.8.rest_6_) | copy-start | bytes 196612
  77.7 7.1 %copy-start.14 = (f32[128,128]{1,0:T(8,128)}, f32[128,128]{1,0:T(8,128)S(1)}, u32[]{:S(2)}) copy-start(f32[128,128]{1,0:T(8,128)S(1)} %collective-permute-done.9.rest_7_) | copy-start | bytes 196612
  84.8 0.6 copy-start.15

commit v2 on v1

--- a/solution.py
+++ b/solution.py
@@ -42,7 +42,7 @@
 VMEM = pl.BlockSpec(memory_space=pltpu.VMEM)
 SMEM = pl.BlockSpec(memory_space=pltpu.SMEM)
 HBM = pl.BlockSpec(memory_space=pltpu.HBM)
-WHOLE = 60
+WHOLE = 53.5
 PART = 24
 
 
@@ -53,7 +53,7 @@
         in_specs=in_specs,
         out_specs=out_specs,
         scratch_shapes=list(scratch),
-        compiler_params=pltpu.CompilerParams(vmem_limit_bytes=limit << 20),
+        compiler_params=pltpu.CompilerParams(vmem_limit_bytes=int(limit * (1 << 20))),
         cost_estimate=pl.CostEstimate(flops=flops, bytes_accessed=1 << 20, transcendentals=0),
     )
 
@@ -163,6 +163,12 @@
     return (left & first) | (~left & second)
 
 
+def fetch(source, target, sem):
+    copy = pltpu.make_async_copy(source, target, sem)
+    copy.start()
+    return copy
+
+
 def strip_body(g, meta, data, unused_a, unused_b, out, held, planes, sems):
     three = range(ITERS - 1)
     left, sub = lane_ids() < HALF, sub_ids()
@@ -357,8 +363,9 @@
     return [tile_rows(vt) for vt in (pair // g.ct * 2, pair // g.ct * 2 + 1)]
 
 
-def local_body(g, meta, data, interp_in, a0_out, a1_out, a2_out, totals, peaks,
-               held, interp, f0, f1, f2, a0, a1, a2, masks, sems, out_sems):
+def local_body(g, meta_in, data, interp_in, a0_out, a1_out, a2_out, totals_out, peaks_out,
+               meta, totals, peaks, held, interp, f0, f1, f2, a0, a1, a2, masks, sems, out_sems):
+    meta_copy = fetch(meta_in, meta, sems.at[6 + 2 * g.ct])
     f, a, outs = (f0, f1, f2), (a0, a1, a2), (a0_out, a1_out, a2_out)
     split = BLOCK_Z // 2
     groups = ([], [])
@@ -374,8 +381,9 @@
         for copy in group:
             copy.start()
     left = lane_ids() < HALF
+    peaks[...] = jnp.zeros_like(peaks)
+    meta_copy.wait()
     fill_masks(g, meta, masks, (0, 1, 2), left)
-    peaks[...] = jnp.zeros_like(peaks)
     for copy in groups[0]:
         copy.wait()
 
@@ -439,15 +447,22 @@
                 writes[-1].start()
     for t in range(3):
         totals[t] = carry[t]
+    writes.append(fetch(totals, totals_out, out_sems.at[9 * g.ct]))
+    writes.append(fetch(peaks, peaks_out, out_sems.at[9 * g.ct + 1]))
     for write in writes:
         write.wait()
 
 
-def middle_body(g, meta, strips, interp_halo, totals, a0_in, a1_in, a2_in,
-                out, ca0_out, ca1_out, cb1_out, halos,
-                a0, a1, a2, b1, ca0, ca1, cb1, a0_halo, a1_halo, b1_halo, masks, sems, out_sems):
+def middle_body(g, meta_in, strips_in, interp_halo_in, totals_in, a0_in, a1_in, a2_in,
+                out_hbm, ca0_out, ca1_out, cb1_out, halos_out,
+                meta, strips, interp_halo, totals, out, halos, a0, a1, a2, b1, ca0, ca1, cb1, a0_halo, a1_halo, b1_halo, masks, sems, out_sems):
     split = BLOCK_Z // 2
-    groups, at = ([], []), 0
+    groups, at = ([], []), 6 * g.ct
+    small = []
+    for source, target in ((meta_in, meta), (strips_in, strips), (interp_halo_in, interp_halo), (totals_in, totals)):
+        small.append(fetch(source, target, sems.at[at]))
+        at += 1
+    at = 0
     for source, target, layers in ((a0_in, a0, LAYERS[0]), (a1_in, a1, LAYERS[1]), (a2_in, a2, BLOCK_Z)):
         for col in range(g.ct):
             for group, span in ((0, slice(split, layers)), (1, slice(0, split))):
@@ -456,6 +471,12 @@
     for group in groups:
         for copy in group:
             copy.start()
+    none = LAYERS[0]
+    for col in range(g.ct):
+        for field in (a1, a2, b1, ca0):
+            field[col, none] = jnp.zeros((g.span, LANES), F32)
+    for copy in small:
+        copy.wait()
     edge_z, edge_v = edges(meta)
     stencil = Stencil(g, edge_v)
     left = lane_ids() < HALF
@@ -472,10 +493,6 @@
             a1_halo[col, z] = jnp.where(live1[z >= BLOCK_Z][col], value, 0.0)
     get0, get1, getb = reader(g, a0, a0_halo), reader(g, a1, a1_halo), reader(g, b1, b1_halo)
     top0, top1 = LAYERS[1] - 1, LAYERS[2] - 1
-    none = LAYERS[0]
-    for col in range(g.ct):
-        for field in (a1, a2, b1, ca0):
-            field[col, none] = jnp.zeros((g.span, LANES), F32)
     for copy in groups[0]:
         copy.wait()
 
@@ -536,8 +553,10 @@
                 sem = out_sems.at[(index * 3 + which) * g.ct + col]
                 writes.append(pltpu.make_async_copy(source.at[col, span], target.at[col, span], sem))
                 writes[-1].start()
+    writes.append(fetch(halos, halos_out, out_sems.at[9 * g.ct]))
     values = [totals[0], totals[1], carry[0], carry[1], totals[2]] + list(carry[2:])
     out[...] = spread_rows(values, out.shape[0])
+    writes.append(fetch(out, out_hbm, out_sems.at[9 * g.ct + 1]))
     for write in writes:
         write.wait()
 
@@ -568,12 +587,16 @@
     return [jnp.broadcast_to(w, TILE) for w in (w0, w1, weight_of(total, live_cells(g, meta, 2)))]
 
 
-def last_body(g, meta, parts, strips, interp_halo, halos_in, peaks0, a0_in, a1_in, a2_in, interp_in, ca0_in, ca1_in, cb1_in,
+def last_body(g, meta_in, parts, strips_in, interp_halo_in, halos_hbm, peaks0_in, a0_in, a1_in, a2_in, interp_in, ca0_in, ca1_in, cb1_in,
               *rest):
     data, rest = rest[: g.zm], rest[g.zm :]
-    (sum_hbm, r3_hbm, errors, out,
-     held, f3, a0, a1, a2, interp, ca0, ca1, cb1, r2, r2_halo, change, sum_out, r3, masks, peaks, sems, out_sems) = rest
+    (sum_hbm, r3_hbm, errors_out, out,
+     meta, strips, interp_halo, halos_in, peaks0, errors, held, f3, a0, a1, a2, interp, ca0, ca1, cb1, r2, r2_halo, change, sum_out, r3, masks, peaks, sems, out_sems) = rest
     top = LAYERS[2] - 1
+    small = []
+    for source, target in ((meta_in, meta), (strips_in, strips), (interp_halo_in, interp_halo), (halos_hbm, halos_in),
+                           (peaks0_in, peaks0)):
+        small.append(fetch(source, target, sems.at[g.zm + 28 * g.ct + len(small)]))
     chunks = segments(top, (5, 4, 4, 4))
     reads, at = [], 0
     for lowest, highest in chunks:
@@ -593,6 +616,9 @@
     for group in reads:
         for copy in group:
             copy.start()
+    peaks[...] = jnp.zeros_like(peaks)
+    for copy in small:
+        copy.wait()
     edge_z, edge_v = edges(meta)
     stencil = Stencil(g, edge_v)
     left = lane_ids() < HALF
@@ -600,7 +626,6 @@
     w0, w1, w2 = three_weights(g, meta, parts)
     w01 = w0 * w1
     live = halo_live(g, meta, 2, left)
-    peaks[...] = jnp.zeros_like(peaks)
     for col in range(g.ct):
         for z in range(LAYERS[2]):
             value = interp_halo[col, z] + w0 * halos_in[0, col, z] + w1 * halos_in[1, col, z] - w01 * halos_in[2, col, z]
@@ -679,12 +704,14 @@
             found = found + jnp.sum(jnp.where(lane_p == place, column, 0.0), axis=0, keepdims=True)
         errors[i : i + 1, :] = found
         line = jnp.where(lane == 1 + i, jnp.max(found, axis=1, keepdims=True), line)
+    writes.append(fetch(errors, errors_out, out_sems.at[8 * g.ct]))
+    line = jnp.where(lane == 1 + ITERS, live_cells(g, meta, ITERS - 1), line)
     out[...] = jnp.broadcast_to(line, out.shape)
     for write in writes:
         write.wait()
 
 
-def finish_body(g, meta, parts, table_in, change_in, r3_in, out_hbm, worst, table, change, r3, out, sems, out_sems):
+def finish_body(g, parts, table_in, change_in, r3_in, out_hbm, worst_out, table, change, r3, out, worst, sems, out_sems):
     quarter = BLOCK_Z // 4
     spans = [slice(part * quarter, (part + 1) * quarter) for part in range(4)]
     reads = []
@@ -700,8 +727,11 @@
         for read in group:
             read.start()
     total = lane_values(jnp.sum(parts[...], axis=0, keepdims=True), 1)[0]
-    w3 = jnp.broadcast_to(weight_of(total, live_cells(g, meta, 3)), TILE)
-    writes = []
+    largest = lane_values(jnp.max(parts[...], axis=0, keepdims=True), 2 + ITERS)
+    w3 = jnp.broadcast_to(weight_of(total, largest[1 + ITERS]), TILE)
+    for i in range(ITERS):
+        worst[i] = jnp.max(largest[1 + i])
+    writes = [fetch(worst, worst_out, out_sems.at[4])]
     for part, span in enumerate(spans):
         for read in reads[part]:
             read.wait()
@@ -713,9 +743,6 @@
                     out[z, rows, lanes] = table[z, rows, lanes] + (change[col, z, rows, :] + w3 * r3[col, z, rows, :])
         writes.append(pltpu.make_async_copy(out.at[span], out_hbm.at[span], out_sems.at[part]))
         writes[-1].start()
-    line = jnp.max(parts[...], axis=0, keepdims=True)
-    for i, value in enumerate(lane_values(line, 1 + ITERS)[1:]):
-        worst[i] = jnp.max(value)
     for write in writes:
         write.wait()
 
@@ -765,7 +792,7 @@
         part(pack_three_body, g), [struct(g.zm, OFFSET[3], LANES), struct(ITERS, *table.shape[1:])], [SMEM, HBM, HBM], [HBM] * 2,
         [pltpu.SMEM((ITERS, g.zm), jnp.int32), vmem(3 * g.slots, ROWS, LANES), vmem(g.zm, OFFSET[3] - 3 * ROWS, LANES),
          vmem(ITERS, *table.shape[1:]), dma(3 * g.slots + 1), dma(3 * g.zm + 4)],
-        WHOLE,
+        60,
     )(slots, views, table)
     below = from_next(top, "zm")
     data = lax.all_to_all(packed, "zm", 0, 0, tiled=True)
@@ -793,33 +820,38 @@
     own, more, most = struct(*main(BLOCK_Z)), struct(*main(LAYERS[2])), struct(*main(LAYERS[1]))
     a0, a1, a2, totals, peaks0 = call(
         part(local_body, g), [struct(*main(LAYERS[0])), most, more, struct(3, *TILE), struct(g.pairs, *TILE)],
-        [SMEM] + [HBM] * 2, [HBM] * 3 + [VMEM] * 2,
-        [vmem(*data.shape)] + [vmem(*main(LAYERS[0]))] * 7
-        + [vmem(3, 2, g.pairs, *TILE), dma(6 + 2 * g.ct), dma(9 * g.ct)], WHOLE,
+        [HBM] * 3, [HBM] * 5,
+        [pltpu.SMEM(meta.shape, jnp.int32), vmem(3, *TILE), vmem(g.pairs, *TILE), vmem(*data.shape)]
+        + [vmem(*main(LAYERS[0]))] * 7
+        + [vmem(3, 2, g.pairs, *TILE), dma(7 + 2 * g.ct), dma(9 * g.ct + 2)], WHOLE,
     )(meta, data, interp)
     products, ca0, ca1, cb1, halos = call(
         part(middle_body, g), [struct(everyone, 128), more, more, more, struct(3, *halo(LAYERS[1]))],
-        [SMEM] + [VMEM] * 3 + [HBM] * 3, [VMEM] + [HBM] * 3 + [VMEM],
-        [vmem(*main(LAYERS[0] + 1))] * 7 + [vmem(*halo(LAYERS[0] + 1))] * 3
-        + [vmem(2, 2, g.pairs, *TILE), dma(6 * g.ct), dma(9 * g.ct)],
+        [HBM] * 7, [HBM] * 5,
+        [pltpu.SMEM(meta.shape, jnp.int32), vmem(*strips.shape), vmem(*interp_halo.shape), vmem(3, *TILE),
+         vmem(everyone, 128), vmem(3, *halo(LAYERS[1]))]
+        + [vmem(*main(LAYERS[0] + 1))] * 7 + [vmem(*halo(LAYERS[0] + 1))] * 3
+        + [vmem(2, 2, g.pairs, *TILE), dma(6 * g.ct + 4), dma(9 * g.ct + 2)],
         WHOLE,
     )(meta, strips, interp_halo, totals, a0, a1, a2)
     products = to_all(products)
     change, r3, errors, stats = call(
         part(last_body, g), [own, own, struct(ITERS, 128), struct(everyone, 128)],
-        [SMEM] + [VMEM] * 5 + [HBM] * (7 + g.zm), [HBM] * 2 + [VMEM] * 2,
-        [vmem(g.zm, ROWS, LANES)] + [vmem(*main(BLOCK_Z))] * 3 + [vmem(*main(LAYERS[2])), vmem(*main(BLOCK_Z))]
+        [HBM, VMEM] + [HBM] * (11 + g.zm), [HBM] * 3 + [VMEM],
+        [pltpu.SMEM(meta.shape, jnp.int32), vmem(*strips.shape), vmem(*interp_halo.shape), vmem(*halos.shape),
+         vmem(*peaks0.shape), vmem(ITERS, 128), vmem(g.zm, ROWS, LANES)] + [vmem(*main(BLOCK_Z))] * 3 + [vmem(*main(LAYERS[2])), vmem(*main(BLOCK_Z))]
         + [vmem(*main(LAYERS[2]))] * 4 + [vmem(*halo(LAYERS[2])), vmem(*main(LAYERS[2]))]
         + [vmem(*main(BLOCK_Z))] * 2
-        + [vmem(3, 2, g.pairs, *TILE), vmem(3, g.pairs, *TILE), dma(g.zm + 28 * g.ct), dma(8 * g.ct)],
+        + [vmem(3, 2, g.pairs, *TILE), vmem(3, g.pairs, *TILE), dma(g.zm + 28 * g.ct + 5), dma(8 * g.ct + 1)],
         WHOLE,
     )(meta, products, strips, interp_halo, halos, peaks0, a0, a1, a2, interp, ca0, ca1, cb1, *last_data)
     stats = to_all(stats)
     table_out, worst = call(
-        part(finish_body, g), [struct(*table.shape), struct(ITERS)], [SMEM, VMEM] + [HBM] * 3, [HBM, SMEM],
-        [vmem(*table.shape)] + [vmem(*main(BLOCK_Z))] * 2 + [vmem(*table.shape), dma(4 * (1 + 2 * g.ct)), dma(4)],
+        part(finish_body, g), [struct(*table.shape), struct(ITERS)], [VMEM] + [HBM] * 3, [HBM] * 2,
+        [vmem(*table.shape)] + [vmem(*main(BLOCK_Z))] * 2
+        + [vmem(*table.shape), pltpu.SMEM((ITERS,), F32), dma(4 * (1 + 2 * g.ct)), dma(5)],
         WHOLE,
-    )(meta, stats, table, change, r3)
+    )(stats, table, change, r3)
     return (table_out, errors[:, : g.blocks], worst)
 
 

time: 108 us -> 102 us (0.944)
  Pallas kernels: 37.5 us -> 32.5 us
  blocking collectives: 10.2 us -> 8.89 us
  waiting for transfers between devices: 20.5 us -> 19.4 us
    pallas_call x1, Pallas kernels: 7.69 us -> 6.3 us  [shards(): call(part(last_body, g), [own, own, struct(ITERS, 128), struct(everyone,...]
    all_to_all x1, blocking collectives: 10.2 us -> 8.89 us  [to_all(): lax.all_to_all(rows.reshape(count, 1, 128), AXES, 0, 0, tiled=True)]
    pallas_call x1, Pallas kernels: 7.2 us -> 5.91 us  [shards(): call(part(local_body, g), [struct(*main(LAYERS[0])), most, more, struct(3...]
    pallas_call x1, Pallas kernels: 4.05 us -> 2.82 us  [shards(): call(part(finish_body, g), [struct(*table.shape), struct(ITERS)], [VMEM]...]
    pallas_call x1, Pallas kernels: 7.49 us -> 6.31 us  [shards(): call(part(middle_body, g), [struct(everyone, 128), more, more, more, stru...]
    unnamed x49 -> x37, local copies, waits for them, and re-layouts: 1.79 us -> 2.45 us
  transfers between devices with their start and end apart: 12 -> 12, of which waited for: 5 -> 5; matrix products, arithmetic and copies ran while one was open for 2% -> 2% of each run, Pallas kernels for 19% -> 18%
where the time goes in v2:
time: 102 us; the launch traced here: 101 us
  starting transfers between devices  35.1 us (34%)
  Pallas kernels  32.5 us (32%)
  waiting for transfers between devices  19.4 us (19%)
  blocking collectives  8.89 us (9%)
  local copies, waits for them, and re-layouts  2.76 us (3%)
  other arithmetic  1.25 us (1%)
    ppermute x7, starting transfers between devices, shards(): lax.ppermute(packed[k], 'zm', [(i, i ^ k) for i in range(g.zm)])  18.9 us
    all_to_all x1, blocking collectives, to_all(): lax.all_to_all(rows.reshape(count, 1, 128), AXES, 0, 0, tiled=True)  8.89 us
    all_to_all x1, waiting for transfers between devices, shards(): data = lax.all_to_all(packed, 'zm', 0, 0, tiled=True)  7.47 us
    all_to_all x1, waiting for transfers between devices, to_all(): lax.all_to_all(rows.reshape(count, 1, 128), AXES, 0, 0, tiled=True)  7.11 us
    all_to_all x1, starting transfers between devices, to_all(): lax.all_to_all(rows.reshape(count, 1, 128), AXES, 0, 0, tiled=True)  7.01 us
    pallas_call x1, Pallas kernels, shards(): call(part(middle_body, g), [struct(everyone, 128), more, more, more, stru...  6.31 us
    pallas_call x1, Pallas kernels, shards(): call(part(last_body, g), [own, own, struct(ITERS, 128), struct(everyone,...  6.3 us
    pallas_call x1, Pallas kernels, shards(): call(part(local_body, g), [struct(*main(LAYERS[0])), most, more, struct(3...  5.91 us
  transfers between devices with their start and end apart: 12, of which 5 were waited for; matrix products, arithmetic and copies ran while one was open for 2% of the time, Pallas kernels for 18%

profile of v2, /device:TPU:0, one launch (start us, length us, event | category | flops | bytes accessed | tf_op | source)
XLA Modules:
  0.0 101.0 jit_solution(5955763062689406498)
XLA Ops:
  0.6 3.7 %shard_map.58 = (f32[8,432,128]{2,1,0:T(8,128)}, f32[4,64,256]{2,1,0:T(8,128)}) custom-call(s32[32,32]{1,0:T(8,128)} %bitcast.20, f32[32,128,128]{2,1,0:T(8,128)} %bitcast.25, f32[16,64,256]{2,1,0:T(8,128)} %table_in.1), custom_call_target="tpu_custom_call" | custom-call | flops 2000000 | bytes 1048576 | tf_op jit(solution)/shard_map/pallas_call | solution.py:791
  4.3 0.0 copy-start.15
  4.3 0.0 copy-start.5
  4.3 0.0 slice-start
  4.4 5.3 %all-to-all-start = ((f32[8,432,128]{2,1,0:T(8,128)}), f32[8,432,128]{2,1,0:T(8,128)S(1)}, u32[]{:S(2)}, u32[]{:S(2)}) async-start(f32[8,432,128]{2,1,0:T(8,128)} %get-tuple-element.31), calls=%async_computation | async-start | bytes 3538944 | tf_op jit(solution)/shard_map/all_to_all | solution.py:798
  9.7 1.3 %collective-permute-start = (f32[4,64,256]{2,1,0:T(8,128)S(1)}, f32[4,64,256]{2,1,0:T(8,128)S(1)}, u32[]{:S(2)}, u32[]{:S(2)}) collective-permute-start(f32[4,64,256]{2,1,0:T(8,128)S(1)} %copy-done.15), channel_id=1, source_target_pairs={{4,0},{8,4},{12,8},{16,12},{20,16},{24,20},{28,24},{5,1},{9,5},{13... | collective-permute-start | bytes 786440 | tf_op jit(solution)/shard_map/ppermute | solution.py:778
  11.1 0.2 convert_reduce_fusion
  11.2 0.1 broadcast_select_fusion
  11.3 1.8 %collective-permute-done.below = f32[4,64,256]{2,1,0:T(8,128)S(1)} collective-permute-done((f32[4,64,256]{2,1,0:T(8,128)S(1)}, f32[4,64,256]{2,1,0:T(8,128)S(1)}, u32[]{:S(2)}, u32[]{:S(2)}) %collective-permute-start) | collective-permute-done | bytes 262176 | tf_op jit(solution)/shard_map/ppermute | solution.py:778
  13.1 0.7 pad_maximum_fusion
  13.8 1.3 %collective-permute-start.1 = (f32[20,8,256]{2,1,0:T(8,128)}, f32[20,8,256]{2,1,0:T(8,128)}, u32[]{:S(2)}, u32[]{:S(2)}) collective-permute-start(f32[20,8,256]{2,1,0:T(8,128)} %pad_maximum_fusion), channel_id=1, source_target_pairs={{1,0},{2,1},{3,2},{5,4},{6,5},{7,6},{9,8},{10,9},{11,10},{13,12},{... | collective-permute-start | bytes 491528 | tf_op jit(solution)/shard_map/ppermute | solution.py:778
  15.1 0.1 add_convert_fusion
  15.2 0.1 copy.13
  15.3 0.1 copy.14
  15.4 0.1 eq.32
  15.5 0.2 select_reduce_fusion
  15.7 0.1 concatenate.10.meta.meta_in
  15.8 2.7 %shard_map.60 = (f32[128,128]{1,0:T(8,128)S(1)}, f32[128,128]{1,0:T(8,128)S(1)}, f32[128,128]{1,0:T(8,128)S(1)}, f32[128,128]{1,0:T(8,128)S(1)}, f32[128,128]{1,...) custom-call(s32[32,32]{1,0:T(8,128)S(1)} %bitcast.21, f32[32,128,128]{2,1,0:T(8,128)} %bitcast.26), custom_call_target="tpu_custom_call" | custom-call | flops 2000000 | bytes 1048576 | tf_op jit(solution)/shard_map/pallas_call | solution.py:801
  18.5 0.6 copy-done.6
  19.2 0.6 copy-done.10
  19.8 1.5 %collective-permute-done.1.strip = f32[20,8,256]{2,1,0:T(8,128)} collective-permute-done((f32[20,8,256]{2,1,0:T(8,128)}, f32[20,8,256]{2,1,0:T(8,128)}, u32[]{:S(2)}, u32[]{:S(2)}) %collective-permute-start.1) | collective-permute-done | bytes 163872 | tf_op jit(solution)/shard_map/ppermute | solution.py:778
  21.3 2.9 %shard_map.59 = (f32[2,19,64,128]{3,2,1,0:T(8,128)S(1)}, f32[2,19,8,128]{3,2,1,0:T(8,128)S(1)}) custom-call(s32[4,128]{1,0:T(4,128)S(1)} %concatenate.10.meta.meta_in, f32[16,64,256]{2,1,0:T(8,128)S(1)} %copy-done.1, f32[4,64,256]{2,1,0:T(8,128)S(1)} %collective-permute-done.below, f32[20,8,256]{2,1,0:T(8,128)} %collective-permute-done.1.strip), custom_call_target="tpu_custom_call" | custom-call | flops 2000000 | bytes 1048576 | tf_op jit(solution)/shard_map/pallas_call | solution.py:809
  24.3 1.1 %copy-done.2 = f32[2,19,64,128]{3,2,1,0:T(8,128)} copy-done((f32[2,19,64,128]{3,2,1,0:T(8,128)}, f32[2,19,64,128]{3,2,1,0:T(8,128)S(1)}, u32[]{:S(2)}) %copy-start.2) | copy-done | bytes 1245208
  25.3 7.5 %all-to-all-done.data = f32[8,432,128]{2,1,0:T(8,128)S(1)} async-done(((f32[8,432,128]{2,1,0:T(8,128)}), f32[8,432,128]{2,1,0:T(8,128)S(1)}, u32[]{:S(2)}, u32[]{:S(2)}) %all-to-all-start) | async-done | bytes 1769504 | tf_op jit(solution)/shard_map/all_to_all | solution.py:798
  32.8 1.9 %shard_map.61 = f32[37,8,128]{2,1,0:T(8,128)S(1)} custom-call(s32[4,128]{1,0:T(4,128)S(1)} %concatenate.10.meta.meta_in, f32[8,432,128]{2,1,0:T(8,128)S(1)} %all-to-all-done.data, f32[2,19,8,128]{3,2,1,0:T(8,128)S(1)} %get-tuple-element.33.unused_a.interp_halo_in, f32[128,128]{1,0:T(8,128)S(1)} %get-tuple-element.34.unused_b.rest_0_), custom_call_target="tpu_custom_call" | custom-call | flops 2000000 | bytes 1048576 | tf_op jit(solution)/shard_map/pallas_call | solution.py:814
  34.7 1.3 %collective-permute-start.2 = (f32[37,8,128]{2,1,0:T(8,128)S(1)}, f32[37,8,128]{2,1,0:T(8,128)S(1)}, u32[]{:S(2)}, u32[]{:S(2)}) collective-permute-start(f32[37,8,128]{2,1,0:T(8,128)S(1)} %shard_map.61), channel_id=1, source_target_pairs={{1,0},{2,1},{3,2},{5,4},{6,5},{7,6},{9,8},{10,9},{11,10},{13,12},{... | collective-permute-start | bytes 454664 | tf_op jit(solution)/shard_map/ppermute | solution.py:778
  36.1 14.5 %collective-permute-start.3 = (f32[128,128]{1,0:T(8,128)S(1)}, f32[128,128]{1,0:T(8,128)S(1)}, u32[]{:S(2)}, u32[]{:S(2)}) collective-permute-start(f32[128,128]{1,0:T(8,128)S(1)} %copy-done.11), channel_id=1, source_target_pairs={{0,4},{4,0},{8,12},{12,8},{16,20},{20,16},{24,28},{28,24},{1,5},{5... | collective-permute-start | bytes 196616 | tf_op jit(solution)/shard_map/ppermute | solution.py:807
  50.6 0.8 collective-permute-start.4
  51.4 0.6 collective-permute-start.5
  52.0 0.8 collective-permute-start.6
  52.9 0.0 collective-permute-done.3.rest_1_
  52.9 1.2 %collective-permute-start.7 = (f32[128,128]{1,0:T(8,128)S(1)}, f32[128,128]{1,0:T(8,128)S(1)}, u32[]{:S(2)}, u32[]{:S(2)}) collective-permute-start(f32[128,128]{1,0:T(8,128)S(1)} %get-tuple-element.50), channel_id=1, source_target_pairs={{0,20},{4,16},{8,28},{12,24},{16,4},{20,0},{24,12},{28,8},{1,21},{... | collective-permute-start | bytes 196616 | tf_op jit(solution)/shard_map/ppermute | solution.py:807
  54.1 1.4 %collective-permute-done.4.rest_2_ = f32[128,128]{1,0:T(8,128)S(1)} collective-permute-done((f32[128,128]{1,0:T(8,128)}, f32[128,128]{1,0:T(8,128)S(1)}, u32[]{:S(2)}, u32[]{:S(2)}) %collective-permute-start.4) | collective-permute-done | bytes 65568 | tf_op jit(solution)/shard_map/ppermute | solution.py:807
  55.5 0.0 collective-permute-start.8
  55.5 0.0 collective-permute-done.2.strips_in
  55.6 0.9 collective-permute-start.9
  56.5 5.9 %shard_map.62 = (f32[2,19,64,128]{3,2,1,0:T(8,128)}, f32[2,18,64,128]{3,2,1,0:T(8,128)}, f32[2,17,64,128]{3,2,1,0:T(8,128)}, f32[3,8,128]{2,1,0:T(8,128)S(1)}, f32[8,8,128]{2,1,0:T(8,128)S(1)}) custom-call(s32[4,128]{1,0:T(4,128)S(1)} %concatenate.10.meta.meta_in, f32[8,432,128]{2,1,0:T(8,128)} %copy-done, f32[2,19,64,128]{3,2,1,0:T(8,128)} %copy-done.2), custom_call_target="tpu_custom_call" | custom-call | flops 2000000 | bytes 1048576 | tf_op jit(solution)/shard_map/pallas_call | solution.py:821
  62.4 6.3 %shard_map.63 = (f32[32,128]{1,0:T(8,128)}, f32[2,17,64,128]{3,2,1,0:T(8,128)}, f32[2,17,64,128]{3,2,1,0:T(8,128)}, f32[2,17,64,128]{3,2,1,0:T(8,128)}, f32[3,2,18,8,128]{4,3,2,1,0:T(8,128)}) custom-call(s32[4,128]{1,0:T(4,128)S(1)} %concatenate.10.meta.meta_in, f32[37,8,128]{2,1,0:T(8,128)S(1)} %collective-permute-done.2.strips_in, ...), custom_call_target="tpu_custom_call" | custom-call | flops 2000000 | bytes 1048576 | tf_op jit(solution)/shard_map/pallas_call | solution.py:828
  68.7 7.0 %all-to-all-start.1 = ((f32[32,1,128]{2,1,0:T(1,128)}), f32[32,1,128]{2,1,0:T(1,128)S(1)}, u32[]{:S(2)}, u32[]{:S(2)}) async-start(f32[32,1,128]{2,1,0:T(1,128)} %bitcast.12), calls=%async_computation.1 | async-start | bytes 32768 | tf_op jit(solution)/shard_map/all_to_all | solution.py:773
  75.7 0.0 collective-permute-done.5.rest_3_
  75.8 0.0 collective-permute-done.6.rest_4_
  75.8 0.0 collective-permute-done.7.rest_5_
  75.8 0.0 collective-permute-done.8.rest_6_
  75.8 0.0 collective-permute-done.9.rest_7_
  75.8 7.1 %all-to-all-done.1 = f32[32,1,128]{2,1,0:T(1,128)S(1)} async-done(((f32[32,1,128]{2,1,0:T(1,128)}), f32[32,1,128]{2,1,0:T(1,128)S(1)}, u32[]{:S(2)}, u32[]{:S(2)}) %all-to-all-start.1) | async-done | bytes 16416 | tf_op jit(solution)/shard_map/all_to_all | solution.py:773
  82.9 6.3 %shard_map.64 = (f32[2,16,64,128]{3,2,1,0:T(8,128)}, f32[2,16,64,128]{3,2,1,0:T(8,128)}, f32[4,128]{1,0:T(4,128)}, f32[32,128]{1,0:T(8,128)S(1)}) custom-call(s32[4,128]{1,0:T(4,128)S(1)} %concatenate.10.meta.meta_in, f32[32,128]{1,0:T(8,128)S(1)} %bitcast.22, f32[37,8,128]{2,1,0:T(8,128)} %copy-done.4, f32[2,19,8,128]{3,2,1,0:T(8,128)} %copy-done.3, ...), custom_call_target="tpu_custom_call" | custom-call | flops 2000000 | bytes 1048576 | tf_op jit(solution)/shard_map/pallas_call | solution.py:838
  89.3 8.9 %all_to_all.15 = f32[32,1,128]{2,1,0:T(1,128)S(1)} all-to-all(f32[32,1,128]{2,1,0:T(1,128)S(1)} %bitcast.24), channel_id=1, replica_groups=mesh['zm'=8,'zv'=4] {'zm','zv'}, dimensions={0} | all-to-all | bytes 32768 | tf_op jit(solution)/shard_map/all_to_all | solution.py:773
  98.2 2.8 %shard_map.65 = (f32[16,64,256]{2,1,0:T(8,128)}, f32[4]{0:T(128)}) custom-call(f32[32,128]{1,0:T(8,128)S(1)} %bitcast.23, f32[16,64,256]{2,1,0:T(8,128)} %table_in.1, f32[2,16,64,128]{3,2,1,0:T(8,128)} %get-tuple-element.54.change_in, f32[2,16,64,128]{3,2,1,0:T(8,128)} %get-tuple-element.55.r3_in), custom_call_target="tpu_custom_call" | custom-call | flops 2000000 | bytes 1048576 | tf_op jit(solution)/shard_map/pallas_call | solution.py:849
  (39 shorter events, 0.1 us)
Async XLA Ops:
  4.3 5.4 %copy-start.15 = (f32[4,64,256]{2,1,0:T(8,128)S(1)}, f32[4,64,256]{2,1,0:T(8,128)}, u32[]{:S(2)}) copy-start(f32[4,64,256]{2,1,0:T(8,128)} %get-tuple-element.32) | copy-start | bytes 786436
  4.3 6.7 %copy-start.5 = (s32[4,32,8]{1,2,0:T(8,128)S(1)}, s32[4,32,8]{1,2,0:T(8,128)}, u32[]{:S(2)}) copy-start(s32[4,32,8]{1,2,0:T(8,128)} %param.5) | copy-start | bytes 12292
  4.3 8.8 %slice-start = ((f32[16,64,256]{2,1,0:T(8,128)}), f32[16,8,256]{2,1,0:T(8,128)S(1)}, s32[]{:S(2)}) async-start(f32[16,64,256]{2,1,0:T(8,128)} %table_in.1), calls=%async_computation.3 | async-start | bytes 262144 | tf_op jit(solution)/shard_map/slice | solution.py:799
  4.4 28.4 %all-to-all-start = ((f32[8,432,128]{2,1,0:T(8,128)}), f32[8,432,128]{2,1,0:T(8,128)S(1)}, u32[]{:S(2)}, u32[]{:S(2)}) async-start(f32[8,432,128]{2,1,0:T(8,128)} %get-tuple-element.31), calls=%async_computation | async-start | bytes 3538944 | tf_op jit(solution)/shard_map/all_to_all | solution.py:798
  9.7 3.4 %collective-permute-start = (f32[4,64,256]{2,1,0:T(8,128)S(1)}, f32[4,64,256]{2,1,0:T(8,128)S(1)}, u32[]{:S(2)}, u32[]{:S(2)}) collective-permute-start(f32[4,64,256]{2,1,0:T(8,128)S(1)} %copy-done.15), channel_id=1, source_target_pairs={{4,0},{8,4},{12,8},{16,12},{20,16},{24,20},{28,24},{5,1},{9,5},{13... | collective-permute-start | bytes 786440 | tf_op jit(solution)/shard_map/ppermute | solution.py:778
  13.1 8.2 %copy-start.1 = (f32[16,64,256]{2,1,0:T(8,128)S(1)}, f32[16,64,256]{2,1,0:T(8,128)}, u32[]{:S(2)}) copy-start(f32[16,64,256]{2,1,0:T(8,128)} %table_in.1) | copy-start | bytes 3145732
  13.8 7.5 %collective-permute-start.1 = (f32[20,8,256]{2,1,0:T(8,128)}, f32[20,8,256]{2,1,0:T(8,128)}, u32[]{:S(2)}, u32[]{:S(2)}) collective-permute-start(f32[20,8,256]{2,1,0:T(8,128)} %pad_maximum_fusion), channel_id=1, source_target_pairs={{1,0},{2,1},{3,2},{5,4},{6,5},{7,6},{9,8},{10,9},{11,10},{13,12},{... | collective-permute-start | bytes 491528 | tf_op jit(solution)/shard_map/ppermute | solution.py:778
  18.5 0.6 copy-start.6
  19.2 0.6 copy-start.10
  19.8 13.0 %copy-start.8 = (f32[128,128]{1,0:T(8,128)}, f32[128,128]{1,0:T(8,128)S(1)}, u32[]{:S(2)}) copy-start(f32[128,128]{1,0:T(8,128)S(1)} %get-tuple-element.48) | copy-start | bytes 196612
  19.8 13.0 %copy-start.9 = (f32[128,128]{1,0:T(8,128)}, f32[128,128]{1,0:T(8,128)S(1)}, u32[]{:S(2)}) copy-start(f32[128,128]{1,0:T(8,128)S(1)} %get-tuple-element.47) | copy-start | bytes 196612
  24.3 1.1 %copy-start.2 = (f32[2,19,64,128]{3,2,1,0:T(8,128)}, f32[2,19,64,128]{3,2,1,0:T(8,128)S(1)}, u32[]{:S(2)}) copy-start(f32[2,19,64,128]{3,2,1,0:T(8,128)S(1)} %get-tuple-element.35.interp_in) | copy-start | bytes 3735556
  25.3 37.1 %copy-start.3 = (f32[2,19,8,128]{3,2,1,0:T(8,128)}, f32[2,19,8,128]{3,2,1,0:T(8,128)S(1)}, u32[]{:S(2)}) copy-start(f32[2,19,8,128]{3,2,1,0:T(8,128)S(1)} %get-tuple-element.33.unused_a.interp_halo_in) | copy-start | bytes 466948
  25.3 10.7 %copy-start.11 = (f32[128,128]{1,0:T(8,128)S(1)}, f32[128,128]{1,0:T(8,128)}, u32[]{:S(2)}) copy-start(f32[128,128]{1,0:T(8,128)} %copy-done.10) | copy-start | bytes 196612
  25.3 26.7 %copy-start.7 = (f32[128,128]{1,0:T(8,128)S(1)}, f32[128,128]{1,0:T(8,128)}, u32[]{:S(2)}) copy-start(f32[128,128]{1,0:T(8,128)} %copy-done.6) | copy-start | bytes 196612
  25.3 30.2 %copy-start.17 = (f32[128,128]{1,0:T(8,128)S(1)}, f32[128,128]{1,0:T(8,128)}, u32[]{:S(2)}) copy-start(f32[128,128]{1,0:T(8,128)} %get-tuple-element.51) | copy-start | bytes 196612
  25.3 30.2 %copy-start.16 = (f32[128,128]{1,0:T(8,128)S(1)}, f32[128,128]{1,0:T(8,128)}, u32[]{:S(2)}) copy-start(f32[128,128]{1,0:T(8,128)} %get-tuple-element.52) | copy-start | bytes 196612
  32.8 23.7 %copy-start = (f32[8,432,128]{2,1,0:T(8,128)}, f32[8,432,128]{2,1,0:T(8,128)S(1)}, u32[]{:S(2)}) copy-start(f32[8,432,128]{2,1,0:T(8,128)S(1)} %all-to-all-done.data) | copy-start | bytes 5308420
  34.7 20.8 %collective-permute-start.2 = (f32[37,8,128]{2,1,0:T(8,128)S(1)}, f32[37,8,128]{2,1,0:T(8,128)S(1)}, u32[]{:S(2)}, u32[]{:S(2)}) collective-permute-start(f32[37,8,128]{2,1,0:T(8,128)S(1)} %shard_map.61), channel_id=1, source_target_pairs={{1,0},{2,1},{3,2},{5,4},{6,5},{7,6},{9,8},{10,9},{11,10},{13,12},{... | collective-permute-start | bytes 454664 | tf_op jit(solution)/shard_map/ppermute | solution.py:778
  36.1 16.8 %collective-permute-start.3 = (f32[128,128]{1,0:T(8,128)S(1)}, f32[128,128]{1,0:T(8,128)S(1)}, u32[]{:S(2)}, u32[]{:S(2)}) collective-permute-start(f32[128,128]{1,0:T(8,128)S(1)} %copy-done.11), channel_id=1, source_target_pairs={{0,4},{4,0},{8,12},{12,8},{16,20},{20,16},{24,28},{28,24},{1,5},{5... | collective-permute-start | bytes 196616 | tf_op jit(solution)/shard_map/ppermute | solution.py:807
  50.6 4.9 %collective-permute-start.4 = (f32[128,128]{1,0:T(8,128)}, f32[128,128]{1,0:T(8,128)S(1)}, u32[]{:S(2)}, u32[]{:S(2)}) collective-permute-start(f32[128,128]{1,0:T(8,128)} %copy-done.9), channel_id=1, source_target_pairs={{0,8},{4,12},{8,0},{12,4},{16,24},{20,28},{24,16},{28,20},{1,9},{5... | collective-permute-start | bytes 196616 | tf_op jit(solution)/shard_map/ppermute | solution.py:807
  51.4 24.4 %collective-permute-start.5 = (f32[128,128]{1,0:T(8,128)}, f32[128,128]{1,0:T(8,128)S(1)}, u32[]{:S(2)}, u32[]{:S(2)}) collective-permute-start(f32[128,128]{1,0:T(8,128)} %copy-done.8), channel_id=1, source_target_pairs={{0,12},{4,8},{8,4},{12,0},{16,28},{20,24},{24,20},{28,16},{1,13},{... | collective-permute-start | bytes 196616 | tf_op jit(solution)/shard_map/ppermute | solution.py:807
  52.0 23.8 %collective-permute-start.6 = (f32[128,128]{1,0:T(8,128)S(1)}, f32[128,128]{1,0:T(8,128)S(1)}, u32[]{:S(2)}, u32[]{:S(2)}) collective-permute-start(f32[128,128]{1,0:T(8,128)S(1)} %copy-done.7), channel_id=1, source_target_pairs={{0,16},{4,20},{8,24},{12,28},{16,0},{20,4},{24,8},{28,12},{1,17},{... | collective-permute-start | bytes 196616 | tf_op jit(solution)/shard_map/ppermute | solution.py:807
  52.9 22.9 %collective-permute-start.7 = (f32[128,128]{1,0:T(8,128)S(1)}, f32[128,128]{1,0:T(8,128)S(1)}, u32[]{:S(2)}, u32[]{:S(2)}) collective-permute-start(f32[128,128]{1,0:T(8,128)S(1)} %get-tuple-element.50), channel_id=1, source_target_pairs={{0,20},{4,16},{8,28},{12,24},{16,4},{20,0},{24,12},{28,8},{1,21},{... | collective-permute-start | bytes 196616 | tf_op jit(solution)/shard_map/ppermute | solution.py:807
  55.5 20.3 %collective-permute-start.8 = (f32[128,128]{1,0:T(8,128)S(1)}, f32[128,128]{1,0:T(8,128)S(1)}, u32[]{:S(2)}, u32[]{:S(2)}) collective-permute-start(f32[128,128]{1,0:T(8,128)S(1)} %copy-done.17), channel_id=1, source_target_pairs={{0,24},{4,28},{8,16},{12,20},{16,8},{20,12},{24,0},{28,4},{1,25},{... | collective-permute-start | bytes 196616 | tf_op jit(solution)/shard_map/ppermute | solution.py:807
  55.5 6.9 %copy-start.4 = (f32[37,8,128]{2,1,0:T(8,128)}, f32[37,8,128]{2,1,0:T(8,128)S(1)}, u32[]{:S(2)}) copy-start(f32[37,8,128]{2,1,0:T(8,128)S(1)} %collective-permute-done.2.strips_in) | copy-start | bytes 454660
  55.6 20.3 %collective-permute-start.9 = (f32[128,128]{1,0:T(8,128)S(1)}, f32[128,128]{1,0:T(8,128)S(1)}, u32[]{:S(2)}, u32[]{:S(2)}) collective-permute-start(f32[128,128]{1,0:T(8,128)S(1)} %copy-done.16), channel_id=1, source_target_pairs={{0,28},{4,24},{8,20},{12,16},{16,12},{20,8},{24,4},{28,0},{1,29},{... | collective-permute-start | bytes 196616 | tf_op jit(solution)/shard_map/ppermute | solution.py:807
  68.7 14.2 %all-to-all-start.1 = ((f32[32,1,128]{2,1,0:T(1,128)}), f32[32,1,128]{2,1,0:T(1,128)S(1)}, u32[]{:S(2)}, u32[]{:S(2)}) async-start(f32[32,1,128]{2,1,0:T(1,128)} %bitcast.12), calls=%async_computation.1 | async-start | bytes 32768 | tf_op jit(solution)/shard_map/all_to_all | solution.py:773
  75.8 7.2 %copy-start.12 = (f32[128,128]{1,0:T(8,128)}, f32[128,128]{1,0:T(8,128)S(1)}, u32[]{:S(2)}) copy-start(f32[128,128]{1,0:T(8,128)S(1)} %collective-permute-done.7.rest_5_) | copy-start | bytes 196612
  75.8 7.1 %copy-start.13 = (f32[128,128]{1,0:T(8,128)}, f32[128,128]{1,0:T(8,128)S(1)}, u32[]{:S(2)}) copy-start(f32[128,128]{1,0:T(8,128)S(1)} %collective-permute-done.8.rest_6_) | copy-start | bytes 196612
  75.8 7.1 %copy-start.14 = (f32[128,128]{1,0:T(8,128)}, f32[128,128]{1,0:T(8,128)S(1)}, u32[]{:S(2)}) copy-start(f32[128,128]{1,0:T(8,128)S(1)} %collective-permute-done.9.rest_7_) | copy-start | bytes 196612

commit v3 on v2

--- a/solution.py
+++ b/solution.py
@@ -99,16 +99,18 @@
                 inverse[t, block // (g.blocks * g.zv)] = slot
 
 
-def pack_three_body(g, assign, refined, table, out, top, inverse, held, extras, rows_held, sems, out_sems):
+def pack_three_body(g, assign_in, refined, table, out, top, assign, inverse, held, extras, rows_held, sems, out_sems):
     three = range(ITERS - 1)
     reads = [
         pltpu.make_async_copy(refined.at[i], held.at[i], sems.at[i]) for i in range(3 * g.slots)
     ]
     rows_in = pltpu.make_async_copy(table.at[0:ITERS], rows_held, sems.at[3 * g.slots])
     rows_out = pltpu.make_async_copy(rows_held, top, out_sems.at[3 * g.zm + 3])
-    rows_in.start()
+    numbers = fetch(assign_in, assign, sems.at[3 * g.slots + 1])
     for read in reads:
         read.start()
+    rows_in.start()
+    numbers.wait()
     fill_inverse(g, three, assign, inverse)
     rows_in.wait()
     rows_out.start()
@@ -342,14 +344,19 @@
     return result
 
 
-def convert(g, meta, t, held, offset, z, out, left):
-    row = offset + z // 8 * 8 * PAIRS + z % 8
+def fill_first_rows(g, meta, iterations, rows, first_rows):
+    for t in iterations:
+        for block in range(g.blocks):
+            first_rows[t, block] = jnp.maximum(meta[t, block], 0) * rows + (OFFSET[t] if t < ITERS - 1 else 0)
+
+
+def convert(g, first_rows, t, held, z, out, left):
+    row = z // 8 * 8 * PAIRS + z % 8
     for pair in range(g.pairs):
         vb, col = pair // g.ct, pair % g.ct
         tiles = []
         for half in range(2):
-            owner = jnp.maximum(meta[t, vb * g.cb + 2 * col + half], 0)
-            tiles.append(held[owner, pl.ds(row, PAIRS, stride=8), :])
+            tiles.append(held[pl.ds(first_rows[t, vb * g.cb + 2 * col + half] + row, PAIRS, stride=8), :])
         even, odd = pair_tiles(left, *tiles)
         out[col, z, pl.ds(vb * BLOCK_V, PAIRS, stride=2), :] = even
         out[col, z, pl.ds(vb * BLOCK_V + 1, PAIRS, stride=2), :] = odd
@@ -364,25 +371,26 @@
 
 
 def local_body(g, meta_in, data, interp_in, a0_out, a1_out, a2_out, totals_out, peaks_out,
-               meta, totals, peaks, held, interp, f0, f1, f2, a0, a1, a2, masks, sems, out_sems):
-    meta_copy = fetch(meta_in, meta, sems.at[6 + 2 * g.ct])
+               meta, first_rows, totals, peaks, arrived, interp, f0, f1, f2, a0, a1, a2, masks, sems, out_sems):
+    meta_copy = fetch(meta_in, meta, sems.at[8])
+    held = arrived.reshape(g.zm * OFFSET[3], LANES)
     f, a, outs = (f0, f1, f2), (a0, a1, a2), (a0_out, a1_out, a2_out)
     split = BLOCK_Z // 2
     groups = ([], [])
     for t in range(3):
         first, middle, end = OFFSET[t], OFFSET[t] + ROWS // 2, OFFSET[t + 1]
         for group, rows in ((0, slice(middle, end)), (1, slice(first, middle))):
-            groups[group].append(pltpu.make_async_copy(data.at[:, rows, :], held.at[:, rows, :], sems.at[2 * t + group]))
-    for col in range(g.ct):
-        for group, layers in ((0, slice(split, LAYERS[0])), (1, slice(0, split))):
-            sem = sems.at[6 + 2 * col + group]
-            groups[group].append(pltpu.make_async_copy(interp_in.at[col, layers], interp.at[col, layers], sem))
+            copy = pltpu.make_async_copy(data.at[:, rows, :], arrived.at[:, rows, :], sems.at[2 * t + group])
+            groups[group].append(copy)
+    for group, layers in ((0, slice(split, LAYERS[0])), (1, slice(0, split))):
+        groups[group].append(pltpu.make_async_copy(interp_in.at[:, layers], interp.at[:, layers], sems.at[6 + group]))
     for group in groups:
         for copy in group:
             copy.start()
     left = lane_ids() < HALF
     peaks[...] = jnp.zeros_like(peaks)
     meta_copy.wait()
+    fill_first_rows(g, meta, range(3), OFFSET[3], first_rows)
     fill_masks(g, meta, masks, (0, 1, 2), left)
     for copy in groups[0]:
         copy.wait()
@@ -393,10 +401,10 @@
         row = pl.multiple_of(vb * BLOCK_V, BLOCK_V)
         column = g.blocks + vb * g.cb + 2 * col
         for t in range(3):
-            owners = [jnp.maximum(meta[t, column + half], 0) for half in range(2)]
+            starts = [jnp.maximum(meta[t, column + half], 0) * OFFSET[3] for half in range(2)]
             for z in range(BLOCK_Z, LAYERS[t]):
-                at = OFFSET[t] + z * PAIRS
-                even, odd = pair_tiles(left, *[held[owner, at : at + PAIRS, :] for owner in owners])
+                at = [pl.multiple_of(start + OFFSET[t] + z * PAIRS, PAIRS) for start in starts]
+                even, odd = pair_tiles(left, *[held[pl.ds(row_at, PAIRS), :] for row_at in at])
                 f[t][col, z, pl.ds(row, PAIRS, stride=2), :] = even
                 f[t][col, z, pl.ds(row + 1, PAIRS, stride=2), :] = odd
         for t in range(3):
@@ -427,12 +435,12 @@
             peaks[pair] = peak
         at = clip(base, BLOCK_Z - 1)
         for t in range(3):
-            convert(g, meta, t, held, OFFSET[t], at, f[t], left)
+            convert(g, first_rows, t, held, at, f[t], left)
         return tuple(carry)
 
     carry = (jnp.zeros(TILE, F32),) * 3
-    writes, bounds = [], (0, split, split + 5, BLOCK_Z + 1)
-    for index in range(3):
+    writes, bounds = [], (0, split, split + 4, BLOCK_Z - 1, BLOCK_Z + 1)
+    for index in range(4):
         if index == 1:
             for copy in groups[1]:
                 copy.wait()
@@ -440,34 +448,30 @@
         lowest = BLOCK_Z - bounds[index + 1] + 1
         for t in range(3):
             highest = BLOCK_Z - bounds[index] if index else LAYERS[t] - 1
-            for col in range(g.ct):
-                span = slice(lowest, highest + 1)
-                sem = out_sems.at[(index * 3 + t) * g.ct + col]
-                writes.append(pltpu.make_async_copy(a[t].at[col, span], outs[t].at[col, span], sem))
-                writes[-1].start()
+            span = slice(lowest, highest + 1)
+            writes.append(fetch(a[t].at[:, span], outs[t].at[:, span], out_sems.at[index * 3 + t]))
     for t in range(3):
         totals[t] = carry[t]
-    writes.append(fetch(totals, totals_out, out_sems.at[9 * g.ct]))
-    writes.append(fetch(peaks, peaks_out, out_sems.at[9 * g.ct + 1]))
+    writes.append(fetch(totals, totals_out, out_sems.at[12]))
+    writes.append(fetch(peaks, peaks_out, out_sems.at[13]))
     for write in writes:
         write.wait()
 
 
 def middle_body(g, meta_in, strips_in, interp_halo_in, totals_in, a0_in, a1_in, a2_in,
-                out_hbm, ca0_out, ca1_out, cb1_out, halos_out,
-                meta, strips, interp_halo, totals, out, halos, a0, a1, a2, b1, ca0, ca1, cb1, a0_halo, a1_halo, b1_halo, masks, sems, out_sems):
-    split = BLOCK_Z // 2
-    groups, at = ([], []), 6 * g.ct
+                out, ca0_out, ca1_out, cb1_out, halos_out,
+                meta, strips, interp_halo, totals, halos, a0, a1, a2, b1, ca0, ca1, cb1, a0_halo, a1_halo, b1_halo, masks, sems, out_sems):
+    cuts = (12, 6, 0)
+    groups, at = ([], [], []), 9
     small = []
     for source, target in ((meta_in, meta), (strips_in, strips), (interp_halo_in, interp_halo), (totals_in, totals)):
         small.append(fetch(source, target, sems.at[at]))
         at += 1
     at = 0
     for source, target, layers in ((a0_in, a0, LAYERS[0]), (a1_in, a1, LAYERS[1]), (a2_in, a2, BLOCK_Z)):
-        for col in range(g.ct):
-            for group, span in ((0, slice(split, layers)), (1, slice(0, split))):
-                groups[group].append(pltpu.make_async_copy(source.at[col, span], target.at[col, span], sems.at[at]))
-                at += 1
+        for group, span in enumerate((slice(cuts[0], layers), slice(cuts[1], cuts[0]), slice(0, cuts[1]))):
+            groups[group].append(pltpu.make_async_copy(source.at[:, span], target.at[:, span], sems.at[at]))
+            at += 1
     for group in groups:
         for copy in group:
             copy.start()
@@ -539,24 +543,20 @@
 
     carry = (jnp.zeros(TILE, F32),) * 11
     writes = []
-    bounds = (0, top0 - split + 1, top0 - split + 6, top0 + 2)
-    for index in range(3):
-        if index == 1:
-            for copy in groups[1]:
+    bounds = (0, top0 - cuts[0] + 1, top0 - cuts[1] + 1, top0, top0 + 2)
+    for index in range(4):
+        if index in (1, 2):
+            for copy in groups[index]:
                 copy.wait()
         carry = lax.fori_loop(bounds[index], bounds[index + 1], step, carry)
         lowest = top0 - bounds[index + 1] + 2
         highest = top0 - bounds[index] + 1 if index else top1
         for which, (source, target) in enumerate(((ca0, ca0_out), (ca1, ca1_out), (cb1, cb1_out))):
-            for col in range(g.ct):
-                span = slice(lowest, highest + 1)
-                sem = out_sems.at[(index * 3 + which) * g.ct + col]
-                writes.append(pltpu.make_async_copy(source.at[col, span], target.at[col, span], sem))
-                writes[-1].start()
-    writes.append(fetch(halos, halos_out, out_sems.at[9 * g.ct]))
+            span = slice(lowest, highest + 1)
+            writes.append(fetch(source.at[:, span], target.at[:, span], out_sems.at[index * 3 + which]))
+    writes.append(fetch(halos, halos_out, out_sems.at[12]))
     values = [totals[0], totals[1], carry[0], carry[1], totals[2]] + list(carry[2:])
     out[...] = spread_rows(values, out.shape[0])
-    writes.append(fetch(out, out_hbm, out_sems.at[9 * g.ct + 1]))
     for write in writes:
         write.wait()
 
@@ -591,27 +591,26 @@
               *rest):
     data, rest = rest[: g.zm], rest[g.zm :]
     (sum_hbm, r3_hbm, errors_out, out,
-     meta, strips, interp_halo, halos_in, peaks0, errors, held, f3, a0, a1, a2, interp, ca0, ca1, cb1, r2, r2_halo, change, sum_out, r3, masks, peaks, sems, out_sems) = rest
+     meta, first_rows, strips, interp_halo, halos_in, peaks0, errors, held, f3, a0, a1, a2, interp, ca0, ca1, cb1, r2, r2_halo, change, sum_out, r3, masks, peaks, sems, out_sems) = rest
     top = LAYERS[2] - 1
     small = []
     for source, target in ((meta_in, meta), (strips_in, strips), (interp_halo_in, interp_halo), (halos_hbm, halos_in),
                            (peaks0_in, peaks0)):
-        small.append(fetch(source, target, sems.at[g.zm + 28 * g.ct + len(small)]))
-    chunks = segments(top, (5, 4, 4, 4))
+        small.append(fetch(source, target, sems.at[g.zm + 28 + len(small)]))
+    chunks = segments(top, (3, 5, 5, 4))
     reads, at = [], 0
     for lowest, highest in chunks:
         group = []
         if not reads:
             for k in range(g.zm):
-                group.append(pltpu.make_async_copy(data[k], held.at[k], sems.at[at]))
+                group.append(pltpu.make_async_copy(data[k], held.at[k * ROWS : (k + 1) * ROWS, :], sems.at[at]))
                 at += 1
         for source, target, layers in ((ca0_in, ca0, BLOCK_Z + 1), (ca1_in, ca1, BLOCK_Z + 1), (cb1_in, cb1, BLOCK_Z + 1),
                                        (a0_in, a0, BLOCK_Z), (a1_in, a1, BLOCK_Z), (a2_in, a2, BLOCK_Z + 1),
                                        (interp_in, interp, BLOCK_Z)):
-            for col in range(g.ct):
-                span = slice(lowest, min(highest + 1, layers))
-                group.append(pltpu.make_async_copy(source.at[col, span], target.at[col, span], sems.at[at]))
-                at += 1
+            span = slice(lowest, min(highest + 1, layers))
+            group.append(pltpu.make_async_copy(source.at[:, span], target.at[:, span], sems.at[at]))
+            at += 1
         reads.append(group)
     for group in reads:
         for copy in group:
@@ -623,6 +622,7 @@
     stencil = Stencil(g, edge_v)
     left = lane_ids() < HALF
     fill_masks(g, meta, masks, (1, 2, 3), left)
+    fill_first_rows(g, meta, [ITERS - 1], ROWS, first_rows)
     w0, w1, w2 = three_weights(g, meta, parts)
     w01 = w0 * w1
     live = halo_live(g, meta, 2, left)
@@ -669,7 +669,7 @@
                 sum_out[col, own, rows, :] = w0 * a0[col, own, rows, :] + w1 * one + w2 * value
             peaks[0, pair] = peak1
             peaks[1, pair] = peak2
-        convert(g, meta, ITERS - 1, held, 0, own, f3, left)
+        convert(g, first_rows, ITERS - 1, held, own, f3, left)
         return total
 
     total, start, writes = jnp.zeros(TILE, F32), 0, []
@@ -684,10 +684,7 @@
         for which, (source, target, layers) in enumerate(
             ((sum_out, sum_hbm, slice(lowest, min(highest, BLOCK_Z - 1) + 1)), (r3, r3_hbm, slice(below, above + 1)))
         ):
-            for col in range(g.ct):
-                sem = out_sems.at[(index * 2 + which) * g.ct + col]
-                writes.append(pltpu.make_async_copy(source.at[col, layers], target.at[col, layers], sem))
-                writes[-1].start()
+            writes.append(fetch(source.at[:, layers], target.at[:, layers], out_sems.at[index * 2 + which]))
 
     line = spread_rows([total], 1)
     lane = lax.broadcasted_iota(jnp.int32, (1, 128), 1)
@@ -704,7 +701,7 @@
             found = found + jnp.sum(jnp.where(lane_p == place, column, 0.0), axis=0, keepdims=True)
         errors[i : i + 1, :] = found
         line = jnp.where(lane == 1 + i, jnp.max(found, axis=1, keepdims=True), line)
-    writes.append(fetch(errors, errors_out, out_sems.at[8 * g.ct]))
+    writes.append(fetch(errors, errors_out, out_sems.at[8]))
     line = jnp.where(lane == 1 + ITERS, live_cells(g, meta, ITERS - 1), line)
     out[...] = jnp.broadcast_to(line, out.shape)
     for write in writes:
@@ -716,12 +713,9 @@
     spans = [slice(part * quarter, (part + 1) * quarter) for part in range(4)]
     reads = []
     for part, span in enumerate(spans):
-        at = part * (1 + 2 * g.ct)
-        group = [pltpu.make_async_copy(table_in.at[span], table.at[span], sems.at[at])]
-        for col in range(g.ct):
-            at += 2
-            group.append(pltpu.make_async_copy(change_in.at[col, span], change.at[col, span], sems.at[at - 1]))
-            group.append(pltpu.make_async_copy(r3_in.at[col, span], r3.at[col, span], sems.at[at]))
+        group = [pltpu.make_async_copy(table_in.at[span], table.at[span], sems.at[3 * part])]
+        for i, (source, target) in enumerate(((change_in, change), (r3_in, r3))):
+            group.append(pltpu.make_async_copy(source.at[:, span], target.at[:, span], sems.at[3 * part + 1 + i]))
         reads.append(group)
     for group in reads:
         for read in group:
@@ -789,9 +783,9 @@
     main, halo = g.main, g.halo
 
     packed, top = call(
-        part(pack_three_body, g), [struct(g.zm, OFFSET[3], LANES), struct(ITERS, *table.shape[1:])], [SMEM, HBM, HBM], [HBM] * 2,
-        [pltpu.SMEM((ITERS, g.zm), jnp.int32), vmem(3 * g.slots, ROWS, LANES), vmem(g.zm, OFFSET[3] - 3 * ROWS, LANES),
-         vmem(ITERS, *table.shape[1:]), dma(3 * g.slots + 1), dma(3 * g.zm + 4)],
+        part(pack_three_body, g), [struct(g.zm, OFFSET[3], LANES), struct(ITERS, *table.shape[1:])], [HBM] * 3, [HBM] * 2,
+        [pltpu.SMEM(slots.shape, jnp.int32), pltpu.SMEM((ITERS, g.zm), jnp.int32), vmem(3 * g.slots, ROWS, LANES), vmem(g.zm, OFFSET[3] - 3 * ROWS, LANES),
+         vmem(ITERS, *table.shape[1:]), dma(3 * g.slots + 2), dma(3 * g.zm + 4)],
         60,
     )(slots, views, table)
     below = from_next(top, "zm")
@@ -821,35 +815,37 @@
     a0, a1, a2, totals, peaks0 = call(
         part(local_body, g), [struct(*main(LAYERS[0])), most, more, struct(3, *TILE), struct(g.pairs, *TILE)],
         [HBM] * 3, [HBM] * 5,
-        [pltpu.SMEM(meta.shape, jnp.int32), vmem(3, *TILE), vmem(g.pairs, *TILE), vmem(*data.shape)]
+        [pltpu.SMEM(meta.shape, jnp.int32), pltpu.SMEM((ITERS, g.blocks), jnp.int32), vmem(3, *TILE),
+         vmem(g.pairs, *TILE), vmem(*data.shape)]
         + [vmem(*main(LAYERS[0]))] * 7
-        + [vmem(3, 2, g.pairs, *TILE), dma(7 + 2 * g.ct), dma(9 * g.ct + 2)], WHOLE,
+        + [vmem(3, 2, g.pairs, *TILE), dma(9), dma(14)], WHOLE,
     )(meta, data, interp)
     products, ca0, ca1, cb1, halos = call(
         part(middle_body, g), [struct(everyone, 128), more, more, more, struct(3, *halo(LAYERS[1]))],
-        [HBM] * 7, [HBM] * 5,
+        [HBM] * 7, [VMEM] + [HBM] * 4,
         [pltpu.SMEM(meta.shape, jnp.int32), vmem(*strips.shape), vmem(*interp_halo.shape), vmem(3, *TILE),
-         vmem(everyone, 128), vmem(3, *halo(LAYERS[1]))]
+         vmem(3, *halo(LAYERS[1]))]
         + [vmem(*main(LAYERS[0] + 1))] * 7 + [vmem(*halo(LAYERS[0] + 1))] * 3
-        + [vmem(2, 2, g.pairs, *TILE), dma(6 * g.ct + 4), dma(9 * g.ct + 2)],
+        + [vmem(2, 2, g.pairs, *TILE), dma(13), dma(13)],
         WHOLE,
     )(meta, strips, interp_halo, totals, a0, a1, a2)
+    products, *last_data = lax.optimization_barrier((products, *last_data))
     products = to_all(products)
     change, r3, errors, stats = call(
         part(last_body, g), [own, own, struct(ITERS, 128), struct(everyone, 128)],
         [HBM, VMEM] + [HBM] * (11 + g.zm), [HBM] * 3 + [VMEM],
-        [pltpu.SMEM(meta.shape, jnp.int32), vmem(*strips.shape), vmem(*interp_halo.shape), vmem(*halos.shape),
-         vmem(*peaks0.shape), vmem(ITERS, 128), vmem(g.zm, ROWS, LANES)] + [vmem(*main(BLOCK_Z))] * 3 + [vmem(*main(LAYERS[2])), vmem(*main(BLOCK_Z))]
+        [pltpu.SMEM(meta.shape, jnp.int32), pltpu.SMEM((ITERS, g.blocks), jnp.int32), vmem(*strips.shape),
+         vmem(*interp_halo.shape), vmem(*halos.shape), vmem(*peaks0.shape), vmem(ITERS, 128), vmem(g.zm * ROWS, LANES)] + [vmem(*main(BLOCK_Z))] * 3 + [vmem(*main(LAYERS[2])), vmem(*main(BLOCK_Z))]
         + [vmem(*main(LAYERS[2]))] * 4 + [vmem(*halo(LAYERS[2])), vmem(*main(LAYERS[2]))]
         + [vmem(*main(BLOCK_Z))] * 2
-        + [vmem(3, 2, g.pairs, *TILE), vmem(3, g.pairs, *TILE), dma(g.zm + 28 * g.ct + 5), dma(8 * g.ct + 1)],
+        + [vmem(3, 2, g.pairs, *TILE), vmem(3, g.pairs, *TILE), dma(g.zm + 33), dma(9)],
         WHOLE,
     )(meta, products, strips, interp_halo, halos, peaks0, a0, a1, a2, interp, ca0, ca1, cb1, *last_data)
     stats = to_all(stats)
     table_out, worst = call(
         part(finish_body, g), [struct(*table.shape), struct(ITERS)], [VMEM] + [HBM] * 3, [HBM] * 2,
         [vmem(*table.shape)] + [vmem(*main(BLOCK_Z))] * 2
-        + [vmem(*table.shape), pltpu.SMEM((ITERS,), F32), dma(4 * (1 + 2 * g.ct)), dma(5)],
+        + [vmem(*table.shape), pltpu.SMEM((ITERS,), F32), dma(12), dma(5)],
         WHOLE,
     )(stats, table, change, r3)
     return (table_out, errors[:, : g.blocks], worst)

time: 102 us -> 99.5 us (0.975)
  blocking collectives: 8.89 us -> 22.9 us
  waiting for transfers between devices: 19.4 us -> 12.3 us
  starting transfers between devices: 35.1 us -> 28.2 us
  Pallas kernels: 32.5 us -> 30.7 us
    all_to_all x1 -> x2, blocking collectives: 8.89 us -> 22.9 us  [to_all(): lax.all_to_all(rows.reshape(count, 1, 128), AXES, 0, 0, tiled=True)]
    all_to_all x1 -> x0, waiting for transfers between devices: 7.11 us -> none  [to_all(): lax.all_to_all(rows.reshape(count, 1, 128), AXES, 0, 0, tiled=True)]
    all_to_all x1 -> x0, starting transfers between devices: 7.01 us -> none  [to_all(): lax.all_to_all(rows.reshape(count, 1, 128), AXES, 0, 0, tiled=True)]
  transfers between devices with their start and end apart: 12 -> 11, of which waited for: 5 -> 4; matrix products, arithmetic and copies ran while one was open for 2% -> 2% of each run, Pallas kernels for 18% -> 17%
where the time goes in v3:
time: 99.5 us; the launch traced here: 99 us
  Pallas kernels  30.7 us (31%)
  starting transfers between devices  28.2 us (28%)
  blocking collectives  22.9 us (23%)
  waiting for transfers between devices  12.3 us (12%)
  local copies, waits for them, and re-layouts  2.77 us (3%)
  other arithmetic  1.25 us (1%)
    all_to_all x2, blocking collectives, to_all(): lax.all_to_all(rows.reshape(count, 1, 128), AXES, 0, 0, tiled=True)  22.9 us
    ppermute x7, starting transfers between devices, shards(): lax.ppermute(packed[k], 'zm', [(i, i ^ k) for i in range(g.zm)])  18.9 us
    all_to_all x1, waiting for transfers between devices, shards(): data = lax.all_to_all(packed, 'zm', 0, 0, tiled=True)  7.46 us
    pallas_call x1, Pallas kernels, shards(): call(part(last_body, g), [own, own, struct(ITERS, 128), struct(everyone,...  5.95 us
    pallas_call x1, Pallas kernels, shards(): call(part(middle_body, g), [struct(everyone, 128), more, more, more, stru...  5.85 us
    pallas_call x1, Pallas kernels, shards(): call(part(local_body, g), [struct(*main(LAYERS[0])), most, more, struct(3...  5.36 us
    all_to_all x1, starting transfers between devices, shards(): data = lax.all_to_all(packed, 'zm', 0, 0, tiled=True)  5.34 us
    ppermute x3, starting transfers between devices, from_next(): return lax.ppermute(value, axis, [(i, i - 1) for i in range(1, count)])  3.86 us
  transfers between devices with their start and end apart: 11, of which 4 were waited for; matrix products, arithmetic and copies ran while one was open for 2% of the time, Pallas kernels for 17%

profile of v3, /device:TPU:0, one launch (start us, length us, event | category | flops | bytes accessed | tf_op | source)
XLA Modules:
  0.0 99.0 jit_solution(2269712994449909699)
XLA Ops:
  0.6 3.3 %shard_map.58 = (f32[8,432,128]{2,1,0:T(8,128)}, f32[4,64,256]{2,1,0:T(8,128)}) custom-call(s32[32,32]{1,0:T(8,128)} %bitcast.20, f32[32,128,128]{2,1,0:T(8,128)} %bitcast.26, f32[16,64,256]{2,1,0:T(8,128)} %table_in.1), custom_call_target="tpu_custom_call" | custom-call | flops 2000000 | bytes 1048576 | tf_op jit(solution)/shard_map/pallas_call | solution.py:785
  3.9 0.0 copy-start.15
  3.9 0.0 copy-start.5
  4.0 0.0 slice-start
  4.0 5.3 %all-to-all-start = ((f32[8,432,128]{2,1,0:T(8,128)}), f32[8,432,128]{2,1,0:T(8,128)S(1)}, u32[]{:S(2)}, u32[]{:S(2)}) async-start(f32[8,432,128]{2,1,0:T(8,128)} %get-tuple-element.40), calls=%async_computation | async-start | bytes 3538944 | tf_op jit(solution)/shard_map/all_to_all | solution.py:792
  9.3 1.3 %collective-permute-start = (f32[4,64,256]{2,1,0:T(8,128)S(1)}, f32[4,64,256]{2,1,0:T(8,128)S(1)}, u32[]{:S(2)}, u32[]{:S(2)}) collective-permute-start(f32[4,64,256]{2,1,0:T(8,128)S(1)} %copy-done.15), channel_id=1, source_target_pairs={{4,0},{8,4},{12,8},{16,12},{20,16},{24,20},{28,24},{5,1},{9,5},{13... | collective-permute-start | bytes 786440 | tf_op jit(solution)/shard_map/ppermute | solution.py:772
  10.7 0.0 copy-done.5
  10.7 0.2 convert_reduce_fusion
  10.9 0.1 broadcast_select_fusion
  10.9 1.8 %collective-permute-done.below = f32[4,64,256]{2,1,0:T(8,128)S(1)} collective-permute-done((f32[4,64,256]{2,1,0:T(8,128)S(1)}, f32[4,64,256]{2,1,0:T(8,128)S(1)}, u32[]{:S(2)}, u32[]{:S(2)}) %collective-permute-start) | collective-permute-done | bytes 262176 | tf_op jit(solution)/shard_map/ppermute | solution.py:772
  12.8 0.7 pad_maximum_fusion
  13.4 1.3 %collective-permute-start.1 = (f32[20,8,256]{2,1,0:T(8,128)}, f32[20,8,256]{2,1,0:T(8,128)}, u32[]{:S(2)}, u32[]{:S(2)}) collective-permute-start(f32[20,8,256]{2,1,0:T(8,128)} %pad_maximum_fusion), channel_id=1, source_target_pairs={{1,0},{2,1},{3,2},{5,4},{6,5},{7,6},{9,8},{10,9},{11,10},{13,12},{... | collective-permute-start | bytes 491528 | tf_op jit(solution)/shard_map/ppermute | solution.py:772
  14.7 0.1 add_convert_fusion
  14.8 0.1 copy.13
  14.9 0.1 copy.14
  15.0 0.1 eq.32
  15.1 0.2 select_reduce_fusion
  15.3 0.1 concatenate.10.meta.meta_in
  15.4 2.7 %shard_map.60 = (f32[128,128]{1,0:T(8,128)S(1)}, f32[128,128]{1,0:T(8,128)S(1)}, f32[128,128]{1,0:T(8,128)S(1)}, f32[128,128]{1,0:T(8,128)S(1)}, f32[128,128]{1,...) custom-call(s32[32,32]{1,0:T(8,128)S(1)} %bitcast.21, f32[32,128,128]{2,1,0:T(8,128)} %bitcast.27), custom_call_target="tpu_custom_call" | custom-call | flops 2000000 | bytes 1048576 | tf_op jit(solution)/shard_map/pallas_call | solution.py:795
  18.2 0.6 copy-done.6
  18.8 0.6 copy-done.10
  19.4 1.5 %collective-permute-done.1.strip = f32[20,8,256]{2,1,0:T(8,128)} collective-permute-done((f32[20,8,256]{2,1,0:T(8,128)}, f32[20,8,256]{2,1,0:T(8,128)}, u32[]{:S(2)}, u32[]{:S(2)}) %collective-permute-start.1) | collective-permute-done | bytes 163872 | tf_op jit(solution)/shard_map/ppermute | solution.py:772
  21.0 2.9 %shard_map.59 = (f32[2,19,64,128]{3,2,1,0:T(8,128)S(1)}, f32[2,19,8,128]{3,2,1,0:T(8,128)S(1)}) custom-call(s32[4,128]{1,0:T(4,128)S(1)} %concatenate.10.meta.meta_in, f32[16,64,256]{2,1,0:T(8,128)S(1)} %copy-done.1, f32[4,64,256]{2,1,0:T(8,128)S(1)} %collective-permute-done.below, f32[20,8,256]{2,1,0:T(8,128)} %collective-permute-done.1.strip), custom_call_target="tpu_custom_call" | custom-call | flops 2000000 | bytes 1048576 | tf_op jit(solution)/shard_map/pallas_call | solution.py:803
  23.9 1.1 %copy-done.2 = f32[2,19,64,128]{3,2,1,0:T(8,128)} copy-done((f32[2,19,64,128]{3,2,1,0:T(8,128)}, f32[2,19,64,128]{3,2,1,0:T(8,128)S(1)}, u32[]{:S(2)}) %copy-start.2) | copy-done | bytes 1245208
  25.0 7.5 %all-to-all-done.data = f32[8,432,128]{2,1,0:T(8,128)S(1)} async-done(((f32[8,432,128]{2,1,0:T(8,128)}), f32[8,432,128]{2,1,0:T(8,128)S(1)}, u32[]{:S(2)}, u32[]{:S(2)}) %all-to-all-start) | async-done | bytes 1769504 | tf_op jit(solution)/shard_map/all_to_all | solution.py:792
  32.4 1.9 %shard_map.61 = f32[37,8,128]{2,1,0:T(8,128)S(1)} custom-call(s32[4,128]{1,0:T(4,128)S(1)} %concatenate.10.meta.meta_in, f32[8,432,128]{2,1,0:T(8,128)S(1)} %all-to-all-done.data, f32[2,19,8,128]{3,2,1,0:T(8,128)S(1)} %get-tuple-element.42.unused_a.interp_halo_in, f32[128,128]{1,0:T(8,128)S(1)} %get-tuple-element.63.unused_b.rest_0_), custom_call_target="tpu_custom_call" | custom-call | flops 2000000 | bytes 1048576 | tf_op jit(solution)/shard_map/pallas_call | solution.py:808
  34.4 1.3 %collective-permute-start.2 = (f32[37,8,128]{2,1,0:T(8,128)S(1)}, f32[37,8,128]{2,1,0:T(8,128)S(1)}, u32[]{:S(2)}, u32[]{:S(2)}) collective-permute-start(f32[37,8,128]{2,1,0:T(8,128)S(1)} %shard_map.61), channel_id=1, source_target_pairs={{1,0},{2,1},{3,2},{5,4},{6,5},{7,6},{9,8},{10,9},{11,10},{13,12},{... | collective-permute-start | bytes 454664 | tf_op jit(solution)/shard_map/ppermute | solution.py:772
  35.7 14.5 %collective-permute-start.3 = (f32[128,128]{1,0:T(8,128)S(1)}, f32[128,128]{1,0:T(8,128)S(1)}, u32[]{:S(2)}, u32[]{:S(2)}) collective-permute-start(f32[128,128]{1,0:T(8,128)S(1)} %copy-done.11), channel_id=1, source_target_pairs={{0,4},{4,0},{8,12},{12,8},{16,20},{20,16},{24,28},{28,24},{1,5},{5... | collective-permute-start | bytes 196616 | tf_op jit(solution)/shard_map/ppermute | solution.py:801
  50.2 0.8 collective-permute-start.4
  51.0 0.6 collective-permute-start.5
  51.6 0.8 collective-permute-start.6
  52.5 0.0 collective-permute-done.3.rest_1_
  52.5 1.2 %collective-permute-start.7 = (f32[128,128]{1,0:T(8,128)S(1)}, f32[128,128]{1,0:T(8,128)S(1)}, u32[]{:S(2)}, u32[]{:S(2)}) collective-permute-start(f32[128,128]{1,0:T(8,128)S(1)} %get-tuple-element.54), channel_id=1, source_target_pairs={{0,20},{4,16},{8,28},{12,24},{16,4},{20,0},{24,12},{28,8},{1,21},{... | collective-permute-start | bytes 196616 | tf_op jit(solution)/shard_map/ppermute | solution.py:801
  53.7 1.4 %collective-permute-done.4.rest_2_ = f32[128,128]{1,0:T(8,128)S(1)} collective-permute-done((f32[128,128]{1,0:T(8,128)}, f32[128,128]{1,0:T(8,128)S(1)}, u32[]{:S(2)}, u32[]{:S(2)}) %collective-permute-start.4) | collective-permute-done | bytes 65568 | tf_op jit(solution)/shard_map/ppermute | solution.py:801
  55.1 0.0 collective-permute-start.8
  55.2 0.0 collective-permute-done.2.strips_in
  55.2 0.9 collective-permute-start.9
  56.1 5.4 %shard_map.62 = (f32[2,19,64,128]{3,2,1,0:T(8,128)}, f32[2,18,64,128]{3,2,1,0:T(8,128)}, f32[2,17,64,128]{3,2,1,0:T(8,128)}, f32[3,8,128]{2,1,0:T(8,128)S(1)}, f32[8,8,128]{2,1,0:T(8,128)S(1)}) custom-call(s32[4,128]{1,0:T(4,128)S(1)} %concatenate.10.meta.meta_in, f32[8,432,128]{2,1,0:T(8,128)} %copy-done, f32[2,19,64,128]{3,2,1,0:T(8,128)} %copy-done.2), custom_call_target="tpu_custom_call" | custom-call | flops 2000000 | bytes 1048576 | tf_op jit(solution)/shard_map/pallas_call | solution.py:815
  61.5 5.9 %shard_map.63 = (f32[32,128]{1,0:T(8,128)S(1)}, f32[2,17,64,128]{3,2,1,0:T(8,128)}, f32[2,17,64,128]{3,2,1,0:T(8,128)}, f32[2,17,64,128]{3,2,1,0:T(8,128)}, f32[3,2,18,8,128]{4,3,2,1,0:T(8,128)}) custom-call(s32[4,128]{1,0:T(4,128)S(1)} %concatenate.10.meta.meta_in, f32[37,8,128]{2,1,0:T(8,128)S(1)} %collective-permute-done.2.strips_in, ...), custom_call_target="tpu_custom_call" | custom-call | flops 2000000 | bytes 1048576 | tf_op jit(solution)/shard_map/pallas_call | solution.py:823
  67.4 0.0 collective-permute-done.5.rest_3_
  67.4 0.0 collective-permute-done.6.rest_4_
  67.4 0.0 collective-permute-done.7.rest_5_
  67.4 0.0 collective-permute-done.8.rest_6_
  67.4 0.0 collective-permute-done.9.rest_7_
  67.4 14.0 %all_to_all.15 = f32[32,1,128]{2,1,0:T(1,128)S(1)} all-to-all(f32[32,1,128]{2,1,0:T(1,128)S(1)} %bitcast.24), channel_id=1, replica_groups=mesh['zm'=8,'zv'=4] {'zm','zv'}, dimensions={0} | all-to-all | bytes 32768 | tf_op jit(solution)/shard_map/all_to_all | solution.py:767
  81.5 6.0 %shard_map.64 = (f32[2,16,64,128]{3,2,1,0:T(8,128)}, f32[2,16,64,128]{3,2,1,0:T(8,128)}, f32[4,128]{1,0:T(4,128)}, f32[32,128]{1,0:T(8,128)S(1)}) custom-call(s32[4,128]{1,0:T(4,128)S(1)} %concatenate.10.meta.meta_in, f32[32,128]{1,0:T(8,128)S(1)} %bitcast.22, f32[37,8,128]{2,1,0:T(8,128)} %copy-done.4, f32[2,19,8,128]{3,2,1,0:T(8,128)} %copy-done.3, ...), custom_call_target="tpu_custom_call" | custom-call | flops 2000000 | bytes 1048576 | tf_op jit(solution)/shard_map/pallas_call | solution.py:834
  87.4 8.9 %all_to_all.16 = f32[32,1,128]{2,1,0:T(1,128)S(1)} all-to-all(f32[32,1,128]{2,1,0:T(1,128)S(1)} %bitcast.25), channel_id=1, replica_groups=mesh['zm'=8,'zv'=4] {'zm','zv'}, dimensions={0} | all-to-all | bytes 32768 | tf_op jit(solution)/shard_map/all_to_all | solution.py:767
  96.3 2.7 %shard_map.65 = (f32[16,64,256]{2,1,0:T(8,128)}, f32[4]{0:T(128)}) custom-call(f32[32,128]{1,0:T(8,128)S(1)} %bitcast.23, f32[16,64,256]{2,1,0:T(8,128)} %table_in.1, f32[2,16,64,128]{3,2,1,0:T(8,128)} %get-tuple-element.72.change_in, f32[2,16,64,128]{3,2,1,0:T(8,128)} %get-tuple-element.73.r3_in), custom_call_target="tpu_custom_call" | custom-call | flops 2000000 | bytes 1048576 | tf_op jit(solution)/shard_map/pallas_call | solution.py:845
  (38 shorter events, 0.1 us)
Async XLA Ops:
  3.9 5.4 %copy-start.15 = (f32[4,64,256]{2,1,0:T(8,128)S(1)}, f32[4,64,256]{2,1,0:T(8,128)}, u32[]{:S(2)}) copy-start(f32[4,64,256]{2,1,0:T(8,128)} %get-tuple-element.41) | copy-start | bytes 786436
  3.9 6.7 %copy-start.5 = (s32[4,32,8]{1,2,0:T(8,128)S(1)}, s32[4,32,8]{1,2,0:T(8,128)}, u32[]{:S(2)}) copy-start(s32[4,32,8]{1,2,0:T(8,128)} %param.5) | copy-start | bytes 12292
  4.0 8.8 %slice-start = ((f32[16,64,256]{2,1,0:T(8,128)}), f32[16,8,256]{2,1,0:T(8,128)S(1)}, s32[]{:S(2)}) async-start(f32[16,64,256]{2,1,0:T(8,128)} %table_in.1), calls=%async_computation.3 | async-start | bytes 262144 | tf_op jit(solution)/shard_map/slice | solution.py:793
  4.0 28.4 %all-to-all-start = ((f32[8,432,128]{2,1,0:T(8,128)}), f32[8,432,128]{2,1,0:T(8,128)S(1)}, u32[]{:S(2)}, u32[]{:S(2)}) async-start(f32[8,432,128]{2,1,0:T(8,128)} %get-tuple-element.40), calls=%async_computation | async-start | bytes 3538944 | tf_op jit(solution)/shard_map/all_to_all | solution.py:792
  9.3 3.4 %collective-permute-start = (f32[4,64,256]{2,1,0:T(8,128)S(1)}, f32[4,64,256]{2,1,0:T(8,128)S(1)}, u32[]{:S(2)}, u32[]{:S(2)}) collective-permute-start(f32[4,64,256]{2,1,0:T(8,128)S(1)} %copy-done.15), channel_id=1, source_target_pairs={{4,0},{8,4},{12,8},{16,12},{20,16},{24,20},{28,24},{5,1},{9,5},{13... | collective-permute-start | bytes 786440 | tf_op jit(solution)/shard_map/ppermute | solution.py:772
  12.8 8.2 %copy-start.1 = (f32[16,64,256]{2,1,0:T(8,128)S(1)}, f32[16,64,256]{2,1,0:T(8,128)}, u32[]{:S(2)}) copy-start(f32[16,64,256]{2,1,0:T(8,128)} %table_in.1) | copy-start | bytes 3145732
  13.4 7.5 %collective-permute-start.1 = (f32[20,8,256]{2,1,0:T(8,128)}, f32[20,8,256]{2,1,0:T(8,128)}, u32[]{:S(2)}, u32[]{:S(2)}) collective-permute-start(f32[20,8,256]{2,1,0:T(8,128)} %pad_maximum_fusion), channel_id=1, source_target_pairs={{1,0},{2,1},{3,2},{5,4},{6,5},{7,6},{9,8},{10,9},{11,10},{13,12},{... | collective-permute-start | bytes 491528 | tf_op jit(solution)/shard_map/ppermute | solution.py:772
  18.1 0.6 copy-start.6
  18.8 0.6 copy-start.10
  19.4 13.0 %copy-start.8 = (f32[128,128]{1,0:T(8,128)}, f32[128,128]{1,0:T(8,128)S(1)}, u32[]{:S(2)}) copy-start(f32[128,128]{1,0:T(8,128)S(1)} %get-tuple-element.52) | copy-start | bytes 196612
  19.4 13.0 %copy-start.9 = (f32[128,128]{1,0:T(8,128)}, f32[128,128]{1,0:T(8,128)S(1)}, u32[]{:S(2)}) copy-start(f32[128,128]{1,0:T(8,128)S(1)} %get-tuple-element.51) | copy-start | bytes 196612
  23.9 1.1 %copy-start.2 = (f32[2,19,64,128]{3,2,1,0:T(8,128)}, f32[2,19,64,128]{3,2,1,0:T(8,128)S(1)}, u32[]{:S(2)}) copy-start(f32[2,19,64,128]{3,2,1,0:T(8,128)S(1)} %get-tuple-element.44.interp_in) | copy-start | bytes 3735556
  24.9 36.5 %copy-start.3 = (f32[2,19,8,128]{3,2,1,0:T(8,128)}, f32[2,19,8,128]{3,2,1,0:T(8,128)S(1)}, u32[]{:S(2)}) copy-start(f32[2,19,8,128]{3,2,1,0:T(8,128)S(1)} %get-tuple-element.42.unused_a.interp_halo_in) | copy-start | bytes 466948
  24.9 10.7 %copy-start.11 = (f32[128,128]{1,0:T(8,128)S(1)}, f32[128,128]{1,0:T(8,128)}, u32[]{:S(2)}) copy-start(f32[128,128]{1,0:T(8,128)} %copy-done.10) | copy-start | bytes 196612
  24.9 26.7 %copy-start.7 = (f32[128,128]{1,0:T(8,128)S(1)}, f32[128,128]{1,0:T(8,128)}, u32[]{:S(2)}) copy-start(f32[128,128]{1,0:T(8,128)} %copy-done.6) | copy-start | bytes 196612
  24.9 30.2 %copy-start.17 = (f32[128,128]{1,0:T(8,128)S(1)}, f32[128,128]{1,0:T(8,128)}, u32[]{:S(2)}) copy-start(f32[128,128]{1,0:T(8,128)} %get-tuple-element.55) | copy-start | bytes 196612
  24.9 30.2 %copy-start.16 = (f32[128,128]{1,0:T(8,128)S(1)}, f32[128,128]{1,0:T(8,128)}, u32[]{:S(2)}) copy-start(f32[128,128]{1,0:T(8,128)} %get-tuple-element.56) | copy-start | bytes 196612
  32.4 23.7 %copy-start = (f32[8,432,128]{2,1,0:T(8,128)}, f32[8,432,128]{2,1,0:T(8,128)S(1)}, u32[]{:S(2)}) copy-start(f32[8,432,128]{2,1,0:T(8,128)S(1)} %all-to-all-done.data) | copy-start | bytes 5308420
  34.4 20.8 %collective-permute-start.2 = (f32[37,8,128]{2,1,0:T(8,128)S(1)}, f32[37,8,128]{2,1,0:T(8,128)S(1)}, u32[]{:S(2)}, u32[]{:S(2)}) collective-permute-start(f32[37,8,128]{2,1,0:T(8,128)S(1)} %shard_map.61), channel_id=1, source_target_pairs={{1,0},{2,1},{3,2},{5,4},{6,5},{7,6},{9,8},{10,9},{11,10},{13,12},{... | collective-permute-start | bytes 454664 | tf_op jit(solution)/shard_map/ppermute | solution.py:772
  35.7 16.8 %collective-permute-start.3 = (f32[128,128]{1,0:T(8,128)S(1)}, f32[128,128]{1,0:T(8,128)S(1)}, u32[]{:S(2)}, u32[]{:S(2)}) collective-permute-start(f32[128,128]{1,0:T(8,128)S(1)} %copy-done.11), channel_id=1, source_target_pairs={{0,4},{4,0},{8,12},{12,8},{16,20},{20,16},{24,28},{28,24},{1,5},{5... | collective-permute-start | bytes 196616 | tf_op jit(solution)/shard_map/ppermute | solution.py:801
  50.2 4.9 %collective-permute-start.4 = (f32[128,128]{1,0:T(8,128)}, f32[128,128]{1,0:T(8,128)S(1)}, u32[]{:S(2)}, u32[]{:S(2)}) collective-permute-start(f32[128,128]{1,0:T(8,128)} %copy-done.9), channel_id=1, source_target_pairs={{0,8},{4,12},{8,0},{12,4},{16,24},{20,28},{24,16},{28,20},{1,9},{5... | collective-permute-start | bytes 196616 | tf_op jit(solution)/shard_map/ppermute | solution.py:801
  51.0 16.4 %collective-permute-start.5 = (f32[128,128]{1,0:T(8,128)}, f32[128,128]{1,0:T(8,128)S(1)}, u32[]{:S(2)}, u32[]{:S(2)}) collective-permute-start(f32[128,128]{1,0:T(8,128)} %copy-done.8), channel_id=1, source_target_pairs={{0,12},{4,8},{8,4},{12,0},{16,28},{20,24},{24,20},{28,16},{1,13},{... | collective-permute-start | bytes 196616 | tf_op jit(solution)/shard_map/ppermute | solution.py:801
  51.6 15.7 %collective-permute-start.6 = (f32[128,128]{1,0:T(8,128)S(1)}, f32[128,128]{1,0:T(8,128)S(1)}, u32[]{:S(2)}, u32[]{:S(2)}) collective-permute-start(f32[128,128]{1,0:T(8,128)S(1)} %copy-done.7), channel_id=1, source_target_pairs={{0,16},{4,20},{8,24},{12,28},{16,0},{20,4},{24,8},{28,12},{1,17},{... | collective-permute-start | bytes 196616 | tf_op jit(solution)/shard_map/ppermute | solution.py:801
  52.5 14.9 %collective-permute-start.7 = (f32[128,128]{1,0:T(8,128)S(1)}, f32[128,128]{1,0:T(8,128)S(1)}, u32[]{:S(2)}, u32[]{:S(2)}) collective-permute-start(f32[128,128]{1,0:T(8,128)S(1)} %get-tuple-element.54), channel_id=1, source_target_pairs={{0,20},{4,16},{8,28},{12,24},{16,4},{20,0},{24,12},{28,8},{1,21},{... | collective-permute-start | bytes 196616 | tf_op jit(solution)/shard_map/ppermute | solution.py:801
  55.1 12.2 %collective-permute-start.8 = (f32[128,128]{1,0:T(8,128)S(1)}, f32[128,128]{1,0:T(8,128)S(1)}, u32[]{:S(2)}, u32[]{:S(2)}) collective-permute-start(f32[128,128]{1,0:T(8,128)S(1)} %copy-done.17), channel_id=1, source_target_pairs={{0,24},{4,28},{8,16},{12,20},{16,8},{20,12},{24,0},{28,4},{1,25},{... | collective-permute-start | bytes 196616 | tf_op jit(solution)/shard_map/ppermute | solution.py:801
  55.2 6.3 %copy-start.4 = (f32[37,8,128]{2,1,0:T(8,128)}, f32[37,8,128]{2,1,0:T(8,128)S(1)}, u32[]{:S(2)}) copy-start(f32[37,8,128]{2,1,0:T(8,128)S(1)} %collective-permute-done.2.strips_in) | copy-start | bytes 454660
  55.2 12.2 %collective-permute-start.9 = (f32[128,128]{1,0:T(8,128)S(1)}, f32[128,128]{1,0:T(8,128)S(1)}, u32[]{:S(2)}, u32[]{:S(2)}) collective-permute-start(f32[128,128]{1,0:T(8,128)S(1)} %copy-done.16), channel_id=1, source_target_pairs={{0,28},{4,24},{8,20},{12,16},{16,12},{20,8},{24,4},{28,0},{1,29},{... | collective-permute-start | bytes 196616 | tf_op jit(solution)/shard_map/ppermute | solution.py:801
  67.4 14.1 %copy-start.12 = (f32[128,128]{1,0:T(8,128)}, f32[128,128]{1,0:T(8,128)S(1)}, u32[]{:S(2)}) copy-start(f32[128,128]{1,0:T(8,128)S(1)} %collective-permute-done.7.rest_5_) | copy-start | bytes 196612
  67.4 14.0 %copy-start.13 = (f32[128,128]{1,0:T(8,128)}, f32[128,128]{1,0:T(8,128)S(1)}, u32[]{:S(2)}) copy-start(f32[128,128]{1,0:T(8,128)S(1)} %collective-permute-done.8.rest_6_) | copy-start | bytes 196612
  67.4 14.0 %copy-start.14 = (f32[128,128]{1,0:T(8,128)}, f32[128,128]{1,0:T(8,128)S(1)}, u32[]{:S(2)}) copy-start(f32[128,128]{1,0:T(8,128)S(1)} %collective-permute-done.9.rest_7_) | copy-start | bytes 196612

commit v4 on v3

--- a/solution.py
+++ b/solution.py
@@ -82,6 +82,9 @@
     def main(self, layers):
         return (self.ct, layers, self.span, LANES)
 
+    def wide_main(self, layers):
+        return (self.ct, layers, self.span + 8, LANES)
+
     def halo(self, layers):
         return (self.ct, layers, 8, LANES)
 
@@ -101,12 +104,11 @@
 
 def pack_three_body(g, assign_in, refined, table, out, top, assign, inverse, held, extras, rows_held, sems, out_sems):
     three = range(ITERS - 1)
-    reads = [
-        pltpu.make_async_copy(refined.at[i], held.at[i], sems.at[i]) for i in range(3 * g.slots)
-    ]
-    rows_in = pltpu.make_async_copy(table.at[0:ITERS], rows_held, sems.at[3 * g.slots])
+    spans = [slice(t * g.slots, (t + 1) * g.slots) for t in three]
+    reads = [pltpu.make_async_copy(refined.at[span], held.at[span], sems.at[t]) for t, span in enumerate(spans)]
+    rows_in = pltpu.make_async_copy(table.at[0:ITERS], rows_held, sems.at[3])
     rows_out = pltpu.make_async_copy(rows_held, top, out_sems.at[3 * g.zm + 3])
-    numbers = fetch(assign_in, assign, sems.at[3 * g.slots + 1])
+    numbers = fetch(assign_in, assign, sems.at[4])
     for read in reads:
         read.start()
     rows_in.start()
@@ -116,8 +118,7 @@
     rows_out.start()
     writes = []
     for t in three:
-        for slot in range(g.slots):
-            reads[t * g.slots + slot].wait()
+        reads[t].wait()
         for peer in range(g.zm):
             source = held.at[t * g.slots + inverse[t, peer]]
             target = out.at[peer, OFFSET[t] : OFFSET[t] + ROWS, :]
@@ -285,6 +286,11 @@
             main[col, z, tile_rows(vt), :] = value
 
 
+def put_wide(main, z, values):
+    for (col, vt), value in values.items():
+        main[col, z, tile_rows(vt), :] = value
+
+
 def interp_body(g, meta, table, below, strip, interp, interp_halo, nodes, nodes_halo):
     edge_z, edge_v = edges(meta)
     stencil = Stencil(g, edge_v)
@@ -459,8 +465,8 @@
 
 
 def middle_body(g, meta_in, strips_in, interp_halo_in, totals_in, a0_in, a1_in, a2_in,
-                out, ca0_out, ca1_out, cb1_out, halos_out,
-                meta, strips, interp_halo, totals, halos, a0, a1, a2, b1, ca0, ca1, cb1, a0_halo, a1_halo, b1_halo, masks, sems, out_sems):
+                out, ca0_out, ca1_out, cb1_out,
+                meta, strips, interp_halo, totals, a0, a1, a2, b1, ca0, ca1, cb1, a0_halo, a1_halo, b1_halo, masks, sems, out_sems):
     cuts = (12, 6, 0)
     groups, at = ([], [], []), 9
     small = []
@@ -477,8 +483,9 @@
             copy.start()
     none = LAYERS[0]
     for col in range(g.ct):
-        for field in (a1, a2, b1, ca0):
+        for field in (a1, a2, b1):
             field[col, none] = jnp.zeros((g.span, LANES), F32)
+        ca0[col, none] = jnp.zeros((g.span + 8, LANES), F32)
     for copy in small:
         copy.wait()
     edge_z, edge_v = edges(meta)
@@ -508,8 +515,8 @@
         low = layer_below(at, edge_z)
         after_a = stencil(get1, at, low)
         after_b = stencil(getb, at, low)
-        put(g, ca1, halos.at[1], at, after_a)
-        put(g, cb1, halos.at[2], at, after_b)
+        put_wide(ca1, at, after_a)
+        put_wide(cb1, at, after_b)
         own = (z >= 0) & (z < BLOCK_Z)
         row, kind = jnp.where(own, z, none), jnp.where(own, 0, 1)
         for pair in range(g.pairs):
@@ -530,7 +537,7 @@
                         slot += 1
         at = clip(base, top0)
         after = stencil(get0, at, layer_below(at, edge_z))
-        put(g, ca0, halos.at[0], at, after)
+        put_wide(ca0, at, after)
         far = jnp.where(at >= BLOCK_Z, 1, 0)
         for (col, vt), value in after.items():
             if vt == g.vt:
@@ -554,7 +561,6 @@
         for which, (source, target) in enumerate(((ca0, ca0_out), (ca1, ca1_out), (cb1, cb1_out))):
             span = slice(lowest, highest + 1)
             writes.append(fetch(source.at[:, span], target.at[:, span], out_sems.at[index * 3 + which]))
-    writes.append(fetch(halos, halos_out, out_sems.at[12]))
     values = [totals[0], totals[1], carry[0], carry[1], totals[2]] + list(carry[2:])
     out[...] = spread_rows(values, out.shape[0])
     for write in writes:
@@ -587,15 +593,14 @@
     return [jnp.broadcast_to(w, TILE) for w in (w0, w1, weight_of(total, live_cells(g, meta, 2)))]
 
 
-def last_body(g, meta_in, parts, strips_in, interp_halo_in, halos_hbm, peaks0_in, a0_in, a1_in, a2_in, interp_in, ca0_in, ca1_in, cb1_in,
+def last_body(g, meta_in, parts, strips_in, interp_halo_in, peaks0_in, a0_in, a1_in, a2_in, interp_in, ca0_in, ca1_in, cb1_in,
               *rest):
     data, rest = rest[: g.zm], rest[g.zm :]
-    (sum_hbm, r3_hbm, errors_out, out,
-     meta, first_rows, strips, interp_halo, halos_in, peaks0, errors, held, f3, a0, a1, a2, interp, ca0, ca1, cb1, r2, r2_halo, change, sum_out, r3, masks, peaks, sems, out_sems) = rest
+    (sum_out, r3, errors_out, out,
+     meta, first_rows, strips, interp_halo, peaks0, errors, held, f3, a0, a1, a2, interp, ca0, ca1, cb1, r2, r2_halo, change, masks, peaks, sems, out_sems) = rest
     top = LAYERS[2] - 1
     small = []
-    for source, target in ((meta_in, meta), (strips_in, strips), (interp_halo_in, interp_halo), (halos_hbm, halos_in),
-                           (peaks0_in, peaks0)):
+    for source, target in ((meta_in, meta), (strips_in, strips), (interp_halo_in, interp_halo), (peaks0_in, peaks0)):
         small.append(fetch(source, target, sems.at[g.zm + 28 + len(small)]))
     chunks = segments(top, (3, 5, 5, 4))
     reads, at = [], 0
@@ -626,10 +631,6 @@
     w0, w1, w2 = three_weights(g, meta, parts)
     w01 = w0 * w1
     live = halo_live(g, meta, 2, left)
-    for col in range(g.ct):
-        for z in range(LAYERS[2]):
-            value = interp_halo[col, z] + w0 * halos_in[0, col, z] + w1 * halos_in[1, col, z] - w01 * halos_in[2, col, z]
-            r2_halo[col, z] = jnp.where(live[z >= BLOCK_Z][col], strip_tile(strips, 2, z, col) - value, 0.0)
     get = reader(g, r2, r2_halo)
 
     def step(i, total):
@@ -650,6 +651,12 @@
                 peak = jnp.maximum(peak, jnp.abs(value))
             peaks[2, pair] = peak
         at = clip(base, top)
+        edge = tile_rows(g.vt)
+        for col in range(g.ct):
+            value = strip_tile(strips, 2, at, col) - interp_halo[col, at] - w0 * ca0[col, at, edge, :]
+            value = value - w1 * ca1[col, at, edge, :] + w01 * cb1[col, at, edge, :]
+            there = (live[0][col] & (at < BLOCK_Z)) | (live[1][col] & (at >= BLOCK_Z))
+            r2_halo[col, at] = jnp.where(there, value, 0.0)
         far = jnp.where(at >= BLOCK_Z, 1, 0)
         own = jnp.minimum(at, BLOCK_Z - 1)
         inside = jnp.full(TILE, between(at), F32) > 0.5
@@ -679,12 +686,6 @@
         stop = top - lowest + 1 + (1 if lowest == 0 else 0)
         total = lax.fori_loop(start, stop, step, total)
         start = stop
-        below = lowest + 1 if lowest else 0
-        above = min((chunks[index - 1][0] if index else BLOCK_Z - 1), BLOCK_Z - 1)
-        for which, (source, target, layers) in enumerate(
-            ((sum_out, sum_hbm, slice(lowest, min(highest, BLOCK_Z - 1) + 1)), (r3, r3_hbm, slice(below, above + 1)))
-        ):
-            writes.append(fetch(source.at[:, layers], target.at[:, layers], out_sems.at[index * 2 + which]))
 
     line = spread_rows([total], 1)
     lane = lax.broadcasted_iota(jnp.int32, (1, 128), 1)
@@ -701,21 +702,19 @@
             found = found + jnp.sum(jnp.where(lane_p == place, column, 0.0), axis=0, keepdims=True)
         errors[i : i + 1, :] = found
         line = jnp.where(lane == 1 + i, jnp.max(found, axis=1, keepdims=True), line)
-    writes.append(fetch(errors, errors_out, out_sems.at[8]))
+    writes.append(fetch(errors, errors_out, out_sems.at[0]))
     line = jnp.where(lane == 1 + ITERS, live_cells(g, meta, ITERS - 1), line)
     out[...] = jnp.broadcast_to(line, out.shape)
     for write in writes:
         write.wait()
 
 
-def finish_body(g, parts, table_in, change_in, r3_in, out_hbm, worst_out, table, change, r3, out, worst, sems, out_sems):
+def finish_body(g, parts, table_in, change, r3, out_hbm, worst_out, table, out, worst, sems, out_sems):
     quarter = BLOCK_Z // 4
     spans = [slice(part * quarter, (part + 1) * quarter) for part in range(4)]
     reads = []
     for part, span in enumerate(spans):
         group = [pltpu.make_async_copy(table_in.at[span], table.at[span], sems.at[3 * part])]
-        for i, (source, target) in enumerate(((change_in, change), (r3_in, r3))):
-            group.append(pltpu.make_async_copy(source.at[:, span], target.at[:, span], sems.at[3 * part + 1 + i]))
         reads.append(group)
     for group in reads:
         for read in group:
@@ -785,7 +784,7 @@
     packed, top = call(
         part(pack_three_body, g), [struct(g.zm, OFFSET[3], LANES), struct(ITERS, *table.shape[1:])], [HBM] * 3, [HBM] * 2,
         [pltpu.SMEM(slots.shape, jnp.int32), pltpu.SMEM((ITERS, g.zm), jnp.int32), vmem(3 * g.slots, ROWS, LANES), vmem(g.zm, OFFSET[3] - 3 * ROWS, LANES),
-         vmem(ITERS, *table.shape[1:]), dma(3 * g.slots + 2), dma(3 * g.zm + 4)],
+         vmem(ITERS, *table.shape[1:]), dma(5), dma(3 * g.zm + 4)],
         60,
     )(slots, views, table)
     below = from_next(top, "zm")
@@ -820,12 +819,12 @@
         + [vmem(*main(LAYERS[0]))] * 7
         + [vmem(3, 2, g.pairs, *TILE), dma(9), dma(14)], WHOLE,
     )(meta, data, interp)
-    products, ca0, ca1, cb1, halos = call(
-        part(middle_body, g), [struct(everyone, 128), more, more, more, struct(3, *halo(LAYERS[1]))],
-        [HBM] * 7, [VMEM] + [HBM] * 4,
-        [pltpu.SMEM(meta.shape, jnp.int32), vmem(*strips.shape), vmem(*interp_halo.shape), vmem(3, *TILE),
-         vmem(3, *halo(LAYERS[1]))]
-        + [vmem(*main(LAYERS[0] + 1))] * 7 + [vmem(*halo(LAYERS[0] + 1))] * 3
+    wide = struct(*g.wide_main(LAYERS[2]))
+    products, ca0, ca1, cb1 = call(
+        part(middle_body, g), [struct(everyone, 128), wide, wide, wide],
+        [HBM] * 7, [VMEM] + [HBM] * 3,
+        [pltpu.SMEM(meta.shape, jnp.int32), vmem(*strips.shape), vmem(*interp_halo.shape), vmem(3, *TILE)]
+        + [vmem(*main(LAYERS[0] + 1))] * 4 + [vmem(*g.wide_main(LAYERS[0] + 1))] * 3 + [vmem(*halo(LAYERS[0] + 1))] * 3
         + [vmem(2, 2, g.pairs, *TILE), dma(13), dma(13)],
         WHOLE,
     )(meta, strips, interp_halo, totals, a0, a1, a2)
@@ -833,20 +832,18 @@
     products = to_all(products)
     change, r3, errors, stats = call(
         part(last_body, g), [own, own, struct(ITERS, 128), struct(everyone, 128)],
-        [HBM, VMEM] + [HBM] * (11 + g.zm), [HBM] * 3 + [VMEM],
+        [HBM, VMEM] + [HBM] * (10 + g.zm), [VMEM] * 2 + [HBM, VMEM],
         [pltpu.SMEM(meta.shape, jnp.int32), pltpu.SMEM((ITERS, g.blocks), jnp.int32), vmem(*strips.shape),
-         vmem(*interp_halo.shape), vmem(*halos.shape), vmem(*peaks0.shape), vmem(ITERS, 128), vmem(g.zm * ROWS, LANES)] + [vmem(*main(BLOCK_Z))] * 3 + [vmem(*main(LAYERS[2])), vmem(*main(BLOCK_Z))]
-        + [vmem(*main(LAYERS[2]))] * 4 + [vmem(*halo(LAYERS[2])), vmem(*main(LAYERS[2]))]
-        + [vmem(*main(BLOCK_Z))] * 2
-        + [vmem(3, 2, g.pairs, *TILE), vmem(3, g.pairs, *TILE), dma(g.zm + 33), dma(9)],
-        WHOLE,
-    )(meta, products, strips, interp_halo, halos, peaks0, a0, a1, a2, interp, ca0, ca1, cb1, *last_data)
+         vmem(*interp_halo.shape), vmem(*peaks0.shape), vmem(ITERS, 128), vmem(g.zm * ROWS, LANES)] + [vmem(*main(BLOCK_Z))] * 3 + [vmem(*main(LAYERS[2])), vmem(*main(BLOCK_Z))]
+        + [vmem(*g.wide_main(LAYERS[2]))] * 3 + [vmem(*main(LAYERS[2])), vmem(*halo(LAYERS[2])), vmem(*main(LAYERS[2]))]
+        + [vmem(3, 2, g.pairs, *TILE), vmem(3, g.pairs, *TILE), dma(g.zm + 33), dma(1)],
+        50.5,
+    )(meta, products, strips, interp_halo, peaks0, a0, a1, a2, interp, ca0, ca1, cb1, *last_data)
     stats = to_all(stats)
     table_out, worst = call(
-        part(finish_body, g), [struct(*table.shape), struct(ITERS)], [VMEM] + [HBM] * 3, [HBM] * 2,
-        [vmem(*table.shape)] + [vmem(*main(BLOCK_Z))] * 2
-        + [vmem(*table.shape), pltpu.SMEM((ITERS,), F32), dma(12), dma(5)],
-        WHOLE,
+        part(finish_body, g), [struct(*table.shape), struct(ITERS)], [VMEM, HBM, VMEM, VMEM], [HBM] * 2,
+        [vmem(*table.shape), vmem(*table.shape), pltpu.SMEM((ITERS,), F32), dma(12), dma(5)],
+        30,
     )(stats, table, change, r3)
     return (table_out, errors[:, : g.blocks], worst)
 

time: 99.5 us -> 98.8 us (level)
  waiting for transfers between devices: 12.3 us -> 10.2 us
  local copies, waits for them, and re-layouts: 2.77 us -> 4.55 us
  Pallas kernels: 30.7 us -> 29.3 us
    unnamed x37 -> x35, local copies, waits for them, and re-layouts: 2.46 us -> 4.24 us
    ppermute x3, waiting for transfers between devices: 3.36 us -> 1.82 us  [from_next(): return lax.ppermute(value, axis, [(i, i - 1) for i in range(1, count)])]
    pallas_call x2, Pallas kernels: 8.56 us -> 7.15 us  [the longest x1 5.81 us: shards(): call(part(middle_body, g), [struct(everyone, 128), wide, wide, wide], [HB...]
  transfers between devices with their start and end apart: 11 -> 11, of which waited for: 4 -> 3; matrix products, arithmetic and copies ran while one was open for 2% -> 2% of each run, Pallas kernels for 17% -> 17%
where the time goes in v4:
time: 98.8 us; the launch traced here: 98.4 us
  Pallas kernels  29.3 us (30%)
  starting transfers between devices  28.4 us (29%)
  blocking collectives  23.8 us (24%)
  waiting for transfers between devices  10.2 us (10%)
  local copies, waits for them, and re-layouts  4.55 us (5%)
  other arithmetic  1.25 us (1%)
    all_to_all x2, blocking collectives, to_all(): lax.all_to_all(rows.reshape(count, 1, 128), AXES, 0, 0, tiled=True)  23.8 us
    ppermute x7, starting transfers between devices, shards(): lax.ppermute(packed[k], 'zm', [(i, i ^ k) for i in range(g.zm)])  19.2 us
    all_to_all x1, waiting for transfers between devices, shards(): data = lax.all_to_all(packed, 'zm', 0, 0, tiled=True)  7.56 us
    pallas_call x1, Pallas kernels, shards(): call(part(last_body, g), [own, own, struct(ITERS, 128), struct(everyone,...  6.61 us
    pallas_call x1, Pallas kernels, shards(): call(part(middle_body, g), [struct(everyone, 128), wide, wide, wide], [HB...  5.81 us
    pallas_call x1, Pallas kernels, shards(): call(part(local_body, g), [struct(*main(LAYERS[0])), most, more, struct(3...  5.35 us
    all_to_all x1, starting transfers between devices, shards(): data = lax.all_to_all(packed, 'zm', 0, 0, tiled=True)  5.34 us
    unnamed x35, local copies, waits for them, and re-layouts  4.24 us
  transfers between devices with their start and end apart: 11, of which 3 were waited for; matrix products, arithmetic and copies ran while one was open for 2% of the time, Pallas kernels for 17%

profile of v4, /device:TPU:0, one launch (start us, length us, event | category | flops | bytes accessed | tf_op | source)
XLA Modules:
  0.0 98.4 jit_solution(14496865461645087047)
XLA Ops:
  0.6 3.0 %shard_map.58 = (f32[8,432,128]{2,1,0:T(8,128)}, f32[4,64,256]{2,1,0:T(8,128)}) custom-call(s32[32,32]{1,0:T(8,128)} %bitcast.20, f32[32,128,128]{2,1,0:T(8,128)} %bitcast.26, f32[16,64,256]{2,1,0:T(8,128)} %table_in.1), custom_call_target="tpu_custom_call" | custom-call | flops 2000000 | bytes 1048576 | tf_op jit(solution)/shard_map/pallas_call | solution.py:784
  3.6 0.0 copy-start.14
  3.6 0.0 copy-start.3
  3.7 0.0 slice-start
  3.7 5.3 %all-to-all-start = ((f32[8,432,128]{2,1,0:T(8,128)}), f32[8,432,128]{2,1,0:T(8,128)S(1)}, u32[]{:S(2)}, u32[]{:S(2)}) async-start(f32[8,432,128]{2,1,0:T(8,128)} %get-tuple-element.39), calls=%async_computation | async-start | bytes 3538944 | tf_op jit(solution)/shard_map/all_to_all | solution.py:791
  9.0 1.3 %collective-permute-start = (f32[4,64,256]{2,1,0:T(8,128)S(1)}, f32[4,64,256]{2,1,0:T(8,128)S(1)}, u32[]{:S(2)}, u32[]{:S(2)}) collective-permute-start(f32[4,64,256]{2,1,0:T(8,128)S(1)} %copy-done.14), channel_id=1, source_target_pairs={{4,0},{8,4},{12,8},{16,12},{20,16},{24,20},{28,24},{5,1},{9,5},{13... | collective-permute-start | bytes 786440 | tf_op jit(solution)/shard_map/ppermute | solution.py:771
  10.4 0.2 convert_reduce_fusion
  10.6 0.1 broadcast_select_fusion
  10.6 1.8 %collective-permute-done.below = f32[4,64,256]{2,1,0:T(8,128)S(1)} collective-permute-done((f32[4,64,256]{2,1,0:T(8,128)S(1)}, f32[4,64,256]{2,1,0:T(8,128)S(1)}, u32[]{:S(2)}, u32[]{:S(2)}) %collective-permute-start) | collective-permute-done | bytes 262176 | tf_op jit(solution)/shard_map/ppermute | solution.py:771
  12.5 0.7 pad_maximum_fusion
  13.1 1.3 %collective-permute-start.1 = (f32[20,8,256]{2,1,0:T(8,128)}, f32[20,8,256]{2,1,0:T(8,128)S(1)}, u32[]{:S(2)}, u32[]{:S(2)}) collective-permute-start(f32[20,8,256]{2,1,0:T(8,128)} %pad_maximum_fusion), channel_id=1, source_target_pairs={{1,0},{2,1},{3,2},{5,4},{6,5},{7,6},{9,8},{10,9},{11,10},{13,12},{... | collective-permute-start | bytes 491528 | tf_op jit(solution)/shard_map/ppermute | solution.py:771
  14.4 0.1 add_convert_fusion
  14.5 0.1 copy.13
  14.6 0.1 copy.14
  14.7 0.1 eq.32
  14.8 0.2 select_reduce_fusion
  15.0 0.1 concatenate.10.meta.meta_in
  15.1 2.7 %shard_map.60 = (f32[128,128]{1,0:T(8,128)S(1)}, f32[128,128]{1,0:T(8,128)S(1)}, f32[128,128]{1,0:T(8,128)S(1)}, f32[128,128]{1,0:T(8,128)S(1)}, f32[128,128]{1,...) custom-call(s32[32,32]{1,0:T(8,128)S(1)} %bitcast.21, f32[32,128,128]{2,1,0:T(8,128)} %bitcast.27), custom_call_target="tpu_custom_call" | custom-call | flops 2000000 | bytes 1048576 | tf_op jit(solution)/shard_map/pallas_call | solution.py:794
  17.8 0.6 copy-done.4
  18.5 0.6 copy-done.6
  19.1 0.6 copy-done.8
  19.7 0.6 copy-done.10
  20.3 0.6 copy-done.12
  20.9 0.0 collective-permute-done.1.strip
  20.9 2.5 %shard_map.59 = (f32[2,19,64,128]{3,2,1,0:T(8,128)S(1)}, f32[2,19,8,128]{3,2,1,0:T(8,128)S(1)}) custom-call(s32[4,128]{1,0:T(4,128)S(1)} %concatenate.10.meta.meta_in, f32[16,64,256]{2,1,0:T(8,128)S(1)} %copy-done.1, f32[4,64,256]{2,1,0:T(8,128)S(1)} %collective-permute-done.below, f32[20,8,256]{2,1,0:T(8,128)S(1)} %collective-permute-done.1.strip), custom_call_target="tpu_custom_call" | custom-call | flops 2000000 | bytes 1048576 | tf_op jit(solution)/shard_map/pallas_call | solution.py:802
  23.5 1.0 %copy-done.2 = f32[2,19,64,128]{3,2,1,0:T(8,128)} copy-done((f32[2,19,64,128]{3,2,1,0:T(8,128)}, f32[2,19,64,128]{3,2,1,0:T(8,128)S(1)}, u32[]{:S(2)}) %copy-start.2) | copy-done | bytes 1245208
  24.6 7.6 %all-to-all-done.data = f32[8,432,128]{2,1,0:T(8,128)S(1)} async-done(((f32[8,432,128]{2,1,0:T(8,128)}), f32[8,432,128]{2,1,0:T(8,128)S(1)}, u32[]{:S(2)}, u32[]{:S(2)}) %all-to-all-start) | async-done | bytes 1769504 | tf_op jit(solution)/shard_map/all_to_all | solution.py:791
  32.1 1.9 %shard_map.61 = f32[37,8,128]{2,1,0:T(8,128)S(1)} custom-call(s32[4,128]{1,0:T(4,128)S(1)} %concatenate.10.meta.meta_in, f32[8,432,128]{2,1,0:T(8,128)S(1)} %all-to-all-done.data, f32[2,19,8,128]{3,2,1,0:T(8,128)S(1)} %get-tuple-element.41.unused_a.interp_halo_in, f32[128,128]{1,0:T(8,128)S(1)} %get-tuple-element.61.unused_b.rest_0_), custom_call_target="tpu_custom_call" | custom-call | flops 2000000 | bytes 1048576 | tf_op jit(solution)/shard_map/pallas_call | solution.py:807
  34.1 1.3 %collective-permute-start.2 = (f32[37,8,128]{2,1,0:T(8,128)S(1)}, f32[37,8,128]{2,1,0:T(8,128)S(1)}, u32[]{:S(2)}, u32[]{:S(2)}) collective-permute-start(f32[37,8,128]{2,1,0:T(8,128)S(1)} %shard_map.61), channel_id=1, source_target_pairs={{1,0},{2,1},{3,2},{5,4},{6,5},{7,6},{9,8},{10,9},{11,10},{13,12},{... | collective-permute-start | bytes 454664 | tf_op jit(solution)/shard_map/ppermute | solution.py:771
  35.4 14.1 %collective-permute-start.3 = (f32[128,128]{1,0:T(8,128)S(1)}, f32[128,128]{1,0:T(8,128)S(1)}, u32[]{:S(2)}, u32[]{:S(2)}) collective-permute-start(f32[128,128]{1,0:T(8,128)S(1)} %copy-done.13), channel_id=1, source_target_pairs={{0,4},{4,0},{8,12},{12,8},{16,20},{20,16},{24,28},{28,24},{1,5},{5... | collective-permute-start | bytes 196616 | tf_op jit(solution)/shard_map/ppermute | solution.py:800
  49.5 1.3 %collective-permute-start.4 = (f32[128,128]{1,0:T(8,128)S(1)}, f32[128,128]{1,0:T(8,128)S(1)}, u32[]{:S(2)}, u32[]{:S(2)}) collective-permute-start(f32[128,128]{1,0:T(8,128)S(1)} %copy-done.11), channel_id=1, source_target_pairs={{0,8},{4,12},{8,0},{12,4},{16,24},{20,28},{24,16},{28,20},{1,9},{5... | collective-permute-start | bytes 196616 | tf_op jit(solution)/shard_map/ppermute | solution.py:800
  50.8 0.2 collective-permute-start.5
  50.9 1.2 %collective-permute-start.6 = (f32[128,128]{1,0:T(8,128)S(1)}, f32[128,128]{1,0:T(8,128)S(1)}, u32[]{:S(2)}, u32[]{:S(2)}) collective-permute-start(f32[128,128]{1,0:T(8,128)S(1)} %copy-done.7), channel_id=1, source_target_pairs={{0,16},{4,20},{8,24},{12,28},{16,0},{20,4},{24,8},{28,12},{1,17},{... | collective-permute-start | bytes 196616 | tf_op jit(solution)/shard_map/ppermute | solution.py:800
  52.2 0.0 collective-permute-done.3.rest_1_
  52.2 0.8 collective-permute-start.7
  53.0 0.8 collective-permute-done.4.rest_2_
  53.8 0.7 collective-permute-start.8
  54.5 0.8 collective-permute-start.9
  55.4 5.4 %shard_map.62 = (f32[2,19,64,128]{3,2,1,0:T(8,128)}, f32[2,18,64,128]{3,2,1,0:T(8,128)}, f32[2,17,64,128]{3,2,1,0:T(8,128)}, f32[3,8,128]{2,1,0:T(8,128)S(1)}, f32[8,8,128]{2,1,0:T(8,128)S(1)}) custom-call(s32[4,128]{1,0:T(4,128)S(1)} %concatenate.10.meta.meta_in, f32[8,432,128]{2,1,0:T(8,128)} %copy-done, f32[2,19,64,128]{3,2,1,0:T(8,128)} %copy-done.2), custom_call_target="tpu_custom_call" | custom-call | flops 2000000 | bytes 1048576 | tf_op jit(solution)/shard_map/pallas_call | solution.py:814
  60.7 5.8 %shard_map.63 = (f32[32,128]{1,0:T(8,128)S(1)}, f32[2,17,72,128]{3,2,1,0:T(8,128)}, f32[2,17,72,128]{3,2,1,0:T(8,128)}, f32[2,17,72,128]{3,2,1,0:T(8,128)}) custom-call(s32[4,128]{1,0:T(4,128)S(1)} %concatenate.10.meta.meta_in, f32[37,8,128]{2,1,0:T(8,128)S(1)} %collective-permute-done.2.strips_in, ...), custom_call_target="tpu_custom_call" | custom-call | flops 2000000 | bytes 1048576 | tf_op jit(solution)/shard_map/pallas_call | solution.py:823
  66.5 0.0 collective-permute-done.5.rest_3_
  66.6 0.0 collective-permute-done.6.rest_4_
  66.6 0.0 collective-permute-done.8.rest_6_
  66.6 0.0 collective-permute-done.9.rest_7_
  66.6 15.0 %all_to_all.15 = f32[32,1,128]{2,1,0:T(1,128)S(1)} all-to-all(f32[32,1,128]{2,1,0:T(1,128)S(1)} %bitcast.24), channel_id=1, replica_groups=mesh['zm'=8,'zv'=4] {'zm','zv'}, dimensions={0} | all-to-all | bytes 32768 | tf_op jit(solution)/shard_map/all_to_all | solution.py:766
  81.5 6.6 %shard_map.64 = (f32[2,16,64,128]{3,2,1,0:T(8,128)S(1)}, f32[2,16,64,128]{3,2,1,0:T(8,128)S(1)}, f32[4,128]{1,0:T(4,128)}, f32[32,128]{1,0:T(8,128)S(1)}) custom-call(s32[4,128]{1,0:T(4,128)S(1)} %concatenate.10.meta.meta_in, f32[32,128]{1,0:T(8,128)S(1)} %bitcast.22, f32[37,8,128]{2,1,0:T(8,128)S(1)} %collective-permute-done.2.strips_in, ...), custom_call_target="tpu_custom_call" | custom-call | flops 2000000 | bytes 1048576 | tf_op jit(solution)/shard_map/pallas_call | solution.py:833
  88.2 8.9 %all_to_all.16 = f32[32,1,128]{2,1,0:T(1,128)S(1)} all-to-all(f32[32,1,128]{2,1,0:T(1,128)S(1)} %bitcast.25), channel_id=1, replica_groups=mesh['zm'=8,'zv'=4] {'zm','zv'}, dimensions={0} | all-to-all | bytes 32768 | tf_op jit(solution)/shard_map/all_to_all | solution.py:766
  97.1 1.3 %shard_map.65 = (f32[16,64,256]{2,1,0:T(8,128)}, f32[4]{0:T(128)}) custom-call(f32[32,128]{1,0:T(8,128)S(1)} %bitcast.23, f32[16,64,256]{2,1,0:T(8,128)S(1)} %copy-done.1, f32[2,16,64,128]{3,2,1,0:T(8,128)S(1)} %get-tuple-element.70.change, f32[2,16,64,128]{3,2,1,0:T(8,128)S(1)} %get-tuple-element.71.r3), custom_call_target="tpu_custom_call" | custom-call | flops 2000000 | bytes 1048576 | tf_op jit(solution)/shard_map/pallas_call | solution.py:843
  (36 shorter events, 0.1 us)
Async XLA Ops:
  3.6 5.4 %copy-start.14 = (f32[4,64,256]{2,1,0:T(8,128)S(1)}, f32[4,64,256]{2,1,0:T(8,128)}, u32[]{:S(2)}) copy-start(f32[4,64,256]{2,1,0:T(8,128)} %get-tuple-element.40) | copy-start | bytes 786436
  3.6 6.7 %copy-start.3 = (s32[4,32,8]{1,2,0:T(8,128)S(1)}, s32[4,32,8]{1,2,0:T(8,128)}, u32[]{:S(2)}) copy-start(s32[4,32,8]{1,2,0:T(8,128)} %param.5) | copy-start | bytes 12292
  3.7 8.8 %slice-start = ((f32[16,64,256]{2,1,0:T(8,128)}), f32[16,8,256]{2,1,0:T(8,128)S(1)}, s32[]{:S(2)}) async-start(f32[16,64,256]{2,1,0:T(8,128)} %table_in.1), calls=%async_computation.3 | async-start | bytes 262144 | tf_op jit(solution)/shard_map/slice | solution.py:792
  3.7 28.4 %all-to-all-start = ((f32[8,432,128]{2,1,0:T(8,128)}), f32[8,432,128]{2,1,0:T(8,128)S(1)}, u32[]{:S(2)}, u32[]{:S(2)}) async-start(f32[8,432,128]{2,1,0:T(8,128)} %get-tuple-element.39), calls=%async_computation | async-start | bytes 3538944 | tf_op jit(solution)/shard_map/all_to_all | solution.py:791
  9.0 3.4 %collective-permute-start = (f32[4,64,256]{2,1,0:T(8,128)S(1)}, f32[4,64,256]{2,1,0:T(8,128)S(1)}, u32[]{:S(2)}, u32[]{:S(2)}) collective-permute-start(f32[4,64,256]{2,1,0:T(8,128)S(1)} %copy-done.14), channel_id=1, source_target_pairs={{4,0},{8,4},{12,8},{16,12},{20,16},{24,20},{28,24},{5,1},{9,5},{13... | collective-permute-start | bytes 786440 | tf_op jit(solution)/shard_map/ppermute | solution.py:771
  12.5 8.5 %copy-start.1 = (f32[16,64,256]{2,1,0:T(8,128)S(1)}, f32[16,64,256]{2,1,0:T(8,128)}, u32[]{:S(2)}) copy-start(f32[16,64,256]{2,1,0:T(8,128)} %table_in.1) | copy-start | bytes 3145732
  13.1 7.8 %collective-permute-start.1 = (f32[20,8,256]{2,1,0:T(8,128)}, f32[20,8,256]{2,1,0:T(8,128)S(1)}, u32[]{:S(2)}, u32[]{:S(2)}) collective-permute-start(f32[20,8,256]{2,1,0:T(8,128)} %pad_maximum_fusion), channel_id=1, source_target_pairs={{1,0},{2,1},{3,2},{5,4},{6,5},{7,6},{9,8},{10,9},{11,10},{13,12},{... | collective-permute-start | bytes 491528 | tf_op jit(solution)/shard_map/ppermute | solution.py:771
  17.8 0.6 copy-start.4
  18.5 0.6 copy-start.6
  19.1 0.6 copy-start.8
  19.7 0.6 copy-start.10
  20.3 0.6 copy-start.12
  23.5 1.0 %copy-start.2 = (f32[2,19,64,128]{3,2,1,0:T(8,128)}, f32[2,19,64,128]{3,2,1,0:T(8,128)S(1)}, u32[]{:S(2)}) copy-start(f32[2,19,64,128]{3,2,1,0:T(8,128)S(1)} %get-tuple-element.43.interp_in) | copy-start | bytes 3735556
  24.5 10.8 %copy-start.13 = (f32[128,128]{1,0:T(8,128)S(1)}, f32[128,128]{1,0:T(8,128)}, u32[]{:S(2)}) copy-start(f32[128,128]{1,0:T(8,128)} %copy-done.12) | copy-start | bytes 196612
  24.5 25.0 %copy-start.11 = (f32[128,128]{1,0:T(8,128)S(1)}, f32[128,128]{1,0:T(8,128)}, u32[]{:S(2)}) copy-start(f32[128,128]{1,0:T(8,128)} %copy-done.10) | copy-start | bytes 196612
  24.5 26.2 %copy-start.9 = (f32[128,128]{1,0:T(8,128)S(1)}, f32[128,128]{1,0:T(8,128)}, u32[]{:S(2)}) copy-start(f32[128,128]{1,0:T(8,128)} %copy-done.8) | copy-start | bytes 196612
  24.5 26.4 %copy-start.7 = (f32[128,128]{1,0:T(8,128)S(1)}, f32[128,128]{1,0:T(8,128)}, u32[]{:S(2)}) copy-start(f32[128,128]{1,0:T(8,128)} %copy-done.6) | copy-start | bytes 196612
  24.5 27.6 %copy-start.5 = (f32[128,128]{1,0:T(8,128)S(1)}, f32[128,128]{1,0:T(8,128)}, u32[]{:S(2)}) copy-start(f32[128,128]{1,0:T(8,128)} %copy-done.4) | copy-start | bytes 196612
  24.5 30.0 %copy-start.15 = (f32[128,128]{1,0:T(8,128)S(1)}, f32[128,128]{1,0:T(8,128)}, u32[]{:S(2)}) copy-start(f32[128,128]{1,0:T(8,128)} %get-tuple-element.55) | copy-start | bytes 196612
  32.1 23.2 %copy-start = (f32[8,432,128]{2,1,0:T(8,128)}, f32[8,432,128]{2,1,0:T(8,128)S(1)}, u32[]{:S(2)}) copy-start(f32[8,432,128]{2,1,0:T(8,128)S(1)} %all-to-all-done.data) | copy-start | bytes 5308420
  32.1 21.7 %copy-start.16 = (f32[128,128]{1,0:T(8,128)S(1)}, f32[128,128]{1,0:T(8,128)}, u32[]{:S(2)}) copy-start(f32[128,128]{1,0:T(8,128)} %get-tuple-element.54) | copy-start | bytes 196612
  34.1 20.5 %collective-permute-start.2 = (f32[37,8,128]{2,1,0:T(8,128)S(1)}, f32[37,8,128]{2,1,0:T(8,128)S(1)}, u32[]{:S(2)}, u32[]{:S(2)}) collective-permute-start(f32[37,8,128]{2,1,0:T(8,128)S(1)} %shard_map.61), channel_id=1, source_target_pairs={{1,0},{2,1},{3,2},{5,4},{6,5},{7,6},{9,8},{10,9},{11,10},{13,12},{... | collective-permute-start | bytes 454664 | tf_op jit(solution)/shard_map/ppermute | solution.py:771
  35.4 16.8 %collective-permute-start.3 = (f32[128,128]{1,0:T(8,128)S(1)}, f32[128,128]{1,0:T(8,128)S(1)}, u32[]{:S(2)}, u32[]{:S(2)}) collective-permute-start(f32[128,128]{1,0:T(8,128)S(1)} %copy-done.13), channel_id=1, source_target_pairs={{0,4},{4,0},{8,12},{12,8},{16,20},{20,16},{24,28},{28,24},{1,5},{5... | collective-permute-start | bytes 196616 | tf_op jit(solution)/shard_map/ppermute | solution.py:800
  49.5 4.3 %collective-permute-start.4 = (f32[128,128]{1,0:T(8,128)S(1)}, f32[128,128]{1,0:T(8,128)S(1)}, u32[]{:S(2)}, u32[]{:S(2)}) collective-permute-start(f32[128,128]{1,0:T(8,128)S(1)} %copy-done.11), channel_id=1, source_target_pairs={{0,8},{4,12},{8,0},{12,4},{16,24},{20,28},{24,16},{28,20},{1,9},{5... | collective-permute-start | bytes 196616 | tf_op jit(solution)/shard_map/ppermute | solution.py:800
  50.8 15.8 %collective-permute-start.5 = (f32[128,128]{1,0:T(8,128)S(1)}, f32[128,128]{1,0:T(8,128)S(1)}, u32[]{:S(2)}, u32[]{:S(2)}) collective-permute-start(f32[128,128]{1,0:T(8,128)S(1)} %copy-done.9), channel_id=1, source_target_pairs={{0,12},{4,8},{8,4},{12,0},{16,28},{20,24},{24,20},{28,16},{1,13},{... | collective-permute-start | bytes 196616 | tf_op jit(solution)/shard_map/ppermute | solution.py:800
  50.9 15.6 %collective-permute-start.6 = (f32[128,128]{1,0:T(8,128)S(1)}, f32[128,128]{1,0:T(8,128)S(1)}, u32[]{:S(2)}, u32[]{:S(2)}) collective-permute-start(f32[128,128]{1,0:T(8,128)S(1)} %copy-done.7), channel_id=1, source_target_pairs={{0,16},{4,20},{8,24},{12,28},{16,0},{20,4},{24,8},{28,12},{1,17},{... | collective-permute-start | bytes 196616 | tf_op jit(solution)/shard_map/ppermute | solution.py:800
  52.2 14.4 %collective-permute-start.7 = (f32[128,128]{1,0:T(8,128)S(1)}, f32[128,128]{1,0:T(8,128)S(1)}, u32[]{:S(2)}, u32[]{:S(2)}) collective-permute-start(f32[128,128]{1,0:T(8,128)S(1)} %copy-done.5), channel_id=1, source_target_pairs={{0,20},{4,16},{8,28},{12,24},{16,4},{20,0},{24,12},{28,8},{1,21},{... | collective-permute-start | bytes 196616 | tf_op jit(solution)/shard_map/ppermute | solution.py:800
  53.8 12.8 %collective-permute-start.8 = (f32[128,128]{1,0:T(8,128)S(1)}, f32[128,128]{1,0:T(8,128)S(1)}, u32[]{:S(2)}, u32[]{:S(2)}) collective-permute-start(f32[128,128]{1,0:T(8,128)S(1)} %copy-done.16), channel_id=1, source_target_pairs={{0,24},{4,28},{8,16},{12,20},{16,8},{20,12},{24,0},{28,4},{1,25},{... | collective-permute-start | bytes 196616 | tf_op jit(solution)/shard_map/ppermute | solution.py:800
  54.5 12.1 %collective-permute-start.9 = (f32[128,128]{1,0:T(8,128)S(1)}, f32[128,128]{1,0:T(8,128)S(1)}, u32[]{:S(2)}, u32[]{:S(2)}) collective-permute-start(f32[128,128]{1,0:T(8,128)S(1)} %copy-done.15), channel_id=1, source_target_pairs={{0,28},{4,24},{8,20},{12,16},{16,12},{20,8},{24,4},{28,0},{1,29},{... | collective-permute-start | bytes 196616 | tf_op jit(solution)/shard_map/ppermute | solution.py:800

commit v5 on v4

--- a/solution.py
+++ b/solution.py
@@ -172,51 +172,28 @@
     return copy
 
 
-def strip_body(g, meta, data, unused_a, unused_b, out, held, planes, sems):
-    three = range(ITERS - 1)
-    left, sub = lane_ids() < HALF, sub_ids()
-    two = 2 * 8
-
-    def copies(t, c):
-        at, mine = t * g.cb + c, jnp.maximum(meta[t, c], 0)
-        far = data.at[jnp.maximum(meta[t, g.blocks + c], 0), OFFSET[t] + ROWS : OFFSET[t] + LAYERS[t] * PAIRS, :]
-        result = [pltpu.make_async_copy(far, held.at[at, 2 * two : 2 * two + halo_rows(t) * PAIRS, :], sems.at[3 * at])]
-        for zt in range(2):
-            first = OFFSET[t] + zt * 8 * PAIRS
-            source = data.at[mine, first : first + two, :]
-            result.append(pltpu.make_async_copy(source, held.at[at, zt * two : zt * two + two, :], sems.at[3 * at + 1 + zt]))
-        return result
-
-    for t in three:
-        for c in range(g.cb):
-            for copy in copies(t, c):
-                copy.start()
-    for t in three:
-        for c in range(g.cb):
-            for copy in copies(t, c):
-                copy.wait()
-        first = sum(LAYERS[:t])
-        for z in range(LAYERS[t]):
-            for col in range(g.ct):
-                tiles = []
-                for c in (2 * col, 2 * col + 1):
-                    if z < BLOCK_Z:
-                        tiles.append(held[t * g.cb + c, pl.ds(z // 8 * two + z % 8, PAIRS, stride=8), :])
-                    else:
-                        at = 2 * two + (z - BLOCK_Z) * PAIRS
-                        tiles.append(held[t * g.cb + c, at : at + PAIRS, :])
-                even, odd = pair_tiles(left, *tiles)
-                planes[col, first + z, pl.ds(0, PAIRS, stride=2), :] = even
-                planes[col, first + z, pl.ds(1, PAIRS, stride=2), :] = odd
-        if t == 0:
-            for z in range(LAYERS[0]):
-                out[z] = jnp.where(sub < 4, planes[0, z, 0:8, :], pltpu.roll(planes[1, z, 0:8, :], 4, 0))
-    for z in range(LAYERS[1]):
-        one, two_at = LAYERS[0] + z, LAYERS[0] + LAYERS[1] + min(z, LAYERS[2] - 1)
-        low = jnp.where(sub < 2, planes[0, one, 0:8, :], pltpu.roll(planes[1, one, 0:8, :], 2, 0))
-        high = pltpu.roll(planes[0, two_at, 0:8, :], 4, 0)
-        high = jnp.where(sub < 6, high, pltpu.roll(planes[1, two_at, 0:8, :], 6, 0))
-        out[LAYERS[0] + z] = jnp.where(sub < 4, low, high)
+def strip_body(g, meta, data, unused_a, unused_b, out):
+    left = lane_ids() < HALF
+    for t in range(ITERS - 1):
+        columns = (4, 2, 2)[t]
+        base = (0, LAYERS[0] * 8, LAYERS[0] * 8 + 4)[t]
+        for col in range(g.ct):
+            mine = [jnp.maximum(meta[t, 2 * col + half], 0) for half in range(2)]
+            far = [jnp.maximum(meta[t, g.blocks + 2 * col + half], 0) for half in range(2)]
+            row = base + col * columns
+            for zt in range(2):
+                for j in range(columns // 2):
+                    at = OFFSET[t] + zt * 8 * PAIRS + j * 8
+                    even, odd = pair_tiles(left, *[data[owner, at : at + 8, :] for owner in mine])
+                    out[pl.ds(row + zt * 64 + 2 * j, 8, stride=8), :] = even
+                    out[pl.ds(row + zt * 64 + 2 * j + 1, 8, stride=8), :] = odd
+            for z in range(BLOCK_Z, LAYERS[t]):
+                at = OFFSET[t] + z * PAIRS
+                even, odd = pair_tiles(left, *[data[owner, at : at + PAIRS, :] for owner in far])
+                for j in range(columns // 2):
+                    first = row + z * 8 + 2 * j
+                    out[first : first + 1, :] = even[j : j + 1, :]
+                    out[first + 1 : first + 2, :] = odd[j : j + 1, :]
 
 
 def strip_tile(strips, t, z, col):
@@ -401,10 +378,9 @@
     for copy in groups[0]:
         copy.wait()
 
-    @pl.loop(0, g.pairs)
-    def _(pair):
+    for pair in range(g.pairs):
         vb, col = pair // g.ct, pair % g.ct
-        row = pl.multiple_of(vb * BLOCK_V, BLOCK_V)
+        row = vb * BLOCK_V
         column = g.blocks + vb * g.cb + 2 * col
         for t in range(3):
             starts = [jnp.maximum(meta[t, column + half], 0) * OFFSET[3] for half in range(2)]
@@ -805,11 +781,11 @@
     )(meta, table, below, strip)
 
     strips = call(
-        part(strip_body, g), struct(sum(LAYERS[:2]), *TILE), [SMEM] + [HBM] * 3, VMEM,
-        [vmem(3 * g.cb, ROWS, LANES), vmem(g.ct, sum(LAYERS[:3]), BLOCK_V, LANES), dma(9 * g.cb)],
+        part(strip_body, g), struct(sum(LAYERS[:2]) * 8, LANES), [SMEM, VMEM, HBM, HBM], VMEM,
+        [],
         PART,
     )(meta, data, interp_halo, packed[0])
-    strips = from_next(strips, "zv")
+    strips = from_next(strips, "zv").reshape(sum(LAYERS[:2]), *TILE)
     own, more, most = struct(*main(BLOCK_Z)), struct(*main(LAYERS[2])), struct(*main(LAYERS[1]))
     a0, a1, a2, totals, peaks0 = call(
         part(local_body, g), [struct(*main(LAYERS[0])), most, more, struct(3, *TILE), struct(g.pairs, *TILE)],

time: 98.8 us -> 97.1 us (0.983)
  Pallas kernels: 29.3 us -> 27.5 us
    pallas_call x1, Pallas kernels: 1.93 us -> 0.69 us  [shards(): call(part(strip_body, g), struct(sum(LAYERS[:2]) * 8, LANES), [SMEM, VMEM...]
  transfers between devices with their start and end apart: 11 -> 11, of which waited for: 3 -> 3; matrix products, arithmetic and copies ran while one was open for 2% -> 2% of each run, Pallas kernels for 17% -> 16%
where the time goes in v5:
time: 97.1 us; the launch traced here: 96.6 us
  starting transfers between devices  28.3 us (29%)
  Pallas kernels  27.5 us (28%)
  blocking collectives  24 us (25%)
  waiting for transfers between devices  10.2 us (11%)
  local copies, waits for them, and re-layouts  4.55 us (5%)
  other arithmetic  1.25 us (1%)
    all_to_all x2, blocking collectives, to_all(): lax.all_to_all(rows.reshape(count, 1, 128), AXES, 0, 0, tiled=True)  24 us
    ppermute x7, starting transfers between devices, shards(): lax.ppermute(packed[k], 'zm', [(i, i ^ k) for i in range(g.zm)])  19.1 us
    all_to_all x1, waiting for transfers between devices, shards(): data = lax.all_to_all(packed, 'zm', 0, 0, tiled=True)  7.56 us
    pallas_call x1, Pallas kernels, shards(): call(part(last_body, g), [own, own, struct(ITERS, 128), struct(everyone,...  6.61 us
    pallas_call x1, Pallas kernels, shards(): call(part(middle_body, g), [struct(everyone, 128), wide, wide, wide], [HB...  5.81 us
    all_to_all x1, starting transfers between devices, shards(): data = lax.all_to_all(packed, 'zm', 0, 0, tiled=True)  5.34 us
    pallas_call x1, Pallas kernels, shards(): call(part(local_body, g), [struct(*main(LAYERS[0])), most, more, struct(3...  4.82 us
    unnamed x35, local copies, waits for them, and re-layouts  4.24 us
  transfers between devices with their start and end apart: 11, of which 3 were waited for; matrix products, arithmetic and copies ran while one was open for 2% of the time, Pallas kernels for 16%

profile of v5, /device:TPU:0, one launch (start us, length us, event | category | flops | bytes accessed | tf_op | source)
XLA Modules:
  0.0 96.6 jit_solution(8835218269379378683)
XLA Ops:
  0.6 3.0 %shard_map.58 = (f32[8,432,128]{2,1,0:T(8,128)}, f32[4,64,256]{2,1,0:T(8,128)}) custom-call(s32[32,32]{1,0:T(8,128)} %bitcast.23, f32[32,128,128]{2,1,0:T(8,128)} %bitcast.29, f32[16,64,256]{2,1,0:T(8,128)} %table_in.1), custom_call_target="tpu_custom_call" | custom-call | flops 2000000 | bytes 1048576 | tf_op jit(solution)/shard_map/pallas_call | solution.py:760
  3.6 0.0 copy-start.14
  3.6 0.0 copy-start.3
  3.7 0.0 slice-start
  3.7 5.3 %all-to-all-start = ((f32[8,432,128]{2,1,0:T(8,128)}), f32[8,432,128]{2,1,0:T(8,128)S(1)}, u32[]{:S(2)}, u32[]{:S(2)}) async-start(f32[8,432,128]{2,1,0:T(8,128)} %get-tuple-element.39), calls=%async_computation | async-start | bytes 3538944 | tf_op jit(solution)/shard_map/all_to_all | solution.py:767
  9.0 1.3 %collective-permute-start = (f32[4,64,256]{2,1,0:T(8,128)S(1)}, f32[4,64,256]{2,1,0:T(8,128)S(1)}, u32[]{:S(2)}, u32[]{:S(2)}) collective-permute-start(f32[4,64,256]{2,1,0:T(8,128)S(1)} %copy-done.14), channel_id=1, source_target_pairs={{4,0},{8,4},{12,8},{16,12},{20,16},{24,20},{28,24},{5,1},{9,5},{13... | collective-permute-start | bytes 786440 | tf_op jit(solution)/shard_map/ppermute | solution.py:747
  10.4 0.2 convert_reduce_fusion
  10.6 0.1 broadcast_select_fusion
  10.6 1.8 %collective-permute-done.below = f32[4,64,256]{2,1,0:T(8,128)S(1)} collective-permute-done((f32[4,64,256]{2,1,0:T(8,128)S(1)}, f32[4,64,256]{2,1,0:T(8,128)S(1)}, u32[]{:S(2)}, u32[]{:S(2)}) %collective-permute-start) | collective-permute-done | bytes 262176 | tf_op jit(solution)/shard_map/ppermute | solution.py:747
  12.5 0.7 pad_maximum_fusion
  13.1 1.3 %collective-permute-start.1 = (f32[20,8,256]{2,1,0:T(8,128)}, f32[20,8,256]{2,1,0:T(8,128)S(1)}, u32[]{:S(2)}, u32[]{:S(2)}) collective-permute-start(f32[20,8,256]{2,1,0:T(8,128)} %pad_maximum_fusion), channel_id=1, source_target_pairs={{1,0},{2,1},{3,2},{5,4},{6,5},{7,6},{9,8},{10,9},{11,10},{13,12},{... | collective-permute-start | bytes 491528 | tf_op jit(solution)/shard_map/ppermute | solution.py:747
  14.4 0.1 add_convert_fusion
  14.5 0.1 copy.13
  14.6 0.1 copy.14
  14.7 0.1 eq.32
  14.8 0.2 select_reduce_fusion
  15.0 0.1 concatenate.10.meta.meta_in
  15.1 2.7 %shard_map.60 = (f32[128,128]{1,0:T(8,128)S(1)}, f32[128,128]{1,0:T(8,128)S(1)}, f32[128,128]{1,0:T(8,128)S(1)}, f32[128,128]{1,0:T(8,128)S(1)}, f32[128,128]{1,...) custom-call(s32[32,32]{1,0:T(8,128)S(1)} %bitcast.24, f32[32,128,128]{2,1,0:T(8,128)} %bitcast.30), custom_call_target="tpu_custom_call" | custom-call | flops 2000000 | bytes 1048576 | tf_op jit(solution)/shard_map/pallas_call | solution.py:770
  17.8 0.6 copy-done.4
  18.5 0.6 copy-done.6
  19.1 0.6 copy-done.8
  19.7 0.6 copy-done.10
  20.3 0.6 copy-done.12
  20.9 0.0 collective-permute-done.1.strip
  20.9 2.5 %shard_map.59 = (f32[2,19,64,128]{3,2,1,0:T(8,128)S(1)}, f32[2,19,8,128]{3,2,1,0:T(8,128)S(1)}) custom-call(s32[4,128]{1,0:T(4,128)S(1)} %concatenate.10.meta.meta_in, f32[16,64,256]{2,1,0:T(8,128)S(1)} %copy-done.1, f32[4,64,256]{2,1,0:T(8,128)S(1)} %collective-permute-done.below, f32[20,8,256]{2,1,0:T(8,128)S(1)} %collective-permute-done.1.strip), custom_call_target="tpu_custom_call" | custom-call | flops 2000000 | bytes 1048576 | tf_op jit(solution)/shard_map/pallas_call | solution.py:778
  23.5 1.0 %copy-done.2 = f32[2,19,64,128]{3,2,1,0:T(8,128)} copy-done((f32[2,19,64,128]{3,2,1,0:T(8,128)}, f32[2,19,64,128]{3,2,1,0:T(8,128)S(1)}, u32[]{:S(2)}) %copy-start.2) | copy-done | bytes 1245208
  24.6 7.6 %all-to-all-done.data = f32[8,432,128]{2,1,0:T(8,128)S(1)} async-done(((f32[8,432,128]{2,1,0:T(8,128)}), f32[8,432,128]{2,1,0:T(8,128)S(1)}, u32[]{:S(2)}, u32[]{:S(2)}) %all-to-all-start) | async-done | bytes 1769504 | tf_op jit(solution)/shard_map/all_to_all | solution.py:767
  32.1 0.7 shard_map.61
  32.8 1.3 %collective-permute-start.2 = (f32[296,128]{1,0:T(8,128)S(1)}, f32[296,128]{1,0:T(8,128)S(1)}, u32[]{:S(2)}, u32[]{:S(2)}) collective-permute-start(f32[296,128]{1,0:T(8,128)S(1)} %shard_map.61), channel_id=1, source_target_pairs={{1,0},{2,1},{3,2},{5,4},{6,5},{7,6},{9,8},{10,9},{11,10},{13,12},{... | collective-permute-start | bytes 454664 | tf_op jit(solution)/shard_map/ppermute | solution.py:747
  34.1 13.9 %collective-permute-start.3 = (f32[128,128]{1,0:T(8,128)S(1)}, f32[128,128]{1,0:T(8,128)S(1)}, u32[]{:S(2)}, u32[]{:S(2)}) collective-permute-start(f32[128,128]{1,0:T(8,128)S(1)} %copy-done.13), channel_id=1, source_target_pairs={{0,4},{4,0},{8,12},{12,8},{16,20},{20,16},{24,28},{28,24},{1,5},{5... | collective-permute-start | bytes 196616 | tf_op jit(solution)/shard_map/ppermute | solution.py:776
  48.1 1.5 %collective-permute-start.4 = (f32[128,128]{1,0:T(8,128)S(1)}, f32[128,128]{1,0:T(8,128)S(1)}, u32[]{:S(2)}, u32[]{:S(2)}) collective-permute-start(f32[128,128]{1,0:T(8,128)S(1)} %copy-done.11), channel_id=1, source_target_pairs={{0,8},{4,12},{8,0},{12,4},{16,24},{20,28},{24,16},{28,20},{1,9},{5... | collective-permute-start | bytes 196616 | tf_op jit(solution)/shard_map/ppermute | solution.py:776
  49.5 0.0 collective-permute-start.5
  49.5 1.4 %collective-permute-start.6 = (f32[128,128]{1,0:T(8,128)S(1)}, f32[128,128]{1,0:T(8,128)S(1)}, u32[]{:S(2)}, u32[]{:S(2)}) collective-permute-start(f32[128,128]{1,0:T(8,128)S(1)} %copy-done.7), channel_id=1, source_target_pairs={{0,16},{4,20},{8,24},{12,28},{16,0},{20,4},{24,8},{28,12},{1,17},{... | collective-permute-start | bytes 196616 | tf_op jit(solution)/shard_map/ppermute | solution.py:776
  50.9 0.0 collective-permute-done.3.rest_1_
  50.9 0.6 collective-permute-start.7
  51.6 0.8 collective-permute-done.4.rest_2_
  52.3 1.0 %collective-permute-start.8 = (f32[128,128]{1,0:T(8,128)S(1)}, f32[128,128]{1,0:T(8,128)S(1)}, u32[]{:S(2)}, u32[]{:S(2)}) collective-permute-start(f32[128,128]{1,0:T(8,128)S(1)} %copy-done.16), channel_id=1, source_target_pairs={{0,24},{4,28},{8,16},{12,20},{16,8},{20,12},{24,0},{28,4},{1,25},{... | collective-permute-start | bytes 196616 | tf_op jit(solution)/shard_map/ppermute | solution.py:776
  53.3 0.0 collective-permute-done.2
  53.3 0.7 collective-permute-start.9
  54.0 4.8 %shard_map.62 = (f32[2,19,64,128]{3,2,1,0:T(8,128)}, f32[2,18,64,128]{3,2,1,0:T(8,128)}, f32[2,17,64,128]{3,2,1,0:T(8,128)}, f32[3,8,128]{2,1,0:T(8,128)S(1)}, f32[8,8,128]{2,1,0:T(8,128)S(1)}) custom-call(s32[4,128]{1,0:T(4,128)S(1)} %concatenate.10.meta.meta_in, f32[8,432,128]{2,1,0:T(8,128)} %copy-done, f32[2,19,64,128]{3,2,1,0:T(8,128)} %copy-done.2), custom_call_target="tpu_custom_call" | custom-call | flops 2000000 | bytes 1048576 | tf_op jit(solution)/shard_map/pallas_call | solution.py:790
  58.8 5.8 %shard_map.63 = (f32[32,128]{1,0:T(8,128)S(1)}, f32[2,17,72,128]{3,2,1,0:T(8,128)}, f32[2,17,72,128]{3,2,1,0:T(8,128)}, f32[2,17,72,128]{3,2,1,0:T(8,128)}) custom-call(s32[4,128]{1,0:T(4,128)S(1)} %concatenate.10.meta.meta_in, f32[37,8,128]{2,1,0:T(8,128)S(1)} %bitcast.21, f32[2,19,8,128]{3,2,1,0:T(8,128)S(1)} %get-tuple-element.41.unused_a.interp_halo_in, ...), custom_call_target="tpu_custom_call" | custom-call | flops 2000000 | bytes 1048576 | tf_op jit(solution)/shard_map/pallas_call | solution.py:799
  64.7 0.0 collective-permute-done.5.rest_3_
  64.7 0.0 collective-permute-done.6.rest_4_
  64.7 0.0 collective-permute-done.8.rest_6_
  64.7 15.1 %all_to_all.15 = f32[32,1,128]{2,1,0:T(1,128)S(1)} all-to-all(f32[32,1,128]{2,1,0:T(1,128)S(1)} %bitcast.27), channel_id=1, replica_groups=mesh['zm'=8,'zv'=4] {'zm','zv'}, dimensions={0} | all-to-all | bytes 32768 | tf_op jit(solution)/shard_map/all_to_all | solution.py:742
  79.8 6.6 %shard_map.64 = (f32[2,16,64,128]{3,2,1,0:T(8,128)S(1)}, f32[2,16,64,128]{3,2,1,0:T(8,128)S(1)}, f32[4,128]{1,0:T(4,128)}, f32[32,128]{1,0:T(8,128)S(1)}) custom-call(s32[4,128]{1,0:T(4,128)S(1)} %concatenate.10.meta.meta_in, f32[32,128]{1,0:T(8,128)S(1)} %bitcast.25, f32[37,8,128]{2,1,0:T(8,128)S(1)} %bitcast.22, ...), custom_call_target="tpu_custom_call" | custom-call | flops 2000000 | bytes 1048576 | tf_op jit(solution)/shard_map/pallas_call | solution.py:809
  86.4 8.9 %all_to_all.16 = f32[32,1,128]{2,1,0:T(1,128)S(1)} all-to-all(f32[32,1,128]{2,1,0:T(1,128)S(1)} %bitcast.28), channel_id=1, replica_groups=mesh['zm'=8,'zv'=4] {'zm','zv'}, dimensions={0} | all-to-all | bytes 32768 | tf_op jit(solution)/shard_map/all_to_all | solution.py:742
  95.3 1.3 %shard_map.65 = (f32[16,64,256]{2,1,0:T(8,128)}, f32[4]{0:T(128)}) custom-call(f32[32,128]{1,0:T(8,128)S(1)} %bitcast.26, f32[16,64,256]{2,1,0:T(8,128)S(1)} %copy-done.1, f32[2,16,64,128]{3,2,1,0:T(8,128)S(1)} %get-tuple-element.70.change, f32[2,16,64,128]{3,2,1,0:T(8,128)S(1)} %get-tuple-element.71.r3), custom_call_target="tpu_custom_call" | custom-call | flops 2000000 | bytes 1048576 | tf_op jit(solution)/shard_map/pallas_call | solution.py:819
  (36 shorter events, 0.1 us)
Async XLA Ops:
  3.6 5.4 %copy-start.14 = (f32[4,64,256]{2,1,0:T(8,128)S(1)}, f32[4,64,256]{2,1,0:T(8,128)}, u32[]{:S(2)}) copy-start(f32[4,64,256]{2,1,0:T(8,128)} %get-tuple-element.40) | copy-start | bytes 786436
  3.6 6.7 %copy-start.3 = (s32[4,32,8]{1,2,0:T(8,128)S(1)}, s32[4,32,8]{1,2,0:T(8,128)}, u32[]{:S(2)}) copy-start(s32[4,32,8]{1,2,0:T(8,128)} %param.5) | copy-start | bytes 12292
  3.7 8.8 %slice-start = ((f32[16,64,256]{2,1,0:T(8,128)}), f32[16,8,256]{2,1,0:T(8,128)S(1)}, s32[]{:S(2)}) async-start(f32[16,64,256]{2,1,0:T(8,128)} %table_in.1), calls=%async_computation.3 | async-start | bytes 262144 | tf_op jit(solution)/shard_map/slice | solution.py:768
  3.7 28.4 %all-to-all-start = ((f32[8,432,128]{2,1,0:T(8,128)}), f32[8,432,128]{2,1,0:T(8,128)S(1)}, u32[]{:S(2)}, u32[]{:S(2)}) async-start(f32[8,432,128]{2,1,0:T(8,128)} %get-tuple-element.39), calls=%async_computation | async-start | bytes 3538944 | tf_op jit(solution)/shard_map/all_to_all | solution.py:767
  9.0 3.4 %collective-permute-start = (f32[4,64,256]{2,1,0:T(8,128)S(1)}, f32[4,64,256]{2,1,0:T(8,128)S(1)}, u32[]{:S(2)}, u32[]{:S(2)}) collective-permute-start(f32[4,64,256]{2,1,0:T(8,128)S(1)} %copy-done.14), channel_id=1, source_target_pairs={{4,0},{8,4},{12,8},{16,12},{20,16},{24,20},{28,24},{5,1},{9,5},{13... | collective-permute-start | bytes 786440 | tf_op jit(solution)/shard_map/ppermute | solution.py:747
  12.5 8.5 %copy-start.1 = (f32[16,64,256]{2,1,0:T(8,128)S(1)}, f32[16,64,256]{2,1,0:T(8,128)}, u32[]{:S(2)}) copy-start(f32[16,64,256]{2,1,0:T(8,128)} %table_in.1) | copy-start | bytes 3145732
  13.1 7.8 %collective-permute-start.1 = (f32[20,8,256]{2,1,0:T(8,128)}, f32[20,8,256]{2,1,0:T(8,128)S(1)}, u32[]{:S(2)}, u32[]{:S(2)}) collective-permute-start(f32[20,8,256]{2,1,0:T(8,128)} %pad_maximum_fusion), channel_id=1, source_target_pairs={{1,0},{2,1},{3,2},{5,4},{6,5},{7,6},{9,8},{10,9},{11,10},{13,12},{... | collective-permute-start | bytes 491528 | tf_op jit(solution)/shard_map/ppermute | solution.py:747
  17.8 0.6 copy-start.4
  18.5 0.6 copy-start.6
  19.1 0.6 copy-start.8
  19.7 0.6 copy-start.10
  20.3 0.6 copy-start.12
  23.5 1.0 %copy-start.2 = (f32[2,19,64,128]{3,2,1,0:T(8,128)}, f32[2,19,64,128]{3,2,1,0:T(8,128)S(1)}, u32[]{:S(2)}) copy-start(f32[2,19,64,128]{3,2,1,0:T(8,128)S(1)} %get-tuple-element.43.interp_in) | copy-start | bytes 3735556
  24.5 9.6 %copy-start.13 = (f32[128,128]{1,0:T(8,128)S(1)}, f32[128,128]{1,0:T(8,128)}, u32[]{:S(2)}) copy-start(f32[128,128]{1,0:T(8,128)} %copy-done.12) | copy-start | bytes 196612
  24.5 23.5 %copy-start.11 = (f32[128,128]{1,0:T(8,128)S(1)}, f32[128,128]{1,0:T(8,128)}, u32[]{:S(2)}) copy-start(f32[128,128]{1,0:T(8,128)} %copy-done.10) | copy-start | bytes 196612
  24.5 25.0 %copy-start.9 = (f32[128,128]{1,0:T(8,128)S(1)}, f32[128,128]{1,0:T(8,128)}, u32[]{:S(2)}) copy-start(f32[128,128]{1,0:T(8,128)} %copy-done.8) | copy-start | bytes 196612
  24.5 25.0 %copy-start.7 = (f32[128,128]{1,0:T(8,128)S(1)}, f32[128,128]{1,0:T(8,128)}, u32[]{:S(2)}) copy-start(f32[128,128]{1,0:T(8,128)} %copy-done.6) | copy-start | bytes 196612
  24.5 26.4 %copy-start.5 = (f32[128,128]{1,0:T(8,128)S(1)}, f32[128,128]{1,0:T(8,128)}, u32[]{:S(2)}) copy-start(f32[128,128]{1,0:T(8,128)} %copy-done.4) | copy-start | bytes 196612
  24.5 28.8 %copy-start.15 = (f32[128,128]{1,0:T(8,128)S(1)}, f32[128,128]{1,0:T(8,128)}, u32[]{:S(2)}) copy-start(f32[128,128]{1,0:T(8,128)} %get-tuple-element.55) | copy-start | bytes 196612
  32.1 21.9 %copy-start = (f32[8,432,128]{2,1,0:T(8,128)}, f32[8,432,128]{2,1,0:T(8,128)S(1)}, u32[]{:S(2)}) copy-start(f32[8,432,128]{2,1,0:T(8,128)S(1)} %all-to-all-done.data) | copy-start | bytes 5308420
  32.1 20.2 %copy-start.16 = (f32[128,128]{1,0:T(8,128)S(1)}, f32[128,128]{1,0:T(8,128)}, u32[]{:S(2)}) copy-start(f32[128,128]{1,0:T(8,128)} %get-tuple-element.54) | copy-start | bytes 196612
  32.8 20.5 %collective-permute-start.2 = (f32[296,128]{1,0:T(8,128)S(1)}, f32[296,128]{1,0:T(8,128)S(1)}, u32[]{:S(2)}, u32[]{:S(2)}) collective-permute-start(f32[296,128]{1,0:T(8,128)S(1)} %shard_map.61), channel_id=1, source_target_pairs={{1,0},{2,1},{3,2},{5,4},{6,5},{7,6},{9,8},{10,9},{11,10},{13,12},{... | collective-permute-start | bytes 454664 | tf_op jit(solution)/shard_map/ppermute | solution.py:747
  34.1 16.8 %collective-permute-start.3 = (f32[128,128]{1,0:T(8,128)S(1)}, f32[128,128]{1,0:T(8,128)S(1)}, u32[]{:S(2)}, u32[]{:S(2)}) collective-permute-start(f32[128,128]{1,0:T(8,128)S(1)} %copy-done.13), channel_id=1, source_target_pairs={{0,4},{4,0},{8,12},{12,8},{16,20},{20,16},{24,28},{28,24},{1,5},{5... | collective-permute-start | bytes 196616 | tf_op jit(solution)/shard_map/ppermute | solution.py:776
  48.1 4.3 %collective-permute-start.4 = (f32[128,128]{1,0:T(8,128)S(1)}, f32[128,128]{1,0:T(8,128)S(1)}, u32[]{:S(2)}, u32[]{:S(2)}) collective-permute-start(f32[128,128]{1,0:T(8,128)S(1)} %copy-done.11), channel_id=1, source_target_pairs={{0,8},{4,12},{8,0},{12,4},{16,24},{20,28},{24,16},{28,20},{1,9},{5... | collective-permute-start | bytes 196616 | tf_op jit(solution)/shard_map/ppermute | solution.py:776
  49.5 15.1 %collective-permute-start.5 = (f32[128,128]{1,0:T(8,128)S(1)}, f32[128,128]{1,0:T(8,128)S(1)}, u32[]{:S(2)}, u32[]{:S(2)}) collective-permute-start(f32[128,128]{1,0:T(8,128)S(1)} %copy-done.9), channel_id=1, source_target_pairs={{0,12},{4,8},{8,4},{12,0},{16,28},{20,24},{24,20},{28,16},{1,13},{... | collective-permute-start | bytes 196616 | tf_op jit(solution)/shard_map/ppermute | solution.py:776
  49.5 15.1 %collective-permute-start.6 = (f32[128,128]{1,0:T(8,128)S(1)}, f32[128,128]{1,0:T(8,128)S(1)}, u32[]{:S(2)}, u32[]{:S(2)}) collective-permute-start(f32[128,128]{1,0:T(8,128)S(1)} %copy-done.7), channel_id=1, source_target_pairs={{0,16},{4,20},{8,24},{12,28},{16,0},{20,4},{24,8},{28,12},{1,17},{... | collective-permute-start | bytes 196616 | tf_op jit(solution)/shard_map/ppermute | solution.py:776
  50.9 13.8 %collective-permute-start.7 = (f32[128,128]{1,0:T(8,128)S(1)}, f32[128,128]{1,0:T(8,128)S(1)}, u32[]{:S(2)}, u32[]{:S(2)}) collective-permute-start(f32[128,128]{1,0:T(8,128)S(1)} %copy-done.5), channel_id=1, source_target_pairs={{0,20},{4,16},{8,28},{12,24},{16,4},{20,0},{24,12},{28,8},{1,21},{... | collective-permute-start | bytes 196616 | tf_op jit(solution)/shard_map/ppermute | solution.py:776
  52.3 12.4 %collective-permute-start.8 = (f32[128,128]{1,0:T(8,128)S(1)}, f32[128,128]{1,0:T(8,128)S(1)}, u32[]{:S(2)}, u32[]{:S(2)}) collective-permute-start(f32[128,128]{1,0:T(8,128)S(1)} %copy-done.16), channel_id=1, source_target_pairs={{0,24},{4,28},{8,16},{12,20},{16,8},{20,12},{24,0},{28,4},{1,25},{... | collective-permute-start | bytes 196616 | tf_op jit(solution)/shard_map/ppermute | solution.py:776
  53.3 11.4 %collective-permute-start.9 = (f32[128,128]{1,0:T(8,128)S(1)}, f32[128,128]{1,0:T(8,128)S(1)}, u32[]{:S(2)}, u32[]{:S(2)}) collective-permute-start(f32[128,128]{1,0:T(8,128)S(1)} %copy-done.15), channel_id=1, source_target_pairs={{0,28},{4,24},{8,20},{12,16},{16,12},{20,8},{24,4},{28,0},{1,29},{... | collective-permute-start | bytes 196616 | tf_op jit(solution)/shard_map/ppermute | solution.py:776
